TPU v7x, 32 devices: a whole 2x2x4 slice. The times are simulated.
32 devices in a mesh: parts: 2 (over y), row: 16 (over z, x, core).
Axes of the slice: x: 2, y: 2, z: 4, core: 2. Of those that a mesh axis runs over, the one named last changes fastest.
Arguments:
- tokens: bfloat16 [64, 256, 768], P(('parts', 'row')), parts along dimension 0, may hold values from -6 to 6
- w_query: bfloat16 [768, 768], replicated, may hold values from -0.21875 to 0.21875
- w_key: bfloat16 [768, 768], replicated, may hold values from -0.21875 to 0.21875
- w_value: bfloat16 [768, 768], replicated, may hold values from -0.21875 to 0.21875
- w_out: bfloat16 [768, 768], replicated, may hold values from -0.21875 to 0.21875
- omega: bfloat16 [12, 64, 256], replicated, may hold values from -5 to 5
- conv_kernel: float32 [3, 3, 768], replicated, may hold values from -0.6 to 0.6
- norm_gain: float32 [768], replicated, may hold values from 0.1 to 1.9
Outputs:
- layer_out: bfloat16 [64, 256, 768], P(('parts', 'row')), parts along dimension 0
There are 2 independent parts, one for each index of `parts`. A program takes and returns all parts, laid end to end along the dimension named above; an argument that names none is the same for every part. Nothing has to cross between parts.
All inputs are finite; a program needn't handle non-finite values.
Results may differ from a plain program's by a relative error of at most 0.0081.
Values may be sent and summed in bfloat16 or wider, within the bound.
No kernel may reach another device: no remote copies, remote signals or barrier semaphores. Data moves between devices by JAX's collectives and lax.ppermute only.
A program may use at most 64 MiB of HBM per device.

v0:
```python
import jax
import jax.numpy as jnp
from jax import lax
from jax.sharding import PartitionSpec as P


def with_halo(block, sides, width):
    for axis, dim in sides:
        count = lax.axis_size(axis)
        forward = [(i, i + 1) for i in range(count - 1)]
        backward = [(target, source) for source, target in forward]
        low = lax.ppermute(
            lax.slice_in_dim(block, block.shape[dim] - width, None, axis=dim), axis, forward
        )
        high = lax.ppermute(lax.slice_in_dim(block, 0, width, axis=dim), axis, backward)
        block = jnp.concatenate([low, block, high], axis=dim)
    return block


def project(rows, weight):
    return jnp.dot(rows, weight, preferred_element_type=jnp.float32).astype(jnp.bfloat16)


def feature_map(heads_in, omega):
    dim_head = heads_in.shape[-1]
    lifted = jnp.einsum("thd,hdf->thf", heads_in, omega, preferred_element_type=jnp.float32)
    values = heads_in.astype(jnp.float32)
    square = jnp.sum(values * values, axis=-1, keepdims=True)
    feats = jnp.exp(lifted * dim_head ** (-0.25) - square * 0.5 * dim_head ** (-0.5)) * omega.shape[
        -1
    ] ** (-0.5)
    return feats.astype(jnp.bfloat16)


def shards(tokens, w_query, w_key, w_value, w_out, omega, conv_kernel, norm_gain):
    rows_here, cols, width = tokens.shape
    heads, dim_head, nfeat = omega.shape
    flat = tokens.reshape(rows_here * cols, width)
    value = project(flat, w_value)
    value_ext = with_halo(value.reshape(rows_here, cols, width), (("row", 0),), 1)
    feat_key = feature_map(project(flat, w_key).reshape(-1, heads, dim_head), omega)
    local_state = jnp.einsum(
        "thf,thd->fhd",
        feat_key,
        value.reshape(-1, heads, dim_head),
        preferred_element_type=jnp.float32,
    )
    local_sum = jnp.sum(feat_key.astype(jnp.float32), axis=0)
    feat_query = feature_map(project(flat, w_query).reshape(-1, heads, dim_head), omega)
    padded = jnp.pad(value_ext.astype(jnp.float32), ((0, 0), (1, 1), (0, 0)))
    position = jnp.zeros((rows_here, cols, width), jnp.float32)
    for shift_a in range(3):
        for shift_b in range(3):
            position = (
                position
                + padded[shift_a : shift_a + rows_here, shift_b : shift_b + cols, :]
                * conv_kernel[shift_a, shift_b]
            )
    kv_sum, key_sum = lax.psum((local_state.reshape(nfeat, width), local_sum), "row")
    kv_state = kv_sum.astype(jnp.bfloat16).reshape(nfeat, heads, dim_head)
    numer = jnp.einsum("thf,fhd->thd", feat_query, kv_state, preferred_element_type=jnp.float32)
    denom = jnp.einsum(
        "thf,hf->th", feat_query.astype(jnp.float32), key_sum, precision=lax.Precision.HIGHEST
    )
    attn = numer / denom[:, :, None]
    scale = lax.rsqrt(jnp.mean(attn * attn, axis=(1, 2), keepdims=True) + 1e-06)
    normed = (attn * scale).reshape(-1, width) * norm_gain
    mixed = (normed + position.reshape(-1, width)).astype(jnp.bfloat16)
    out = flat.astype(jnp.float32) + jnp.dot(mixed, w_out, preferred_element_type=jnp.float32)
    return out.astype(jnp.bfloat16).reshape(rows_here, cols, width)


def solution(mesh):
    return jax.shard_map(
        shards,
        mesh=mesh,
        in_specs=(P(("parts", "row"), None, None), P(), P(), P(), P(), P(), P(), P()),
        out_specs=P(("parts", "row"), None, None),
        check_vma=False,
    )
```

profile of v0, /device:TPU:0, one launch (start us, length us, event | category | flops | bytes accessed | tf_op | source)
XLA Modules:
  0.0 115.2 jit_solution(12742287627702785171)
XLA Ops:
  0.0 0.0 copy-start
  0.0 1.3 %copy-done = bf16[768,768]{1,0:T(8,128)(2,1)S(1)} copy-done((bf16[768,768]{1,0:T(8,128)(2,1)S(1)}, bf16[768,768]{1,0:T(8,128)(2,1)}, u32[]{:S(2)}) %copy-start) | copy-done | bytes 1179672
  1.3 1.9 %convolution_convert_fusion.2 = bf16[512,768]{1,0:T(8,128)(2,1)S(1)} fusion(bf16[512,768]{1,0:T(8,128)(2,1)} %bitcast.72, bf16[768,768]{1,0:T(8,128)(2,1)S(1)} %copy-done), kind=kOutput, calls=%fused_computation.43 | convolution fusion | flops 604372992 | bytes 2752512 | tf_op jit(solution)/shard_map/dot_general | solution.py:21
  3.2 0.0 copy-start.6
  3.2 0.9 slice_bitcast_fusion.1
  4.1 3.1 %collective-permute-start = (bf16[1,256,768]{2,1,0:T(8,128)(2,1)}, bf16[1,256,768]{2,1,0:T(8,128)(2,1)}, u32[]{:S(2)}, u32[]{:S(2)}) collective-permute-start(bf16[1,256,768]{2,1,0:T(8,128)(2,1)} %get-tuple-element.16), channel_id=1, source_target_pairs={{0,1},{1,2},{2,3},{3,4},{4,5},{5,6},{6,7},{7,8},{8,9},{9,10},{10,1... | collective-permute-start | bytes 1179656 | tf_op jit(solution)/shard_map/ppermute | solution.py:12
  7.3 1.3 %collective-permute-start.1 = (bf16[1,256,768]{2,1,0:T(8,128)(2,1)}, bf16[1,256,768]{2,1,0:T(8,128)(2,1)}, u32[]{:S(2)}, u32[]{:S(2)}) collective-permute-start(bf16[1,256,768]{2,1,0:T(8,128)(2,1)} %get-tuple-element.17), channel_id=1, source_target_pairs={{1,0},{2,1},{3,2},{4,3},{5,4},{6,5},{7,6},{8,7},{9,8},{10,9},{11,1... | collective-permute-start | bytes 1179656 | tf_op jit(solution)/shard_map/ppermute | solution.py:15
  8.6 0.3 copy.13
  8.8 0.0 copy-done.6
  8.9 2.9 %convolution_convert_fusion.1 = bf16[512,768]{1,0:T(8,128)(2,1)} fusion(bf16[512,768]{1,0:T(8,128)(2,1)S(1)} %bitcast.73, bf16[768,768]{1,0:T(8,128)(2,1)} %param.10), kind=kOutput, calls=%fused_computation.42 | convolution fusion | flops 604372992 | bytes 2752512 | tf_op jit(solution)/shard_map/dot_general | solution.py:21
  11.8 1.4 %copy.14 = bf16[512,768]{0,1:T(8,128)(2,1)S(1)} copy(bf16[512,768]{1,0:T(8,128)(2,1)} %convolution_convert_fusion.1) | data formatting | bytes 1572864 | tf_op jit(solution)/shard_map/convert_element_type | solution.py:21
  13.2 0.2 multiply_reduce_fusion.2
  13.4 3.2 %convert_reduce_fusion = (f32[12,256]{1,0:T(8,128)S(1)}, bf16[512,12,256]{2,0,1:T(8,128)(2,1)S(1)}) fusion(f32[512,12]{0,1:T(8,128)S(1)} %broadcast_multiply_fusion.2, bf16[512,12,64]{0,2,1:T(8,128)(2,1)S(1)} %bitcast.67, bf16[12,64,256]{2,1,0:T(8,128)(2,1)} %param.13), kind=kOutput, calls=%fused_computation.8 | convolution fusion | flops 210760704 | bytes 4362240 | tf_op jit(solution)/shard_map/thd,hdf->thf/dot_general | solution.py:26
  16.7 0.0 copy-start.4
  16.7 0.0 copy-start.7
  16.7 0.7 fusion.24
  17.3 0.6 copy-done.4
  17.9 0.2 copy-done.7
  18.2 1.7 %convolution_convert_fusion = bf16[512,768]{1,0:T(8,128)(2,1)} fusion(bf16[512,768]{1,0:T(8,128)(2,1)S(1)} %bitcast.74, bf16[768,768]{1,0:T(8,128)(2,1)S(1)} %copy-done.4), kind=kOutput, calls=%fused_computation.41 | convolution fusion | flops 604372992 | bytes 2752512 | tf_op jit(solution)/shard_map/dot_general | solution.py:21
  19.8 1.4 %copy.15 = bf16[512,768]{0,1:T(8,128)(2,1)S(1)} copy(bf16[512,768]{1,0:T(8,128)(2,1)} %convolution_convert_fusion) | data formatting | bytes 1572864 | tf_op jit(solution)/shard_map/convert_element_type | solution.py:21
  21.2 0.2 multiply_reduce_fusion.1
  21.4 4.1 %fusion.2 = bf16[512,12,256]{2,0,1:T(8,128)(2,1)} fusion(f32[512,12]{0,1:T(8,128)S(1)} %broadcast_multiply_fusion.1, bf16[512,12,64]{0,2,1:T(8,128)(2,1)S(1)} %bitcast.69, bf16[12,64,256]{2,1,0:T(8,128)(2,1)} %param.13), kind=kOutput, calls=%fused_computation.3 | convolution fusion | flops 207618048 | bytes 4349952 | tf_op jit(solution)/shard_map/thd,hdf->thf/dot_general | solution.py:26
  25.6 73.0 %all-reduce.3 = (bf16[256,768]{0,1:T(8,128)(2,1)S(1)}, f32[12,256]{1,0:T(8,128)S(1)}) all-reduce(f32[256,768]{0,1:T(8,128)S(1)} %bitcast.64, f32[12,256]{1,0:T(8,128)S(1)} %get-tuple-element.18), channel_id=1, replica_groups=mesh['parts'=2,'row'=16] {'row'}, use_global_device_ids=true, to_apply=%region_1.0 | all-reduce | flops 199680 | bytes 1204224 | tf_op jit(solution)/shard_map/psum | solution.py:59
  98.6 0.0 copy-start.1
  98.6 4.6 %fusion.22 = f32[12,1,512]{2,1,0:T(1,128)S(1)} fusion(bf16[512,12,256]{2,0,1:T(8,128)(2,1)} %fusion.2, f32[12,256,1]{1,0,2:T(8,128)S(1)} %bitcast.71), kind=kOutput, calls=%fused_computation.50 | convolution fusion | flops 18874368 | bytes 3182592 | tf_op jit(solution)/shard_map/thf,hf->th/dot_general | solution.py:62
  103.2 0.0 copy-done.1
  103.2 0.0 copy-start.2
  103.2 1.1 multiply_reduce_fusion
  104.4 0.0 copy-done.2
  104.4 0.1 slice_reduce_fusion.8
  104.4 1.3 %broadcast_multiply_fusion = f32[512,12,64]{0,2,1:T(8,128)} fusion(f32[512,12,64]{0,2,1:T(8,128)S(1)} %get-tuple-element.21, f32[512]{0:T(512)S(1)} %add_rsqrt_fusion), kind=kLoop, calls=%fused_computation.44 | loop fusion | flops 393216 | bytes 3147776 | tf_op jit(solution)/shard_map/mul | solution.py:67
  105.8 0.0 collective-permute-done
  105.8 0.0 collective-permute-done.1
  105.8 1.4 %maximum_convert_fusion = f32[4,256,768]{2,1,0:T(8,128)S(1)} fusion(bf16[1,256,768]{2,1,0:T(8,128)(2,1)} %collective-permute-done.1, bf16[2,256,768]{2,1,0:T(8,128)(2,1)S(1)} %bitcast.62, bf16[1,256,768]{2,1,0:T(8,128)(2,1)} %collective-permute-done), kind=kLoop, calls=%fused_computation.32 | loop fusion | flops 2359296 | bytes 4718592 | tf_op jit(solution)/shard_map/convert_element_type | solution.py:50
  107.1 2.5 %fusion.14 = f32[2,256,768]{2,1,0:T(8,128)} fusion(f32[4,256,768]{2,1,0:T(8,128)S(1)} %maximum_convert_fusion, f32[768]{0:T(1024)S(1)} %get-tuple-element.12, f32[768]{0:T(1024)S(1)} %get-tuple-element.13, f32[768]{0:T(1024)S(1)} %get-tuple-element.6, f32[768]{0:T(1024)S(1)} %get-tuple-element.7, f32[768]{0:T(1024)S(1)} %get-tuple-element.8, ...), kind=kLoop, calls=%fused_computation.23 | loop fusion | flops 6684672 | bytes 9474048 | tf_op jit(solution)/shard_map/add | solution.py:55
  109.6 0.0 copy-start.3
  109.6 1.9 %copy.16 = f32[512,768]{0,1:T(8,128)S(1)} copy(f32[512,768]{1,0:T(8,128)} %bitcast.63) | data formatting | bytes 3145728 | tf_op jit(solution)/shard_map/reshape | solution.py:68
  111.5 0.0 copy-done.3
  111.5 0.0 copy-start.5
  111.5 0.0 copy-start.8
  111.6 1.7 %fusion.21 = bf16[512,768]{0,1:T(8,128)(2,1)S(1)} fusion(f32[512,768]{0,1:T(8,128)S(1)} %copy.16, f32[512,12,64]{0,2,1:T(8,128)} %broadcast_multiply_fusion, f32[768]{0:T(1024)S(1)} %copy-done.3), kind=kLoop, calls=%fused_computation.35 | loop fusion | flops 1179648 | bytes 3935232 | tf_op jit(solution)/shard_map/convert_element_type | solution.py:68
  113.3 0.0 copy-done.5
  113.3 0.2 copy-done.8
  113.5 1.7 %add_convert_fusion = bf16[512,768]{1,0:T(8,128)(2,1)} fusion(bf16[512,768]{1,0:T(8,128)(2,1)S(1)} %bitcast.75, bf16[512,768]{0,1:T(8,128)(2,1)S(1)} %fusion.21, bf16[768,768]{1,0:T(8,128)(2,1)S(1)} %copy-done.5), kind=kOutput, calls=%fused_computation.37 | convolution fusion | flops 605159424 | bytes 3538944 | tf_op jit(solution)/shard_map/dot_general | solution.py:69
  (4 shorter events, 0.0 us)
Async XLA Ops:
  0.0 1.3 %copy-start = (bf16[768,768]{1,0:T(8,128)(2,1)S(1)}, bf16[768,768]{1,0:T(8,128)(2,1)}, u32[]{:S(2)}) copy-start(bf16[768,768]{1,0:T(8,128)(2,1)} %param.11) | copy-start | bytes 3538948
  3.2 5.7 %copy-start.6 = (bf16[2,256,768]{2,1,0:T(8,128)(2,1)S(1)}, bf16[2,256,768]{2,1,0:T(8,128)(2,1)}, u32[]{:S(2)}) copy-start(bf16[2,256,768]{2,1,0:T(8,128)(2,1)} %param.8) | copy-start | bytes 2359300
  4.1 101.6 %collective-permute-start = (bf16[1,256,768]{2,1,0:T(8,128)(2,1)}, bf16[1,256,768]{2,1,0:T(8,128)(2,1)}, u32[]{:S(2)}, u32[]{:S(2)}) collective-permute-start(bf16[1,256,768]{2,1,0:T(8,128)(2,1)} %get-tuple-element.16), channel_id=1, source_target_pairs={{0,1},{1,2},{2,3},{3,4},{4,5},{5,6},{6,7},{7,8},{8,9},{9,10},{10,1... | collective-permute-start | bytes 1179656 | tf_op jit(solution)/shard_map/ppermute | solution.py:12
  7.3 98.5 %collective-permute-start.1 = (bf16[1,256,768]{2,1,0:T(8,128)(2,1)}, bf16[1,256,768]{2,1,0:T(8,128)(2,1)}, u32[]{:S(2)}, u32[]{:S(2)}) collective-permute-start(bf16[1,256,768]{2,1,0:T(8,128)(2,1)} %get-tuple-element.17), channel_id=1, source_target_pairs={{1,0},{2,1},{3,2},{4,3},{5,4},{6,5},{7,6},{8,7},{9,8},{10,9},{11,1... | collective-permute-start | bytes 1179656 | tf_op jit(solution)/shard_map/ppermute | solution.py:15
  16.7 1.3 %copy-start.4 = (bf16[768,768]{1,0:T(8,128)(2,1)S(1)}, bf16[768,768]{1,0:T(8,128)(2,1)}, u32[]{:S(2)}) copy-start(bf16[768,768]{1,0:T(8,128)(2,1)} %param.9) | copy-start | bytes 3538948
  16.7 1.5 %copy-start.7 = (bf16[2,256,768]{2,1,0:T(8,128)(2,1)S(1)}, bf16[2,256,768]{2,1,0:T(8,128)(2,1)}, u32[]{:S(2)}) copy-start(bf16[2,256,768]{2,1,0:T(8,128)(2,1)} %param.8) | copy-start | bytes 2359300
  98.6 4.6 %copy-start.1 = (bf16[512,12,256]{2,0,1:T(8,128)(2,1)S(1)}, bf16[512,12,256]{2,0,1:T(8,128)(2,1)}, u32[]{:S(2)}) copy-start(bf16[512,12,256]{2,0,1:T(8,128)(2,1)} %fusion.2) | copy-start | bytes 9437188
  103.2 1.1 copy-start.2
  109.6 1.9 %copy-start.3 = (f32[768]{0:T(1024)S(1)}, f32[768]{0:T(1024)}, u32[]{:S(2)}) copy-start(f32[768]{0:T(1024)} %param.15) | copy-start | bytes 9220
  111.5 1.8 %copy-start.5 = (bf16[768,768]{1,0:T(8,128)(2,1)S(1)}, bf16[768,768]{1,0:T(8,128)(2,1)}, u32[]{:S(2)}) copy-start(bf16[768,768]{1,0:T(8,128)(2,1)} %param.12) | copy-start | bytes 3538948
  111.5 2.0 %copy-start.8 = (bf16[2,256,768]{2,1,0:T(8,128)(2,1)S(1)}, bf16[2,256,768]{2,1,0:T(8,128)(2,1)}, u32[]{:S(2)}) copy-start(bf16[2,256,768]{2,1,0:T(8,128)(2,1)} %param.8) | copy-start | bytes 2359300
where the time goes:
time: 116 us; the launch traced here: 115 us
  blocking collectives  73 us (63%)
  matrix products  21.9 us (19%)
  local copies, waits for them, and re-layouts  8.3 us (7%)
  other arithmetic  7.33 us (6%)
  starting transfers between devices  4.42 us (4%)
    psum x1, blocking collectives, shards(): lax.psum((local_state.reshape(nfeat, width), local_sum), 'row')  73 us
    dot_general x2, matrix products, feature_map(): jnp.einsum('thd,hdf->thf', heads_in, omega, preferred_element_type=jnp.fl...  7.36 us
    dot_general x3, matrix products, project(): jnp.dot(rows, weight, preferred_element_type=jnp.float32)  6.5 us
    dot_general x1, matrix products, shards(): jnp.einsum('thf,hf->th', feat_query.astype(jnp.float32), key_sum, precisi...  4.57 us
    ppermute x1, starting transfers between devices, with_halo(): lax.ppermute(lax.slice_in_dim(block, block.shape[dim] - width, None, axis...  3.14 us
    convert_element_type x3, local copies, waits for them, and re-layouts, project(): jnp.dot(rows, weight, preferred_element_type=jnp.float32)  3.1 us
    add x1, other arithmetic, shards(): position + padded[shift_a:shift_a + rows_here, shift_b:shift_b + cols, :]...  2.48 us
  transfers between devices with their start and end apart: 2, of which 0 were waited for; matrix products, arithmetic and copies ran while one was open for 20% of the time, Pallas kernels for 0%

commit v1 on v0

v1 whole, which is shorter than its diff:
```python
import functools

import jax
import jax.numpy as jnp
from jax import lax
from jax.experimental import pallas as pl
from jax.experimental.pallas import tpu as pltpu
from jax.sharding import PartitionSpec as P

BF = jnp.bfloat16
F32 = jnp.float32
LOG2E = 1.4426950408889634
VMEM_LIMIT = 28 * 1024 * 1024


def vmem_specs(count):
    return [pl.BlockSpec(memory_space=pltpu.VMEM)] * count


def tiles_of(total, wanted):
    return wanted if total % wanted == 0 else total


def feature_tile(proj, omega_pair, ones_pair, dim_head, nfeat):
    rows = proj.shape[0]
    wide = 2 * dim_head
    lifted = jnp.dot(proj, omega_pair, preferred_element_type=F32)
    values = proj.astype(F32)
    square = values * values * (0.5 * dim_head ** (-0.5) * LOG2E)
    high = square.astype(BF)
    low = (square - high.astype(F32)).astype(BF)
    summed = jnp.dot(jnp.concatenate([high, low], axis=1), ones_pair, preferred_element_type=F32)
    halves = []
    shift = 0.5 * jnp.log2(jnp.float32(nfeat))
    for head in range(2):
        drop = summed[:, head * wide : (head + 1) * wide] + shift
        for part in range(nfeat // wide):
            start = head * nfeat + part * wide
            grown = lifted[:, start : start + wide] * (dim_head ** (-0.25) * LOG2E)
            halves.append(jnp.exp2(grown - drop).astype(BF))
    return jnp.concatenate(halves, axis=1)


def fill_pairs(omega_ref, pair_ref, ones_ref):
    heads, dim_head, nfeat = omega_ref.shape
    pair_ref[...] = jnp.zeros_like(pair_ref)
    for head in range(heads):
        side = head % 2
        pair_ref[head // 2, side * dim_head : (side + 1) * dim_head, side * nfeat : (side + 1) * nfeat] = omega_ref[head]
    shape = ones_ref.shape
    row = lax.broadcasted_iota(jnp.int32, shape, 0) // dim_head % 2
    col = lax.broadcasted_iota(jnp.int32, shape, 1) // (2 * dim_head)
    ones_ref[...] = jnp.where(row == col, 1.0, 0.0).astype(BF)


def state_kernel(flip_ref, x_ref, wk_ref, wv_ref, omega_ref, state_ref, value_ref, pair_ref, ones_ref, vt_ref, feat_ref):
    heads, dim_head, nfeat = omega_ref.shape
    tokens, width = x_ref.shape
    half = heads // 2
    fill_pairs(omega_ref, pair_ref, ones_ref)
    x = x_ref[...]
    value = jnp.dot(x, wv_ref[...], preferred_element_type=F32).astype(BF)
    value_ref[...] = value
    turned = value.T
    mark = lax.broadcasted_iota(jnp.int32, (16, tokens), 0)
    for head in range(heads):
        vt_ref[head, :dim_head, :] = turned[head * dim_head : (head + 1) * dim_head]
        vt_ref[head, dim_head:, :] = jnp.where(mark == head % half, 1.0, 0.0).astype(BF)
    rows = tiles_of(tokens, 128)
    chunk = 4 * dim_head
    sums = None
    for first in range(0, heads, 4):
        count = min(4, heads - first)
        key = jnp.dot(x, wk_ref[:, first * dim_head : (first + count) * dim_head], preferred_element_type=F32).astype(BF)
        for pair in range(count // 2):
            which = first // 2 + pair
            for start in range(0, tokens, rows):
                proj = key[start : start + rows, pair * 2 * dim_head : (pair + 1) * 2 * dim_head]
                feat_ref[start : start + rows, :] = feature_tile(proj, pair_ref[which], ones_ref[...], dim_head, nfeat)
            for side in range(2):
                head = 2 * which + side
                local = jnp.dot(vt_ref[head], feat_ref[:, side * nfeat : (side + 1) * nfeat], preferred_element_type=F32)
                slot = lax.rem(flip_ref[0] + head // half, 2)
                place = head % half
                state_ref[slot, place * dim_head : (place + 1) * dim_head, :] = local[:dim_head].astype(BF)
                sums = local[dim_head:] if place == 0 else sums + local[dim_head:]
                if place == half - 1:
                    state_ref[slot, half * dim_head :, :] = sums.astype(BF)


def query_kernel(x_ref, wq_ref, omega_ref, feat_ref, pair_ref, ones_ref):
    heads, dim_head, nfeat = omega_ref.shape
    tokens = x_ref.shape[0]
    fill_pairs(omega_ref, pair_ref, ones_ref)
    rows = tiles_of(tokens, 128)
    for start in range(0, tokens, rows):
        query = jnp.dot(x_ref[start : start + rows, :], wq_ref[...], preferred_element_type=F32).astype(BF)
        for pair in range(heads // 2):
            proj = query[:, pair * 2 * dim_head : (pair + 1) * 2 * dim_head]
            feat_ref[start : start + rows, pair * 2 * nfeat : (pair + 1) * 2 * nfeat] = feature_tile(
                proj, pair_ref[pair], ones_ref[...], dim_head, nfeat
            )


def conv_kernel_body(top_ref, own_ref, low_ref, wv_ref, taps_ref, out_ref, ext_ref):
    here, cols, width = own_ref.shape
    ext_ref[1 : here + 1] = own_ref[...]
    ext_ref[0] = jnp.dot(top_ref[...], wv_ref[...], preferred_element_type=F32).astype(BF)
    ext_ref[here + 1] = jnp.dot(low_ref[...], wv_ref[...], preferred_element_type=F32).astype(BF)
    lanes = 128
    col = lax.broadcasted_iota(jnp.int32, (cols, lanes), 0)
    for start in range(0, width, lanes):
        cut = slice(start, start + lanes)
        for row in range(here):
            sums = []
            for shift in range(3):
                total = None
                for step in range(3):
                    term = ext_ref[row + step, :, cut].astype(F32) * taps_ref[step, shift : shift + 1, cut]
                    total = term if total is None else total + term
                sums.append(total)
            left = jnp.where(col == 0, 0.0, pltpu.roll(sums[0], 1, 0))
            right = jnp.where(col == cols - 1, 0.0, pltpu.roll(sums[2], cols - 1, 0))
            out_ref[row, :, cut] = left + sums[1] + right


def out_kernel(flip_ref, state_ref, feat_ref, pos_ref, x_ref, gain_ref, wo_ref, out_ref, mat_ref, attn_ref, *, heads):
    tokens, width = x_ref.shape
    dim_head = width // heads
    nfeat = state_ref.shape[-1]
    half = heads // 2
    wide = 2 * dim_head
    mat_ref[...] = jnp.zeros_like(mat_ref)
    for head in range(heads):
        pair, side = head // 2, head % 2
        slot = lax.rem(flip_ref[0] + head // half, 2)
        place = head % half
        cut = slice(side * nfeat, (side + 1) * nfeat)
        mat_ref[pair, side * dim_head : (side + 1) * dim_head, cut] = state_ref[slot, place * dim_head : (place + 1) * dim_head, :]
        sums = state_ref[slot, half * dim_head :, :][place : place + 1]
        mat_ref[pair, wide + side * dim_head : wide + (side + 1) * dim_head, cut] = jnp.broadcast_to(sums, (dim_head, nfeat))
    rows = tiles_of(tokens, 256)
    for start in range(0, tokens, rows):
        total = None
        for pair in range(heads // 2):
            both = lax.dot_general(
                feat_ref[start : start + rows, pair * 2 * nfeat : (pair + 1) * 2 * nfeat],
                mat_ref[pair],
                (((1,), (1,)), ((), ())),
                preferred_element_type=F32,
            )
            attn = both[:, :wide] / both[:, wide:]
            attn_ref[:, pair * wide : (pair + 1) * wide] = attn
            total = attn * attn if total is None else total + attn * attn
        scale = lax.rsqrt(jnp.sum(total, axis=1, keepdims=True) * (1.0 / width) + 1e-06)
        mixed = (attn_ref[...] * scale * gain_ref[...] + pos_ref[start : start + rows, :]).astype(BF)
        out = x_ref[start : start + rows, :].astype(F32) + jnp.dot(mixed, wo_ref[...], preferred_element_type=F32)
        out_ref[start : start + rows, :] = out.astype(BF)


def call(kernel, out_shape, n_in, scratch, smem=True, flops=0, nbytes=0):
    specs = ([pl.BlockSpec(memory_space=pltpu.SMEM)] if smem else []) + vmem_specs(n_in)
    many = isinstance(out_shape, (tuple, list))
    return pl.pallas_call(
        kernel,
        out_shape=out_shape,
        in_specs=specs,
        out_specs=vmem_specs(len(out_shape)) if many else vmem_specs(1)[0],
        scratch_shapes=scratch,
        compiler_params=pltpu.CompilerParams(vmem_limit_bytes=VMEM_LIMIT),
        cost_estimate=pl.CostEstimate(flops=flops, bytes_accessed=nbytes, transcendentals=0),
    )


def swap(block, bit, count, keep):
    return lax.ppermute(block, "row", [(i, i ^ bit) for i in range(count) if keep(i)])


def reduce_state(state, count):
    odd = lambda i: i % 2 == 1
    core = lax.rem(lax.axis_index("row"), 2)
    chip = state.astype(F32) + swap(state, 1, count, lambda i: i % 2 == 0).astype(F32)
    part = chip[0] + swap(chip[1].astype(BF), 2, count, odd).astype(F32)
    bit = 4
    while bit < count:
        part = part + swap(part.astype(BF), bit, count, odd).astype(F32)
        bit *= 2
    done = part.astype(BF)
    whole = jnp.stack([done, swap(done, 2, count, odd)])
    return jnp.where(core == 1, whole, swap(whole, 1, count, odd))


def shards(tokens, w_query, w_key, w_value, w_out, omega, conv_kernel, norm_gain):
    here, cols, width = tokens.shape
    heads, dim_head, nfeat = omega.shape
    count = lax.axis_size("row")
    flat = tokens.reshape(here * cols, width)
    amount = here * cols
    half = heads // 2
    flip = lax.rem(lax.axis_index("row") // 2, 2).astype(jnp.int32).reshape(1)
    proj = 2 * amount * width * width
    feats = 2 * amount * width * nfeat
    pairs = [pltpu.VMEM((heads // 2, 2 * dim_head, 2 * nfeat), BF), pltpu.VMEM((4 * dim_head, 4 * dim_head), BF)]

    top = lax.ppermute(tokens[here - 1], "row", [(i, i + 1) for i in range(count - 1)])
    low = lax.ppermute(tokens[0], "row", [(i + 1, i) for i in range(count - 1)])

    state, value = call(
        state_kernel,
        (
            jax.ShapeDtypeStruct((2, half * dim_head + 16, nfeat), BF),
            jax.ShapeDtypeStruct((amount, width), BF),
        ),
        4,
        pairs + [pltpu.VMEM((heads, dim_head + 16, amount), BF), pltpu.VMEM((amount, 2 * nfeat), BF)],
        flops=2 * proj + 2 * feats,
    )(flip, flat, w_key, w_value, omega)
    feat_query = call(
        query_kernel,
        jax.ShapeDtypeStruct((amount, heads * nfeat), BF),
        3,
        pairs,
        smem=False,
        flops=proj + feats,
    )(flat, w_query, omega)
    position = call(
        conv_kernel_body,
        jax.ShapeDtypeStruct((here, cols, width), F32),
        5,
        [pltpu.VMEM((here + 2, cols, width), BF)],
        smem=False,
        flops=proj,
    )(top, value.reshape(here, cols, width), low, w_value, conv_kernel)
    final = reduce_state(state, count)
    out = call(
        functools.partial(out_kernel, heads=heads),
        jax.ShapeDtypeStruct((amount, width), BF),
        6,
        [pltpu.VMEM((heads // 2, 4 * dim_head, 2 * nfeat), BF), pltpu.VMEM((tiles_of(amount, 256), width), F32)],
        flops=proj + 2 * feats,
    )(flip, final, feat_query, position.reshape(amount, width), flat, norm_gain.reshape(1, width), w_out)
    return out.reshape(here, cols, width)


def solution(mesh):
    return jax.shard_map(
        shards,
        mesh=mesh,
        in_specs=(P(("parts", "row"), None, None), P(), P(), P(), P(), P(), P(), P()),
        out_specs=P(("parts", "row"), None, None),
        check_vma=False,
    )
```

time: 116 us -> 60.2 us (0.52)
  the two profiles are of different devices: /device:TPU:0 before, /device:TPU:1 now
where the time goes in v1:
time: 60.2 us; the launch traced here: 59.6 us
  starting transfers between devices  23.9 us (40%)
  waiting for transfers between devices  14.2 us (24%)
  Pallas kernels  11.6 us (19%)
  local copies, waits for them, and re-layouts  8.51 us (14%)
  other arithmetic  1.16 us (2%)
    ppermute x6, starting transfers between devices, swap(): lax.ppermute(block, 'row', [(i, i ^ bit) for i in range(count) if keep(i)])  18.4 us
    ppermute x6, waiting for transfers between devices, swap(): lax.ppermute(block, 'row', [(i, i ^ bit) for i in range(count) if keep(i)])  13.9 us
    unnamed x30, local copies, waits for them, and re-layouts  7.53 us
    pallas_call x1, Pallas kernels, shards(): call(state_kernel, (jax.ShapeDtypeStruct((2, half * dim_head + 16, nfeat)...  4.05 us
    ppermute x1, starting transfers between devices, shards(): lax.ppermute(tokens[here - 1], 'row', [(i, i + 1) for i in range(count -...  3.64 us
    pallas_call x1, Pallas kernels, shards(): call(functools.partial(out_kernel, heads=heads), jax.ShapeDtypeStruct((am...  3.15 us
    pallas_call x1, Pallas kernels, shards(): call(query_kernel, jax.ShapeDtypeStruct((amount, heads * nfeat), BF), 3,...  2.45 us
    pallas_call x1, Pallas kernels, shards(): call(conv_kernel_body, jax.ShapeDtypeStruct((here, cols, width), F32), 5,...  1.99 us
  transfers between devices with their start and end apart: 8, of which 5 were waited for; matrix products, arithmetic and copies ran while one was open for 3% of the time, Pallas kernels for 7%

profile of v1, /device:TPU:1, one launch (start us, length us, event | category | flops | bytes accessed | tf_op | source)
XLA Modules:
  0.0 59.6 jit_solution(13349750332486383354)
XLA Ops:
  0.0 0.0 copy-start
  0.0 1.1 %copy-done = bf16[2,256,768]{2,1,0:T(8,128)(2,1)S(1)} copy-done((bf16[2,256,768]{2,1,0:T(8,128)(2,1)S(1)}, bf16[2,256,768]{2,1,0:T(8,128)(2,1)}, u32[]{:S(2)}) %copy-start) | copy-done | bytes 786456
  1.1 0.0 copy-start.3
  1.1 1.3 %copy-done.3 = bf16[768,768]{1,0:T(8,128)(2,1)S(1)} copy-done((bf16[768,768]{1,0:T(8,128)(2,1)S(1)}, bf16[768,768]{1,0:T(8,128)(2,1)}, u32[]{:S(2)}) %copy-start.3) | copy-done | bytes 1179672
  2.4 0.0 copy-start.6
  2.4 1.0 %copy-done.6 = bf16[12,64,256]{2,1,0:T(8,128)(2,1)S(1)} copy-done((bf16[12,64,256]{2,1,0:T(8,128)(2,1)S(1)}, bf16[12,64,256]{2,1,0:T(8,128)(2,1)}, u32[]{:S(2)}) %copy-start.6) | copy-done | bytes 393240
  3.4 0.0 copy-start.9
  3.4 1.3 %copy-done.9 = bf16[768,768]{1,0:T(8,128)(2,1)S(1)} copy-done((bf16[768,768]{1,0:T(8,128)(2,1)S(1)}, bf16[768,768]{1,0:T(8,128)(2,1)}, u32[]{:S(2)}) %copy-start.9) | copy-done | bytes 1179672
  4.7 4.1 %shard_map.82 = (bf16[2,400,256]{2,1,0:T(8,128)(2,1)S(1)}, bf16[512,768]{1,0:T(8,128)(2,1)S(1)}) custom-call(s32[1]{0:T(128)} %bitcast.flip_ref, bf16[512,768]{1,0:T(8,128)(2,1)S(1)} %bitcast.23, bf16[768,768]{1,0:T(8,128)(2,1)S(1)} %copy-done.9, bf16[768,768]{1,0:T(8,128)(2,1)S(1)} %copy-done.3, bf16[12,64,256]{2,1,0:T(8,128)(2,1)S(1)} %copy-done.6), custom_call_target="tpu_custom_call" | custom-call | flops 1610612736 | tf_op jit(solution)/shard_map/pallas_call | solution.py:208
  8.7 1.3 %collective-permute-start = (bf16[2,400,256]{2,1,0:T(8,128)(2,1)S(1)}, bf16[2,400,256]{2,1,0:T(8,128)(2,1)S(1)}, u32[]{:S(2)}, u32[]{:S(2)}) collective-permute-start(bf16[2,400,256]{2,1,0:T(8,128)(2,1)S(1)} %get-tuple-element.7), channel_id=1, source_target_pairs={{0,1},{2,3},{4,5},{6,7},{8,9},{10,11},{12,13},{14,15},{16,17},{18,... | collective-permute-start | bytes 1228808 | tf_op jit(solution)/shard_map/ppermute | solution.py:176
  10.0 2.3 %collective-permute-done = bf16[2,400,256]{2,1,0:T(8,128)(2,1)S(1)} collective-permute-done((bf16[2,400,256]{2,1,0:T(8,128)(2,1)S(1)}, bf16[2,400,256]{2,1,0:T(8,128)(2,1)S(1)}, u32[]{:S(2)}, u32[]{:S(2)}) %collective-permute-start) | collective-permute-done | bytes 409632 | tf_op jit(solution)/shard_map/ppermute | solution.py:176
  12.4 0.1 convert_add_fusion
  12.5 3.9 %collective-permute-start.1 = (bf16[400,256]{1,0:T(8,128)(2,1)S(1)}, bf16[400,256]{1,0:T(8,128)(2,1)S(1)}, u32[]{:S(2)}, u32[]{:S(2)}) collective-permute-start(bf16[400,256]{1,0:T(8,128)(2,1)S(1)} %fusion.2), channel_id=1, source_target_pairs={{1,3},{3,1},{5,7},{7,5},{9,11},{11,9},{13,15},{15,13},{17,19},{19,... | collective-permute-start | bytes 614408 | tf_op jit(solution)/shard_map/ppermute | solution.py:176
  16.4 3.1 %collective-permute-done.1 = bf16[400,256]{1,0:T(8,128)(2,1)S(1)} collective-permute-done((bf16[400,256]{1,0:T(8,128)(2,1)S(1)}, bf16[400,256]{1,0:T(8,128)(2,1)S(1)}, u32[]{:S(2)}, u32[]{:S(2)}) %collective-permute-start.1) | collective-permute-done | bytes 204832 | tf_op jit(solution)/shard_map/ppermute | solution.py:176
  19.6 3.5 %collective-permute-start.2 = (bf16[400,256]{1,0:T(8,128)(2,1)S(1)}, bf16[400,256]{1,0:T(8,128)(2,1)S(1)}, u32[]{:S(2)}, u32[]{:S(2)}) collective-permute-start(bf16[400,256]{1,0:T(8,128)(2,1)S(1)} %fusion.3), channel_id=1, source_target_pairs={{1,5},{3,7},{5,1},{7,3},{9,13},{11,15},{13,9},{15,11},{17,21},{19,... | collective-permute-start | bytes 614408 | tf_op jit(solution)/shard_map/ppermute | solution.py:176
  23.1 3.1 %collective-permute-done.2 = bf16[400,256]{1,0:T(8,128)(2,1)S(1)} collective-permute-done((bf16[400,256]{1,0:T(8,128)(2,1)S(1)}, bf16[400,256]{1,0:T(8,128)(2,1)S(1)}, u32[]{:S(2)}, u32[]{:S(2)}) %collective-permute-start.2) | collective-permute-done | bytes 204832 | tf_op jit(solution)/shard_map/ppermute | solution.py:176
  26.2 0.1 fusion.1
  26.3 4.4 %collective-permute-start.3 = (bf16[400,256]{1,0:T(8,128)(2,1)S(1)}, bf16[400,256]{1,0:T(8,128)(2,1)S(1)}, u32[]{:S(2)}, u32[]{:S(2)}) collective-permute-start(bf16[400,256]{1,0:T(8,128)(2,1)S(1)} %fusion.1), channel_id=1, source_target_pairs={{1,9},{3,11},{5,13},{7,15},{9,1},{11,3},{13,5},{15,7},{17,25},{19,... | collective-permute-start | bytes 614408 | tf_op jit(solution)/shard_map/ppermute | solution.py:176
  30.7 5.3 %collective-permute-done.3 = bf16[400,256]{1,0:T(8,128)(2,1)S(1)} collective-permute-done((bf16[400,256]{1,0:T(8,128)(2,1)S(1)}, bf16[400,256]{1,0:T(8,128)(2,1)S(1)}, u32[]{:S(2)}, u32[]{:S(2)}) %collective-permute-start.3) | collective-permute-done | bytes 204832 | tf_op jit(solution)/shard_map/ppermute | solution.py:176
  36.0 0.1 add_convert_fusion
  36.1 0.0 copy-start.10
  36.1 0.0 copy-start.14
  36.1 0.0 copy-start.1
  36.1 0.0 copy-start.5
  36.1 3.3 %collective-permute-start.4 = (bf16[400,256]{1,0:T(8,128)(2,1)S(1)}, bf16[400,256]{1,0:T(8,128)(2,1)S(1)}, u32[]{:S(2)}, u32[]{:S(2)}) collective-permute-start(bf16[400,256]{1,0:T(8,128)(2,1)S(1)} %add_convert_fusion), channel_id=1, source_target_pairs={{1,3},{3,1},{5,7},{7,5},{9,11},{11,9},{13,15},{15,13},{17,19},{19,... | collective-permute-start | bytes 614408 | tf_op jit(solution)/shard_map/ppermute | solution.py:176
  39.4 0.9 %slice_bitcast_fusion.1 = (bf16[256,768]{1,0:T(8,128)(2,1)}, bf16[256,768]{1,0:T(8,128)(2,1)}) fusion(bf16[2,256,768]{2,1,0:T(8,128)(2,1)S(1)} %copy-done), kind=kLoop, calls=%fused_computation.8 | loop fusion | bytes 1572864 | tf_op jit(solution)/shard_map/squeeze | solution.py:206
  40.4 1.9 %collective-permute-start.7 = (bf16[256,768]{1,0:T(8,128)(2,1)}, bf16[256,768]{1,0:T(8,128)(2,1)S(1)}, u32[]{:S(2)}, u32[]{:S(2)}) collective-permute-start(bf16[256,768]{1,0:T(8,128)(2,1)} %get-tuple-element.9), channel_id=1, source_target_pairs={{1,0},{2,1},{3,2},{4,3},{5,4},{6,5},{7,6},{8,7},{9,8},{10,9},{11,1... | collective-permute-start | bytes 1179656 | tf_op jit(solution)/shard_map/ppermute | solution.py:206
  42.3 3.6 %collective-permute-start.6 = (bf16[256,768]{1,0:T(8,128)(2,1)}, bf16[256,768]{1,0:T(8,128)(2,1)S(1)}, u32[]{:S(2)}, u32[]{:S(2)}) collective-permute-start(bf16[256,768]{1,0:T(8,128)(2,1)} %get-tuple-element.10), channel_id=1, source_target_pairs={{0,1},{1,2},{2,3},{3,4},{4,5},{5,6},{6,7},{7,8},{8,9},{9,10},{10,1... | collective-permute-start | bytes 1179656 | tf_op jit(solution)/shard_map/ppermute | solution.py:205
  46.0 0.0 collective-permute-done.4
  46.0 0.0 copy-start.12
  46.0 0.7 %copy-done.12 = bf16[400,256]{1,0:T(8,128)(2,1)} copy-done((bf16[400,256]{1,0:T(8,128)(2,1)}, bf16[400,256]{1,0:T(8,128)(2,1)S(1)}, u32[]{:S(2)}) %copy-start.12) | copy-done | bytes 204824
  46.7 0.8 %pad_maximum_fusion = bf16[2,400,256]{2,1,0:T(8,128)(2,1)} fusion(bf16[1,400,256]{2,1,0:T(8,128)(2,1)S(1)} %bitcast.30, bf16[1,400,256]{2,1,0:T(8,128)(2,1)S(1)} %bitcast.28), kind=kLoop, calls=%fused_computation.4 | loop fusion | flops 204800 | bytes 819200 | tf_op jit(solution)/shard_map/stack | solution.py:189
  47.4 0.0 copy-done.10
  47.4 2.0 %collective-permute-start.5 = (bf16[2,400,256]{2,1,0:T(8,128)(2,1)}, bf16[2,400,256]{2,1,0:T(8,128)(2,1)}, u32[]{:S(2)}, u32[]{:S(2)}) collective-permute-start(bf16[2,400,256]{2,1,0:T(8,128)(2,1)} %pad_maximum_fusion), channel_id=1, source_target_pairs={{1,0},{3,2},{5,4},{7,6},{9,8},{11,10},{13,12},{15,14},{17,16},{19,... | collective-permute-start | bytes 1228808 | tf_op jit(solution)/shard_map/ppermute | solution.py:176
  49.5 0.0 copy-done.14
  49.5 0.0 copy-done.1
  49.5 0.0 copy-done.5
  49.5 0.0 copy-start.7
  49.5 1.0 %copy-done.7 = bf16[12,64,256]{2,1,0:T(8,128)(2,1)S(1)} copy-done((bf16[12,64,256]{2,1,0:T(8,128)(2,1)S(1)}, bf16[12,64,256]{2,1,0:T(8,128)(2,1)}, u32[]{:S(2)}) %copy-start.7) | copy-done | bytes 393240
  50.5 0.0 copy-start.4
  50.5 0.0 copy-start.8
  50.5 2.5 %shard_map.83.feat_ref = bf16[512,3072]{1,0:T(8,128)(2,1)S(1)} custom-call(bf16[512,768]{1,0:T(8,128)(2,1)S(1)} %bitcast.24, bf16[768,768]{1,0:T(8,128)(2,1)S(1)} %copy-done.5, bf16[12,64,256]{2,1,0:T(8,128)(2,1)S(1)} %copy-done.7), custom_call_target="tpu_custom_call" | custom-call | flops 805306368 | tf_op jit(solution)/shard_map/pallas_call | solution.py:218
  53.0 0.0 collective-permute-done.7.low_ref
  53.0 0.2 collective-permute-done.6.top_ref
  53.2 0.0 copy-done.4
  53.2 0.0 copy-done.8
  53.2 0.0 copy-start.11
  53.2 0.0 copy-start.13
  53.2 2.0 %shard_map.84 = f32[2,256,768]{2,1,0:T(8,128)S(1)} custom-call(bf16[256,768]{1,0:T(8,128)(2,1)S(1)} %collective-permute-done.6.top_ref, bf16[2,256,768]{2,1,0:T(8,128)(2,1)S(1)} %bitcast.27, bf16[256,768]{1,0:T(8,128)(2,1)S(1)} %collective-permute-done.7.low_ref, bf16[768,768]{1,0:T(8,128)(2,1)S(1)} %copy-done.4, f32[3,3,768]{2,1,0:T(4,128)S(1)} %copy-done.8), custom_call_target="tpu_custom_call" | custom-call | flops 603979776 | tf_op jit(solution)/shard_map/pallas_call | solution.py:226
  55.2 0.0 copy-start.2
  55.2 0.0 collective-permute-done.5
  55.2 0.0 copy-done.11
  55.3 0.0 copy-done.13
  55.3 0.1 broadcast_select_fusion.state_ref
  55.3 1.2 %copy-done.2 = bf16[768,768]{1,0:T(8,128)(2,1)S(1)} copy-done((bf16[768,768]{1,0:T(8,128)(2,1)S(1)}, bf16[768,768]{1,0:T(8,128)(2,1)}, u32[]{:S(2)}) %copy-start.2) | copy-done | bytes 1179672
  56.5 3.1 %shard_map.85 = bf16[512,768]{1,0:T(8,128)(2,1)} custom-call(s32[1]{0:T(128)} %bitcast.flip_ref, bf16[2,400,256]{2,1,0:T(8,128)(2,1)S(1)} %broadcast_select_fusion.state_ref, bf16[512,3072]{1,0:T(8,128)(2,1)S(1)} %shard_map.83.feat_ref, f32[512,768]{1,0:T(8,128)S(1)} %bitcast.26, bf16[512,768]{1,0:T(8,128)(2,1)S(1)} %bitcast.25, ...), custom_call_target="tpu_custom_call" | custom-call | flops 1006632960 | tf_op jit(solution)/shard_map/pallas_call | solution.py:235
  (3 shorter events, 0.1 us)
Async XLA Ops:
  0.0 1.1 %copy-start = (bf16[2,256,768]{2,1,0:T(8,128)(2,1)S(1)}, bf16[2,256,768]{2,1,0:T(8,128)(2,1)}, u32[]{:S(2)}) copy-start(bf16[2,256,768]{2,1,0:T(8,128)(2,1)} %param.8) | copy-start | bytes 2359300
  1.1 1.3 %copy-start.3 = (bf16[768,768]{1,0:T(8,128)(2,1)S(1)}, bf16[768,768]{1,0:T(8,128)(2,1)}, u32[]{:S(2)}) copy-start(bf16[768,768]{1,0:T(8,128)(2,1)} %wv_ref.3) | copy-start | bytes 3538948
  2.4 1.0 %copy-start.6 = (bf16[12,64,256]{2,1,0:T(8,128)(2,1)S(1)}, bf16[12,64,256]{2,1,0:T(8,128)(2,1)}, u32[]{:S(2)}) copy-start(bf16[12,64,256]{2,1,0:T(8,128)(2,1)} %omega_ref.3) | copy-start | bytes 1179652
  3.4 1.3 %copy-start.9 = (bf16[768,768]{1,0:T(8,128)(2,1)S(1)}, bf16[768,768]{1,0:T(8,128)(2,1)}, u32[]{:S(2)}) copy-start(bf16[768,768]{1,0:T(8,128)(2,1)} %wk_ref.1) | copy-start | bytes 3538948
  8.7 3.6 %collective-permute-start = (bf16[2,400,256]{2,1,0:T(8,128)(2,1)S(1)}, bf16[2,400,256]{2,1,0:T(8,128)(2,1)S(1)}, u32[]{:S(2)}, u32[]{:S(2)}) collective-permute-start(bf16[2,400,256]{2,1,0:T(8,128)(2,1)S(1)} %get-tuple-element.7), channel_id=1, source_target_pairs={{0,1},{2,3},{4,5},{6,7},{8,9},{10,11},{12,13},{14,15},{16,17},{18,... | collective-permute-start | bytes 1228808 | tf_op jit(solution)/shard_map/ppermute | solution.py:176
  12.5 7.1 %collective-permute-start.1 = (bf16[400,256]{1,0:T(8,128)(2,1)S(1)}, bf16[400,256]{1,0:T(8,128)(2,1)S(1)}, u32[]{:S(2)}, u32[]{:S(2)}) collective-permute-start(bf16[400,256]{1,0:T(8,128)(2,1)S(1)} %fusion.2), channel_id=1, source_target_pairs={{1,3},{3,1},{5,7},{7,5},{9,11},{11,9},{13,15},{15,13},{17,19},{19,... | collective-permute-start | bytes 614408 | tf_op jit(solution)/shard_map/ppermute | solution.py:176
  19.6 6.6 %collective-permute-start.2 = (bf16[400,256]{1,0:T(8,128)(2,1)S(1)}, bf16[400,256]{1,0:T(8,128)(2,1)S(1)}, u32[]{:S(2)}, u32[]{:S(2)}) collective-permute-start(bf16[400,256]{1,0:T(8,128)(2,1)S(1)} %fusion.3), channel_id=1, source_target_pairs={{1,5},{3,7},{5,1},{7,3},{9,13},{11,15},{13,9},{15,11},{17,21},{19,... | collective-permute-start | bytes 614408 | tf_op jit(solution)/shard_map/ppermute | solution.py:176
  26.3 9.7 %collective-permute-start.3 = (bf16[400,256]{1,0:T(8,128)(2,1)S(1)}, bf16[400,256]{1,0:T(8,128)(2,1)S(1)}, u32[]{:S(2)}, u32[]{:S(2)}) collective-permute-start(bf16[400,256]{1,0:T(8,128)(2,1)S(1)} %fusion.1), channel_id=1, source_target_pairs={{1,9},{3,11},{5,13},{7,15},{9,1},{11,3},{13,5},{15,7},{17,25},{19,... | collective-permute-start | bytes 614408 | tf_op jit(solution)/shard_map/ppermute | solution.py:176
  36.1 11.3 %copy-start.10 = (bf16[400,256]{1,0:T(8,128)(2,1)}, bf16[400,256]{1,0:T(8,128)(2,1)S(1)}, u32[]{:S(2)}) copy-start(bf16[400,256]{1,0:T(8,128)(2,1)S(1)} %add_convert_fusion) | copy-start | bytes 614404
  36.1 13.4 %copy-start.14 = (f32[768]{0:T(1024)S(1)}, f32[768]{0:T(1024)}, u32[]{:S(2)}) copy-start(f32[768]{0:T(1024)} %param.15) | copy-start | bytes 9220
  36.1 13.4 %copy-start.1 = (bf16[2,256,768]{2,1,0:T(8,128)(2,1)S(1)}, bf16[2,256,768]{2,1,0:T(8,128)(2,1)}, u32[]{:S(2)}) copy-start(bf16[2,256,768]{2,1,0:T(8,128)(2,1)} %param.8) | copy-start | bytes 2359300
  36.1 13.4 %copy-start.5 = (bf16[768,768]{1,0:T(8,128)(2,1)S(1)}, bf16[768,768]{1,0:T(8,128)(2,1)}, u32[]{:S(2)}) copy-start(bf16[768,768]{1,0:T(8,128)(2,1)} %wq_ref.1) | copy-start | bytes 3538948
  36.1 9.8 %collective-permute-start.4 = (bf16[400,256]{1,0:T(8,128)(2,1)S(1)}, bf16[400,256]{1,0:T(8,128)(2,1)S(1)}, u32[]{:S(2)}, u32[]{:S(2)}) collective-permute-start(bf16[400,256]{1,0:T(8,128)(2,1)S(1)} %add_convert_fusion), channel_id=1, source_target_pairs={{1,3},{3,1},{5,7},{7,5},{9,11},{11,9},{13,15},{15,13},{17,19},{19,... | collective-permute-start | bytes 614408 | tf_op jit(solution)/shard_map/ppermute | solution.py:176
  40.4 12.6 %collective-permute-start.7 = (bf16[256,768]{1,0:T(8,128)(2,1)}, bf16[256,768]{1,0:T(8,128)(2,1)S(1)}, u32[]{:S(2)}, u32[]{:S(2)}) collective-permute-start(bf16[256,768]{1,0:T(8,128)(2,1)} %get-tuple-element.9), channel_id=1, source_target_pairs={{1,0},{2,1},{3,2},{4,3},{5,4},{6,5},{7,6},{8,7},{9,8},{10,9},{11,1... | collective-permute-start | bytes 1179656 | tf_op jit(solution)/shard_map/ppermute | solution.py:206
  42.3 10.9 %collective-permute-start.6 = (bf16[256,768]{1,0:T(8,128)(2,1)}, bf16[256,768]{1,0:T(8,128)(2,1)S(1)}, u32[]{:S(2)}, u32[]{:S(2)}) collective-permute-start(bf16[256,768]{1,0:T(8,128)(2,1)} %get-tuple-element.10), channel_id=1, source_target_pairs={{0,1},{1,2},{2,3},{3,4},{4,5},{5,6},{6,7},{7,8},{8,9},{9,10},{10,1... | collective-permute-start | bytes 1179656 | tf_op jit(solution)/shard_map/ppermute | solution.py:205
  46.0 0.7 %copy-start.12 = (bf16[400,256]{1,0:T(8,128)(2,1)}, bf16[400,256]{1,0:T(8,128)(2,1)S(1)}, u32[]{:S(2)}) copy-start(bf16[400,256]{1,0:T(8,128)(2,1)S(1)} %collective-permute-done.4) | copy-start | bytes 614404
  47.4 7.8 %collective-permute-start.5 = (bf16[2,400,256]{2,1,0:T(8,128)(2,1)}, bf16[2,400,256]{2,1,0:T(8,128)(2,1)}, u32[]{:S(2)}, u32[]{:S(2)}) collective-permute-start(bf16[2,400,256]{2,1,0:T(8,128)(2,1)} %pad_maximum_fusion), channel_id=1, source_target_pairs={{1,0},{3,2},{5,4},{7,6},{9,8},{11,10},{13,12},{15,14},{17,16},{19,... | collective-permute-start | bytes 1228808 | tf_op jit(solution)/shard_map/ppermute | solution.py:176
  49.5 1.0 %copy-start.7 = (bf16[12,64,256]{2,1,0:T(8,128)(2,1)S(1)}, bf16[12,64,256]{2,1,0:T(8,128)(2,1)}, u32[]{:S(2)}) copy-start(bf16[12,64,256]{2,1,0:T(8,128)(2,1)} %omega_ref.3) | copy-start | bytes 1179652
  50.5 2.7 %copy-start.4 = (bf16[768,768]{1,0:T(8,128)(2,1)S(1)}, bf16[768,768]{1,0:T(8,128)(2,1)}, u32[]{:S(2)}) copy-start(bf16[768,768]{1,0:T(8,128)(2,1)} %wv_ref.3) | copy-start | bytes 3538948
  50.5 2.7 %copy-start.8 = (f32[3,3,768]{2,1,0:T(4,128)S(1)}, f32[3,3,768]{2,1,0:T(4,128)}, u32[]{:S(2)}) copy-start(f32[3,3,768]{2,1,0:T(4,128)} %taps_ref.1) | copy-start | bytes 82948
  53.2 2.0 %copy-start.11 = (bf16[400,256]{1,0:T(8,128)(2,1)S(1)}, bf16[400,256]{1,0:T(8,128)(2,1)}, u32[]{:S(2)}) copy-start(bf16[400,256]{1,0:T(8,128)(2,1)} %copy-done.10) | copy-start | bytes 614404
  53.2 2.0 %copy-start.13 = (bf16[400,256]{1,0:T(8,128)(2,1)S(1)}, bf16[400,256]{1,0:T(8,128)(2,1)}, u32[]{:S(2)}) copy-start(bf16[400,256]{1,0:T(8,128)(2,1)} %copy-done.12) | copy-start | bytes 614404
  55.2 1.3 %copy-start.2 = (bf16[768,768]{1,0:T(8,128)(2,1)S(1)}, bf16[768,768]{1,0:T(8,128)(2,1)}, u32[]{:S(2)}) copy-start(bf16[768,768]{1,0:T(8,128)(2,1)} %wo_ref.1) | copy-start | bytes 3538948

commit v2 on v1

v2 whole, which is shorter than its diff:
```python
import functools
import math

import jax
import jax.numpy as jnp
from jax import lax
from jax.experimental import pallas as pl
from jax.experimental.pallas import tpu as pltpu
from jax.sharding import PartitionSpec as P


BF = jnp.bfloat16
F32 = jnp.float32
LOG2E = 1.4426950408889634
VMEM_LIMIT = 28 * 1024 * 1024
VMEM_ALL = 67043328


def tiles_of(total, wanted):
    return wanted if total % wanted == 0 else total


def lift_scale(dim_head):
    return dim_head ** (-0.25) * LOG2E


def square_lanes(proj, dim_head, nfeat):
    quarter = dim_head // 2
    wide = 2 * dim_head
    scale = lift_scale(dim_head)
    values = proj.astype(F32)
    square = values * values * (0.5 * dim_head ** (-0.5) * LOG2E / scale)
    both = square + pltpu.roll(square, wide - quarter, 1)
    both = both + 0.5 * math.log2(nfeat) / scale / quarter
    high = both.astype(BF).astype(F32)
    low = both - high
    lane = lax.broadcasted_iota(jnp.int32, both.shape, 1)
    return jnp.where(lane % dim_head < quarter, high, pltpu.roll(low, quarter, 1)).astype(BF)


def feature_tile(proj, pair_mat, dim_head, nfeat):
    both = jnp.concatenate([proj, square_lanes(proj, dim_head, nfeat)], axis=1)
    lifted = jnp.dot(both, pair_mat, preferred_element_type=F32)
    return jnp.exp2(lifted * lift_scale(dim_head)).astype(BF)


def fill_pairs(omega_ref, pair_ref):
    heads, dim_head, nfeat = omega_ref.shape
    wide = 2 * dim_head
    empty = jnp.zeros((dim_head, nfeat), BF)
    minus = jnp.full((dim_head, nfeat), -1.0, BF)
    for head in range(heads):
        side = head % 2
        mine, other = slice(side * nfeat, (side + 1) * nfeat), slice((1 - side) * nfeat, (2 - side) * nfeat)
        for base, block in ((0, omega_ref[head]), (wide, minus)):
            rows = slice(base + side * dim_head, base + (side + 1) * dim_head)
            pair_ref[head // 2, rows, mine] = block
            pair_ref[head // 2, rows, other] = empty


def state_kernel(place_ref, x_hbm, wk_hbm, wv_hbm, omega_hbm, *refs):
    heads, dim_head, nfeat = omega_hbm.shape
    tokens, _ = x_hbm.shape
    here = len(refs) - 9
    state_ref, value_refs = refs[0], refs[1 : 1 + here]
    x_ref, wk_ref, wv_ref, omega_ref, sems, pair_ref, vt_ref, feat_ref = refs[1 + here :]
    copies = [
        pltpu.make_async_copy(source, target, sems.at[i])
        for i, (source, target) in enumerate(((x_hbm, x_ref), (wv_hbm, wv_ref), (omega_hbm, omega_ref), (wk_hbm, wk_ref)))
    ]
    for copy in copies:
        copy.start()
    group = heads // 4
    mark = lax.broadcasted_iota(jnp.int32, (16, tokens), 0)
    for head in range(heads):
        vt_ref[head, dim_head:, :] = jnp.where(mark == head % group, 1.0, 0.0).astype(BF)
    copies[0].wait()
    copies[1].wait()
    x = x_ref[...]
    value = jnp.dot(x, wv_ref[...], preferred_element_type=F32).astype(BF)
    cols = tokens // here
    for row in range(here):
        value_refs[row][...] = value[row * cols : (row + 1) * cols]
    turned = value.T
    for head in range(heads):
        vt_ref[head, :dim_head, :] = turned[head * dim_head : (head + 1) * dim_head]
    copies[2].wait()
    fill_pairs(omega_ref, pair_ref)
    copies[3].wait()
    rows = tiles_of(tokens, 128)
    sums = None
    for first in range(0, heads, 4):
        count = min(4, heads - first)
        key = jnp.dot(x, wk_ref[:, first * dim_head : (first + count) * dim_head], preferred_element_type=F32).astype(BF)
        for pair in range(count // 2):
            which = first // 2 + pair
            for start in range(0, tokens, rows):
                proj = key[start : start + rows, pair * 2 * dim_head : (pair + 1) * 2 * dim_head]
                feat_ref[start : start + rows, :] = feature_tile(proj, pair_ref[which], dim_head, nfeat)
            for side in range(2):
                head = 2 * which + side
                local = jnp.dot(vt_ref[head], feat_ref[:, side * nfeat : (side + 1) * nfeat], preferred_element_type=F32)
                owner = head // group
                slot = 2 * lax.rem(place_ref[0] + owner // 2, 2) + lax.rem(place_ref[1] + owner % 2, 2)
                spot = head % group
                state_ref[slot, spot * dim_head : (spot + 1) * dim_head, :] = local[:dim_head].astype(BF)
                sums = local[dim_head:] if spot == 0 else sums + local[dim_head:]
                if spot == group - 1:
                    state_ref[slot, group * dim_head :, :] = sums.astype(BF)


def query_kernel(x_ref, wq_ref, omega_ref, feat_ref, pair_ref):
    heads, dim_head, nfeat = omega_ref.shape
    tokens = x_ref.shape[0]
    fill_pairs(omega_ref, pair_ref)
    rows = tiles_of(tokens, 128)
    for start in range(0, tokens, rows):
        query = jnp.dot(x_ref[start : start + rows, :], wq_ref[...], preferred_element_type=F32).astype(BF)
        for pair in range(heads // 2):
            proj = query[:, pair * 2 * dim_head : (pair + 1) * 2 * dim_head]
            feat_ref[start : start + rows, pair * 2 * nfeat : (pair + 1) * 2 * nfeat] = feature_tile(
                proj, pair_ref[pair], dim_head, nfeat
            )


def conv_kernel_body(*refs):
    taps_ref, out_ref = refs[-2:]
    values = refs[:-2]
    here, cols, width = out_ref.shape
    lanes = 128
    col = lax.broadcasted_iota(jnp.int32, (cols, lanes), 0)
    for start in range(0, width, lanes):
        cut = slice(start, start + lanes)
        wide = [value[:, cut].astype(F32) for value in values]
        for row in range(here):
            sums = []
            for shift in range(3):
                terms = [wide[row + step] * taps_ref[step, shift : shift + 1, cut] for step in range(3)]
                sums.append(terms[0] + terms[1] + terms[2])
            left = jnp.where(col == 0, 0.0, pltpu.roll(sums[0], 1, 0))
            right = jnp.where(col == cols - 1, 0.0, pltpu.roll(sums[2], cols - 1, 0))
            out_ref[row, :, cut] = left + sums[1] + right


def out_kernel(place_ref, state_ref, feat_ref, pos_ref, x_ref, gain_ref, wo_ref, out_ref, mat_ref, attn_ref, *, heads):
    tokens, width = x_ref.shape
    dim_head = width // heads
    nfeat = state_ref.shape[-1]
    group = heads // 4
    wide = 2 * dim_head
    mat_ref[...] = jnp.zeros_like(mat_ref)
    for head in range(heads):
        pair, side = head // 2, head % 2
        owner = head // group
        slot = 2 * lax.rem(place_ref[0] + owner // 2, 2) + lax.rem(place_ref[1] + owner % 2, 2)
        place = head % group
        cut = slice(side * nfeat, (side + 1) * nfeat)
        mat_ref[pair, side * dim_head : (side + 1) * dim_head, cut] = state_ref[slot, place * dim_head : (place + 1) * dim_head, :]
        sums = state_ref[slot, group * dim_head :, :][place : place + 1]
        mat_ref[pair, wide + side * dim_head : wide + (side + 1) * dim_head, cut] = jnp.broadcast_to(sums, (dim_head, nfeat))
    rows = tiles_of(tokens, 256)
    for start in range(0, tokens, rows):
        total = None
        for pair in range(heads // 2):
            both = lax.dot_general(
                feat_ref[start : start + rows, pair * 2 * nfeat : (pair + 1) * 2 * nfeat],
                mat_ref[pair],
                (((1,), (1,)), ((), ())),
                preferred_element_type=F32,
            )
            attn = both[:, :wide] / both[:, wide:]
            attn_ref[:, pair * wide : (pair + 1) * wide] = attn
            total = attn * attn if total is None else total + attn * attn
        scale = lax.rsqrt(jnp.sum(total, axis=1, keepdims=True) * (1.0 / width) + 1e-06)
        mixed = (attn_ref[...] * scale * gain_ref[...] + pos_ref[start : start + rows, :]).astype(BF)
        out = x_ref[start : start + rows, :].astype(F32) + jnp.dot(mixed, wo_ref[...], preferred_element_type=F32)
        out_ref[start : start + rows, :] = out.astype(BF)


def call(kernel, out_shape, in_specs, scratch, flops, limit=VMEM_LIMIT):
    out_specs = [pl.BlockSpec(memory_space=pltpu.VMEM)] * len(out_shape)
    return pl.pallas_call(
        kernel,
        out_shape=out_shape,
        in_specs=in_specs,
        out_specs=out_specs,
        scratch_shapes=scratch,
        compiler_params=pltpu.CompilerParams(vmem_limit_bytes=limit),
        cost_estimate=pl.CostEstimate(flops=flops, bytes_accessed=0, transcendentals=0),
    )


def swap(block, bit, count):
    return lax.ppermute(block, "row", [(i, i ^ bit) for i in range(count)])


def reduce_state(state, count):
    other = swap(state[2:], 1, count)
    chip = state[:2].astype(F32) + other.astype(F32)
    other = swap(chip[1].astype(BF), 2, count)
    part = chip[0] + other.astype(F32)
    bit = 4
    while bit < count:
        other = swap(part.astype(BF), bit, count)
        part = part + other.astype(F32)
        bit *= 2
    done = part.astype(BF)
    other = swap(done, 2, count)
    half = jnp.stack([done, other])
    other = swap(half, 1, count)
    return jnp.concatenate([half, other])


def layer(tokens, w_query, w_key, w_value, w_out, omega, conv_kernel, norm_gain):
    here, cols, width = tokens.shape
    heads, dim_head, nfeat = omega.shape
    count = lax.axis_size("row")
    flat = tokens.reshape(here * cols, width)
    amount = here * cols
    group = heads // 4
    spot = lax.axis_index("row").astype(jnp.int32)
    place = jnp.stack([lax.bitwise_and(spot, 1), lax.bitwise_and(lax.shift_right_logical(spot, 1), 1)])
    proj = 2 * amount * width * width
    feats = 2 * amount * width * nfeat
    pairs = pltpu.VMEM((heads // 2, 4 * dim_head, 2 * nfeat), BF)
    vmem = pl.BlockSpec(memory_space=pltpu.VMEM)
    smem = pl.BlockSpec(memory_space=pltpu.SMEM)
    hbm = pl.BlockSpec(memory_space=pltpu.HBM)

    state, *values = call(
        state_kernel,
        [jax.ShapeDtypeStruct((4, group * dim_head + 16, nfeat), BF)] + [jax.ShapeDtypeStruct((cols, width), BF)] * here,
        [smem] + [hbm] * 4,
        [
            pltpu.VMEM((amount, width), BF),
            pltpu.VMEM((width, width), BF),
            pltpu.VMEM((width, width), BF),
            pltpu.VMEM((heads, dim_head, nfeat), BF),
            pltpu.SemaphoreType.DMA((4,)),
            pairs,
            pltpu.VMEM((heads, dim_head + 16, amount), BF),
            pltpu.VMEM((amount, 2 * nfeat), BF),
        ],
        2 * proj + 2 * feats,
        VMEM_ALL - 2 * (amount * width + 4 * (group * dim_head + 16) * nfeat) - 10400000,
    )(place, flat, w_key, w_value, omega)
    top = lax.ppermute(values[-1], "row", [(i, i + 1) for i in range(count - 1)])
    low = lax.ppermute(values[0], "row", [(i + 1, i) for i in range(count - 1)])
    (feat_query,) = call(
        query_kernel, [jax.ShapeDtypeStruct((amount, heads * nfeat), BF)], [vmem] * 3, [pairs], proj + feats
    )(flat, w_query, omega)
    (position,) = call(
        conv_kernel_body, [jax.ShapeDtypeStruct((here, cols, width), F32)], [vmem] * (here + 3), [], proj
    )(top, *values, low, conv_kernel)
    final = reduce_state(state, count)
    (out,) = call(
        functools.partial(out_kernel, heads=heads),
        [jax.ShapeDtypeStruct((amount, width), BF)],
        [smem] + [vmem] * 6,
        [pltpu.VMEM((heads // 2, 4 * dim_head, 2 * nfeat), BF), pltpu.VMEM((tiles_of(amount, 256), width), F32)],
        proj + 2 * feats,
    )(place, final, feat_query, position.reshape(amount, width), flat, norm_gain.reshape(1, width), w_out)
    return out.reshape(here, cols, width)


def solution(mesh):
    return jax.shard_map(
        layer,
        mesh=mesh,
        in_specs=(P(("parts", "row"), None, None), P(), P(), P(), P(), P(), P(), P()),
        out_specs=P(("parts", "row"), None, None),
        check_vma=False,
    )
```

time: 60.2 us -> 50.3 us (0.84)
  the two profiles are of different devices: /device:TPU:1 before, /device:TPU:13 now
where the time goes in v2:
time: 50.3 us; the launch traced here: 50 us
  Pallas kernels  16.4 us (33%)
  waiting for transfers between devices  16.4 us (33%)
  starting transfers between devices  14.7 us (29%)
  other arithmetic  1.28 us (3%)
  local copies, waits for them, and re-layouts  1.01 us (2%)
    ppermute x6, waiting for transfers between devices, swap(): return lax.ppermute(block, 'row', [(i, i ^ bit) for i in range(count)])  16.4 us
    pallas_call x1, Pallas kernels, layer(): call(state_kernel, [jax.ShapeDtypeStruct((4, group * dim_head + 16, nfeat...  8.12 us
    ppermute x6, starting transfers between devices, swap(): return lax.ppermute(block, 'row', [(i, i ^ bit) for i in range(count)])  7.16 us
    ppermute x1, starting transfers between devices, layer(): lax.ppermute(values[-1], 'row', [(i, i + 1) for i in range(count - 1)])  5.65 us
    pallas_call x1, Pallas kernels, layer(): call(functools.partial(out_kernel, heads=heads), [jax.ShapeDtypeStruct((a...  3.69 us
    pallas_call x1, Pallas kernels, layer(): call(query_kernel, [jax.ShapeDtypeStruct((amount, heads * nfeat), BF)], [...  3.39 us
    ppermute x1, starting transfers between devices, layer(): low = lax.ppermute(values[0], 'row', [(i + 1, i) for i in range(count - 1)])  1.92 us
    pallas_call x1, Pallas kernels, layer(): call(conv_kernel_body, [jax.ShapeDtypeStruct((here, cols, width), F32)],...  1.18 us
  transfers between devices with their start and end apart: 8, of which 4 were waited for; matrix products, arithmetic and copies ran while one was open for 0% of the time, Pallas kernels for 9%

profile of v2, /device:TPU:13, one launch (start us, length us, event | category | flops | bytes accessed | tf_op | source)
XLA Modules:
  0.0 50.0 jit_solution(8709326067917052279)
XLA Ops:
  0.0 0.1 pad_add_fusion.place_ref
  0.1 8.1 %shard_map.82 = (bf16[4,208,256]{2,1,0:T(8,128)(2,1)}, bf16[256,768]{1,0:T(8,128)(2,1)S(1)}, bf16[256,768]{1,0:T(8,128)(2,1)S(1)}) custom-call(s32[2]{0:T(128)S(1)} %pad_add_fusion.place_ref, bf16[512,768]{1,0:T(8,128)(2,1)} %bitcast.20, bf16[768,768]{1,0:T(8,128)(2,1)} %wk_hbm.1, bf16[768,768]{1,0:T(8,128)(2,1)} %wv_hbm.1, bf16[12,64,256]{2,1,0:T(8,128)(2,1)} %omega_ref.1), custom_call_target="tpu_custom_call" | custom-call | flops 1610612736 | tf_op jit(solution)/shard_map/pallas_call | solution.py:230
  8.2 1.0 %slice.14 = bf16[2,208,256]{2,1,0:T(8,128)(2,1)S(1)} slice(bf16[4,208,256]{2,1,0:T(8,128)(2,1)} %get-tuple-element.8), slice={[2:4], [0:208], [0:256]} | slice | bytes 425984 | tf_op jit(solution)/shard_map/slice | solution.py:198
  9.2 0.7 %collective-permute-start = (bf16[2,208,256]{2,1,0:T(8,128)(2,1)S(1)}, bf16[2,208,256]{2,1,0:T(8,128)(2,1)S(1)}, u32[]{:S(2)}, u32[]{:S(2)}) collective-permute-start(bf16[2,208,256]{2,1,0:T(8,128)(2,1)S(1)} %slice.14), channel_id=1, source_target_pairs={{0,1},{1,0},{2,3},{3,2},{4,5},{5,4},{6,7},{7,6},{8,9},{9,8},{10,11... | collective-permute-start | bytes 638984 | tf_op jit(solution)/shard_map/ppermute | solution.py:194
  9.9 1.1 %collective-permute-done = bf16[2,208,256]{2,1,0:T(8,128)(2,1)S(1)} collective-permute-done((bf16[2,208,256]{2,1,0:T(8,128)(2,1)S(1)}, bf16[2,208,256]{2,1,0:T(8,128)(2,1)S(1)}, u32[]{:S(2)}, u32[]{:S(2)}) %collective-permute-start) | collective-permute-done | bytes 213024 | tf_op jit(solution)/shard_map/ppermute | solution.py:194
  11.0 0.0 copy-start.3
  11.0 1.0 %convert_add_fusion = f32[2,208,256]{2,1,0:T(8,128)S(1)} fusion(bf16[2,208,256]{2,1,0:T(8,128)(2,1)S(1)} %collective-permute-done, bf16[4,208,256]{2,1,0:T(8,128)(2,1)} %get-tuple-element.8), kind=kLoop, calls=%fused_computation.1 | loop fusion | flops 319488 | bytes 851968 | tf_op jit(solution)/shard_map/add | solution.py:199
  12.0 0.0 copy-start.5
  12.0 0.0 copy-start
  12.0 0.0 copy-start.2
  12.1 1.3 %collective-permute-start.1 = (bf16[208,256]{1,0:T(8,128)(2,1)S(1)}, bf16[208,256]{1,0:T(8,128)(2,1)S(1)}, u32[]{:S(2)}, u32[]{:S(2)}) collective-permute-start(bf16[208,256]{1,0:T(8,128)(2,1)S(1)} %fusion.2), channel_id=1, source_target_pairs={{0,2},{1,3},{2,0},{3,1},{4,6},{5,7},{6,4},{7,5},{8,10},{9,11},{10,... | collective-permute-start | bytes 319496 | tf_op jit(solution)/shard_map/ppermute | solution.py:194
  13.4 2.9 %collective-permute-done.1 = bf16[208,256]{1,0:T(8,128)(2,1)S(1)} collective-permute-done((bf16[208,256]{1,0:T(8,128)(2,1)S(1)}, bf16[208,256]{1,0:T(8,128)(2,1)S(1)}, u32[]{:S(2)}, u32[]{:S(2)}) %collective-permute-start.1) | collective-permute-done | bytes 106528 | tf_op jit(solution)/shard_map/ppermute | solution.py:194
  16.3 0.2 collective-permute-start.2
  16.6 3.4 %collective-permute-done.2 = bf16[208,256]{1,0:T(8,128)(2,1)S(1)} collective-permute-done((bf16[208,256]{1,0:T(8,128)(2,1)S(1)}, bf16[208,256]{1,0:T(8,128)(2,1)S(1)}, u32[]{:S(2)}, u32[]{:S(2)}) %collective-permute-start.2) | collective-permute-done | bytes 106528 | tf_op jit(solution)/shard_map/ppermute | solution.py:194
  20.0 2.4 %collective-permute-start.3 = (bf16[208,256]{1,0:T(8,128)(2,1)S(1)}, bf16[208,256]{1,0:T(8,128)(2,1)S(1)}, u32[]{:S(2)}, u32[]{:S(2)}) collective-permute-start(bf16[208,256]{1,0:T(8,128)(2,1)S(1)} %fusion.1), channel_id=1, source_target_pairs={{0,8},{1,9},{2,10},{3,11},{4,12},{5,13},{6,14},{7,15},{8,0},{9,1},... | collective-permute-start | bytes 319496 | tf_op jit(solution)/shard_map/ppermute | solution.py:194
  22.4 5.6 %collective-permute-start.6 = (bf16[256,768]{1,0:T(8,128)(2,1)S(1)}, bf16[256,768]{1,0:T(8,128)(2,1)S(1)}, u32[]{:S(2)}, u32[]{:S(2)}) collective-permute-start(bf16[256,768]{1,0:T(8,128)(2,1)S(1)} %get-tuple-element.9.refs_2_), channel_id=1, source_target_pairs={{0,1},{1,2},{2,3},{3,4},{4,5},{5,6},{6,7},{7,8},{8,9},{9,10},{10,1... | collective-permute-start | bytes 1179656 | tf_op jit(solution)/shard_map/ppermute | solution.py:247
  28.0 1.9 %collective-permute-start.7 = (bf16[256,768]{1,0:T(8,128)(2,1)S(1)}, bf16[256,768]{1,0:T(8,128)(2,1)S(1)}, u32[]{:S(2)}, u32[]{:S(2)}) collective-permute-start(bf16[256,768]{1,0:T(8,128)(2,1)S(1)} %get-tuple-element.10.refs_1_), channel_id=1, source_target_pairs={{1,0},{2,1},{3,2},{4,3},{5,4},{6,5},{7,6},{8,7},{9,8},{10,9},{11,1... | collective-permute-start | bytes 1179656 | tf_op jit(solution)/shard_map/ppermute | solution.py:248
  30.0 0.0 collective-permute-done.3
  30.0 0.1 add_convert_fusion
  30.0 0.2 collective-permute-start.4
  30.2 9.0 %collective-permute-done.4 = bf16[208,256]{1,0:T(8,128)(2,1)S(1)} collective-permute-done((bf16[208,256]{1,0:T(8,128)(2,1)S(1)}, bf16[208,256]{1,0:T(8,128)(2,1)S(1)}, u32[]{:S(2)}, u32[]{:S(2)}) %collective-permute-start.4) | collective-permute-done | bytes 106528 | tf_op jit(solution)/shard_map/ppermute | solution.py:194
  39.2 2.4 %collective-permute-start.5 = (bf16[2,208,256]{2,1,0:T(8,128)(2,1)S(1)}, bf16[2,208,256]{2,1,0:T(8,128)(2,1)S(1)}, u32[]{:S(2)}, u32[]{:S(2)}) collective-permute-start(bf16[2,208,256]{2,1,0:T(8,128)(2,1)S(1)} %pad_maximum_fusion.1), channel_id=1, source_target_pairs={{0,1},{1,0},{2,3},{3,2},{4,5},{5,4},{6,7},{7,6},{8,9},{9,8},{10,11... | collective-permute-start | bytes 638984 | tf_op jit(solution)/shard_map/ppermute | solution.py:194
  41.6 0.0 copy-done.5
  41.6 0.0 copy-done.3
  41.6 0.0 copy-done
  41.6 0.0 copy-done.2
  41.6 0.0 copy-start.4
  41.6 3.4 %shard_map.83.feat_ref = bf16[512,3072]{1,0:T(8,128)(2,1)S(1)} custom-call(bf16[512,768]{1,0:T(8,128)(2,1)S(1)} %bitcast.21, bf16[768,768]{1,0:T(8,128)(2,1)S(1)} %copy-done.2, bf16[12,64,256]{2,1,0:T(8,128)(2,1)S(1)} %copy-done.3), custom_call_target="tpu_custom_call" | custom-call | flops 805306368 | tf_op jit(solution)/shard_map/pallas_call | solution.py:249
  45.0 0.0 collective-permute-done.6.refs_0_
  45.0 0.0 collective-permute-done.7.refs_3_
  45.1 0.0 copy-done.4
  45.1 0.0 copy-start.1
  45.1 1.2 %shard_map.84 = f32[2,256,768]{2,1,0:T(8,128)S(1)} custom-call(bf16[256,768]{1,0:T(8,128)(2,1)S(1)} %collective-permute-done.6.refs_0_, bf16[256,768]{1,0:T(8,128)(2,1)S(1)} %get-tuple-element.10.refs_1_, bf16[256,768]{1,0:T(8,128)(2,1)S(1)} %get-tuple-element.9.refs_2_, bf16[256,768]{1,0:T(8,128)(2,1)S(1)} %collective-permute-done.7.refs_3_, ...), custom_call_target="tpu_custom_call" | custom-call | flops 603979776 | tf_op jit(solution)/shard_map/pallas_call | solution.py:252
  46.3 0.0 collective-permute-done.5
  46.3 0.0 copy-done.1
  46.3 3.7 %shard_map.85 = bf16[512,768]{1,0:T(8,128)(2,1)} custom-call(s32[2]{0:T(128)S(1)} %pad_add_fusion.place_ref, bf16[4,208,256]{2,1,0:T(8,128)(2,1)S(1)} %pad_maximum_fusion.state_ref, bf16[512,3072]{1,0:T(8,128)(2,1)S(1)} %shard_map.83.feat_ref, f32[512,768]{1,0:T(8,128)S(1)} %bitcast.19, bf16[512,768]{1,0:T(8,128)(2,1)S(1)} %bitcast.22, ...), custom_call_target="tpu_custom_call" | custom-call | flops 1006632960 | tf_op jit(solution)/shard_map/pallas_call | solution.py:256
  (6 shorter events, 0.1 us)
Async XLA Ops:
  9.2 1.8 %collective-permute-start = (bf16[2,208,256]{2,1,0:T(8,128)(2,1)S(1)}, bf16[2,208,256]{2,1,0:T(8,128)(2,1)S(1)}, u32[]{:S(2)}, u32[]{:S(2)}) collective-permute-start(bf16[2,208,256]{2,1,0:T(8,128)(2,1)S(1)} %slice.14), channel_id=1, source_target_pairs={{0,1},{1,0},{2,3},{3,2},{4,5},{5,4},{6,7},{7,6},{8,9},{9,8},{10,11... | collective-permute-start | bytes 638984 | tf_op jit(solution)/shard_map/ppermute | solution.py:194
  11.0 30.6 %copy-start.3 = (bf16[12,64,256]{2,1,0:T(8,128)(2,1)S(1)}, bf16[12,64,256]{2,1,0:T(8,128)(2,1)}, u32[]{:S(2)}) copy-start(bf16[12,64,256]{2,1,0:T(8,128)(2,1)} %omega_ref.1) | copy-start | bytes 1179652
  12.0 29.6 %copy-start.5 = (f32[768]{0:T(1024)S(1)}, f32[768]{0:T(1024)}, u32[]{:S(2)}) copy-start(f32[768]{0:T(1024)} %param.15) | copy-start | bytes 9220
  12.0 29.6 %copy-start = (bf16[2,256,768]{2,1,0:T(8,128)(2,1)S(1)}, bf16[2,256,768]{2,1,0:T(8,128)(2,1)}, u32[]{:S(2)}) copy-start(bf16[2,256,768]{2,1,0:T(8,128)(2,1)} %param.8) | copy-start | bytes 2359300
  12.0 29.6 %copy-start.2 = (bf16[768,768]{1,0:T(8,128)(2,1)S(1)}, bf16[768,768]{1,0:T(8,128)(2,1)}, u32[]{:S(2)}) copy-start(bf16[768,768]{1,0:T(8,128)(2,1)} %wq_ref.1) | copy-start | bytes 3538948
  12.1 4.2 %collective-permute-start.1 = (bf16[208,256]{1,0:T(8,128)(2,1)S(1)}, bf16[208,256]{1,0:T(8,128)(2,1)S(1)}, u32[]{:S(2)}, u32[]{:S(2)}) collective-permute-start(bf16[208,256]{1,0:T(8,128)(2,1)S(1)} %fusion.2), channel_id=1, source_target_pairs={{0,2},{1,3},{2,0},{3,1},{4,6},{5,7},{6,4},{7,5},{8,10},{9,11},{10,... | collective-permute-start | bytes 319496 | tf_op jit(solution)/shard_map/ppermute | solution.py:194
  16.3 3.6 %collective-permute-start.2 = (bf16[208,256]{1,0:T(8,128)(2,1)S(1)}, bf16[208,256]{1,0:T(8,128)(2,1)S(1)}, u32[]{:S(2)}, u32[]{:S(2)}) collective-permute-start(bf16[208,256]{1,0:T(8,128)(2,1)S(1)} %fusion.3), channel_id=1, source_target_pairs={{0,4},{1,5},{2,6},{3,7},{4,0},{5,1},{6,2},{7,3},{8,12},{9,13},{10,... | collective-permute-start | bytes 319496 | tf_op jit(solution)/shard_map/ppermute | solution.py:194
  20.0 10.0 %collective-permute-start.3 = (bf16[208,256]{1,0:T(8,128)(2,1)S(1)}, bf16[208,256]{1,0:T(8,128)(2,1)S(1)}, u32[]{:S(2)}, u32[]{:S(2)}) collective-permute-start(bf16[208,256]{1,0:T(8,128)(2,1)S(1)} %fusion.1), channel_id=1, source_target_pairs={{0,8},{1,9},{2,10},{3,11},{4,12},{5,13},{6,14},{7,15},{8,0},{9,1},... | collective-permute-start | bytes 319496 | tf_op jit(solution)/shard_map/ppermute | solution.py:194
  22.4 22.7 %collective-permute-start.6 = (bf16[256,768]{1,0:T(8,128)(2,1)S(1)}, bf16[256,768]{1,0:T(8,128)(2,1)S(1)}, u32[]{:S(2)}, u32[]{:S(2)}) collective-permute-start(bf16[256,768]{1,0:T(8,128)(2,1)S(1)} %get-tuple-element.9.refs_2_), channel_id=1, source_target_pairs={{0,1},{1,2},{2,3},{3,4},{4,5},{5,6},{6,7},{7,8},{8,9},{9,10},{10,1... | collective-permute-start | bytes 1179656 | tf_op jit(solution)/shard_map/ppermute | solution.py:247
  28.0 17.0 %collective-permute-start.7 = (bf16[256,768]{1,0:T(8,128)(2,1)S(1)}, bf16[256,768]{1,0:T(8,128)(2,1)S(1)}, u32[]{:S(2)}, u32[]{:S(2)}) collective-permute-start(bf16[256,768]{1,0:T(8,128)(2,1)S(1)} %get-tuple-element.10.refs_1_), channel_id=1, source_target_pairs={{1,0},{2,1},{3,2},{4,3},{5,4},{6,5},{7,6},{8,7},{9,8},{10,9},{11,1... | collective-permute-start | bytes 1179656 | tf_op jit(solution)/shard_map/ppermute | solution.py:248
  30.0 9.2 %collective-permute-start.4 = (bf16[208,256]{1,0:T(8,128)(2,1)S(1)}, bf16[208,256]{1,0:T(8,128)(2,1)S(1)}, u32[]{:S(2)}, u32[]{:S(2)}) collective-permute-start(bf16[208,256]{1,0:T(8,128)(2,1)S(1)} %add_convert_fusion), channel_id=1, source_target_pairs={{0,2},{1,3},{2,0},{3,1},{4,6},{5,7},{6,4},{7,5},{8,10},{9,11},{10,... | collective-permute-start | bytes 319496 | tf_op jit(solution)/shard_map/ppermute | solution.py:194
  39.2 7.0 %collective-permute-start.5 = (bf16[2,208,256]{2,1,0:T(8,128)(2,1)S(1)}, bf16[2,208,256]{2,1,0:T(8,128)(2,1)S(1)}, u32[]{:S(2)}, u32[]{:S(2)}) collective-permute-start(bf16[2,208,256]{2,1,0:T(8,128)(2,1)S(1)} %pad_maximum_fusion.1), channel_id=1, source_target_pairs={{0,1},{1,0},{2,3},{3,2},{4,5},{5,4},{6,7},{7,6},{8,9},{9,8},{10,11... | collective-permute-start | bytes 638984 | tf_op jit(solution)/shard_map/ppermute | solution.py:194
  41.6 3.4 %copy-start.4 = (f32[3,3,768]{2,1,0:T(4,128)S(1)}, f32[3,3,768]{2,1,0:T(4,128)}, u32[]{:S(2)}) copy-start(f32[3,3,768]{2,1,0:T(4,128)} %refs_4_.1) | copy-start | bytes 82948
  45.1 1.3 %copy-start.1 = (bf16[768,768]{1,0:T(8,128)(2,1)S(1)}, bf16[768,768]{1,0:T(8,128)(2,1)}, u32[]{:S(2)}) copy-start(bf16[768,768]{1,0:T(8,128)(2,1)} %wo_ref.1) | copy-start | bytes 3538948

commit v3 on v0

v3 whole, which is shorter than its diff:
```python
import math

import jax
import jax.numpy as jnp
from jax import lax
from jax.experimental import pallas as pl
from jax.experimental.pallas import tpu as pltpu
from jax.sharding import PartitionSpec as P


BF = jnp.bfloat16
F32 = jnp.float32
LOG2E = 1.4426950408889634
VMEM_LIMIT = 28 * 1024 * 1024
FIRST_LIMIT = 54500000


def tiles_of(total, wanted):
    return wanted if total % wanted == 0 else total


def feature_tile(proj, omega_pair, ones_pair, dim_head, nfeat):
    wide = 2 * dim_head
    lifted = jnp.dot(proj, omega_pair, preferred_element_type=F32)
    values = proj.astype(F32)
    square = values * values * (0.5 * dim_head ** (-0.5) * LOG2E)
    high = square.astype(BF)
    low = (square - high.astype(F32)).astype(BF)
    summed = jnp.dot(jnp.concatenate([high, low], axis=1), ones_pair, preferred_element_type=F32)
    parts = []
    for head in range(2):
        drop = summed[:, head * wide : (head + 1) * wide] + 0.5 * math.log2(nfeat)
        for part in range(nfeat // wide):
            start = head * nfeat + part * wide
            grown = lifted[:, start : start + wide] * (dim_head ** (-0.25) * LOG2E)
            parts.append(jnp.exp2(grown - drop).astype(BF))
    return jnp.concatenate(parts, axis=1)


def fill_pair(pair_ref, which, omegas):
    dim_head, nfeat = omegas[0].shape
    empty = jnp.zeros((dim_head, nfeat), BF)
    for side in range(2):
        rows = slice(side * dim_head, (side + 1) * dim_head)
        pair_ref[which, rows, side * nfeat : (side + 1) * nfeat] = omegas[side]
        pair_ref[which, rows, (1 - side) * nfeat : (2 - side) * nfeat] = empty


def fill_ones(ones_ref, dim_head):
    row = lax.broadcasted_iota(jnp.int32, ones_ref.shape, 0) // dim_head % 2
    col = lax.broadcasted_iota(jnp.int32, ones_ref.shape, 1) // (2 * dim_head)
    ones_ref[...] = jnp.where(row == col, 1.0, 0.0).astype(BF)


def fill_marks(vt_ref, group):
    heads, rows, tokens = vt_ref.shape
    mark = lax.broadcasted_iota(jnp.int32, (16, tokens), 0)
    for head in range(heads):
        vt_ref[head, rows - 16 :, :] = jnp.where(mark == head % group, 1.0, 0.0).astype(BF)


def half_state(bit, key, pair_ref, ones_ref, vt_ref, feat_ref, state_ref):
    heads, rows, tokens = vt_ref.shape
    dim_head = rows - 16
    nfeat = feat_ref.shape[1] // 2
    group = heads // 2
    tile = tiles_of(tokens, 128)
    sums = None
    for head in range(heads):
        pair, side = head // 2, head % 2
        if side == 0:
            for start in range(0, tokens, tile):
                proj = key[start : start + tile, pair * 2 * dim_head : (pair + 1) * 2 * dim_head]
                feat_ref[start : start + tile, :] = feature_tile(proj, pair_ref[pair], ones_ref[...], dim_head, nfeat)
        local = jnp.dot(vt_ref[head], feat_ref[:, side * nfeat : (side + 1) * nfeat], preferred_element_type=F32)
        slot = lax.rem(bit + head // group, 2)
        spot = head % group
        state_ref[slot, spot * dim_head : (spot + 1) * dim_head, :] = local[:dim_head].astype(state_ref.dtype)
        sums = local[dim_head:] if spot == 0 else sums + local[dim_head:]
        if spot == group - 1:
            state_ref[slot, group * dim_head :, :] = sums.astype(state_ref.dtype)


def first_kernel(place_ref, x_hbm, wk_hbm, wv_hbm, omega_hbm, *refs):
    heads, dim_head, _ = omega_hbm.shape
    tokens, width = x_hbm.shape
    here = len(refs) - 12
    send_ref, key_ref, own_ref = refs[:3]
    value_refs = refs[3 : 3 + here]
    x_ref, wk_ref, wv_ref, omega_ref, sems, pair_ref, ones_ref, vt_ref, feat_ref = refs[3 + here :]
    half, span = heads // 2, width // 2
    core = place_ref[0]
    sides = [pl.multiple_of((1 - core) * span, span), pl.multiple_of(core * span, span)]
    moves = [(x_hbm, x_ref)]
    moves += [(wv_hbm.at[:, pl.ds(side, span)], wv_ref.at[i]) for i, side in enumerate(sides)]
    moves += [(omega_hbm.at[pl.ds((1 - core) * half, half)], omega_ref)]
    moves += [(wk_hbm.at[:, pl.ds(side, span)], wk_ref.at[i]) for i, side in enumerate(sides)]
    copies = [pltpu.make_async_copy(source, target, sems.at[i]) for i, (source, target) in enumerate(moves)]
    for copy in copies:
        copy.start()
    fill_ones(ones_ref, dim_head)
    fill_marks(vt_ref, half // 2)
    copies[0].wait()
    x = x_ref[...]
    cols = tokens // here
    for i in range(2):
        copies[1 + i].wait()
        value = jnp.dot(x, wv_ref[i], preferred_element_type=F32).astype(BF)
        for row in range(here):
            value_refs[row][:, pl.ds(sides[i], span)] = value[row * cols : (row + 1) * cols]
        if i == 0:
            turned = value.T
            for head in range(half):
                vt_ref[head, :dim_head, :] = turned[head * dim_head : (head + 1) * dim_head]
        else:
            own_ref[...] = value
    copies[3].wait()
    for pair in range(half // 2):
        fill_pair(pair_ref, pair, [omega_ref[2 * pair], omega_ref[2 * pair + 1]])
    copies[4].wait()
    key = jnp.dot(x, wk_ref[0], preferred_element_type=F32).astype(BF)
    half_state(place_ref[1], key, pair_ref, ones_ref, vt_ref, feat_ref, send_ref)
    copies[5].wait()
    key_ref[...] = jnp.dot(x, wk_ref[1], preferred_element_type=F32).astype(BF)


def second_kernel(place_ref, key_ref, own_ref, omega_ref, state_ref, pair_ref, ones_ref, vt_ref, feat_ref):
    heads, dim_head, _ = omega_ref.shape
    half = heads // 2
    base = place_ref[0] * half
    fill_ones(ones_ref, dim_head)
    fill_marks(vt_ref, half // 2)
    turned = own_ref[...].T
    for head in range(half):
        vt_ref[head, :dim_head, :] = turned[head * dim_head : (head + 1) * dim_head]
    for pair in range(half // 2):
        fill_pair(pair_ref, pair, [omega_ref[base + 2 * pair], omega_ref[base + 2 * pair + 1]])
    half_state(place_ref[1], key_ref, pair_ref, ones_ref, vt_ref, feat_ref, state_ref)


def query_kernel(place_ref, x_ref, wq_ref, omega_ref, own_ref, other_ref, pair_ref, ones_ref):
    heads, dim_head, nfeat = omega_ref.shape
    tokens, width = x_ref.shape
    half, span = heads // 2, width // 2
    fill_ones(ones_ref, dim_head)
    tile = tiles_of(tokens, 128)
    for i, feat_ref in enumerate((own_ref, other_ref)):
        part = lax.rem(place_ref[0] + i, 2)
        weight = wq_ref[:, pl.ds(pl.multiple_of(part * span, span), span)]
        for pair in range(half // 2):
            head = part * half + 2 * pair
            fill_pair(pair_ref, i * (half // 2) + pair, [omega_ref[head], omega_ref[head + 1]])
        for start in range(0, tokens, tile):
            query = jnp.dot(x_ref[start : start + tile, :], weight, preferred_element_type=F32).astype(BF)
            for pair in range(half // 2):
                proj = query[:, pair * 2 * dim_head : (pair + 1) * 2 * dim_head]
                feat_ref[start : start + tile, pair * 2 * nfeat : (pair + 1) * 2 * nfeat] = feature_tile(
                    proj, pair_ref[i * (half // 2) + pair], ones_ref[...], dim_head, nfeat
                )


def conv_kernel_body(*refs):
    taps_ref, out_ref = refs[-2:]
    values = refs[:-2]
    here, cols, width = out_ref.shape
    lanes = 128
    col = lax.broadcasted_iota(jnp.int32, (cols, lanes), 0)
    for start in range(0, width, lanes):
        cut = slice(start, start + lanes)
        wide = [value[:, cut].astype(F32) for value in values]
        for row in range(here):
            sums = []
            for shift in range(3):
                terms = [wide[row + step] * taps_ref[step, shift : shift + 1, cut] for step in range(3)]
                sums.append(terms[0] + terms[1] + terms[2])
            left = jnp.where(col == 0, 0.0, pltpu.roll(sums[0], 1, 0))
            right = jnp.where(col == cols - 1, 0.0, pltpu.roll(sums[2], cols - 1, 0))
            out_ref[row, :, cut] = left + sums[1] + right


def fill_mats(bit, state_ref, mat_ref, dim_head):
    pairs, _, both = mat_ref.shape
    nfeat = both // 2
    group = pairs
    wide = 2 * dim_head
    empty = jnp.zeros((dim_head, nfeat), BF)
    for head in range(2 * pairs):
        pair, side = head // 2, head % 2
        slot = lax.rem(bit + head // group, 2)
        spot = head % group
        mine, other = slice(side * nfeat, (side + 1) * nfeat), slice((1 - side) * nfeat, (2 - side) * nfeat)
        sums = state_ref[slot, group * dim_head :, :][spot : spot + 1]
        for base, block in (
            (0, state_ref[slot, spot * dim_head : (spot + 1) * dim_head, :]),
            (wide, jnp.broadcast_to(sums, (dim_head, nfeat))),
        ):
            rows = slice(base + side * dim_head, base + (side + 1) * dim_head)
            mat_ref[pair, rows, mine] = block
            mat_ref[pair, rows, other] = empty


def attend(feat, mat, wide):
    both = lax.dot_general(feat, mat, (((1,), (1,)), ((), ())), preferred_element_type=F32)
    return both[:, :wide] / both[:, wide:]


def own_kernel(place_ref, state_ref, feat_ref, attn_ref, mat_ref):
    pairs, rows, both = mat_ref.shape
    wide = rows // 2
    tokens = attn_ref.shape[0]
    fill_mats(place_ref[1], state_ref, mat_ref, wide // 2)
    tile = tiles_of(tokens, 256)
    for start in range(0, tokens, tile):
        for pair in range(pairs):
            attn_ref[start : start + tile, pair * wide : (pair + 1) * wide] = attend(
                feat_ref[start : start + tile, pair * both : (pair + 1) * both], mat_ref[pair], wide
            )


def out_kernel(place_ref, state_ref, feat_ref, own_ref, pos_ref, x_ref, gain_ref, wo_ref, out_ref, mat_ref, attn_ref):
    pairs, rows, both = mat_ref.shape
    wide = rows // 2
    tokens, width = x_ref.shape
    span = width // 2
    core = place_ref[0]
    fill_mats(place_ref[1], state_ref, mat_ref, wide // 2)
    mine = pl.ds(pl.multiple_of(core * span, span), span)
    other = pl.ds(pl.multiple_of((1 - core) * span, span), span)
    tile = tiles_of(tokens, 256)
    for start in range(0, tokens, tile):
        cut = slice(start, start + tile)
        total = None
        for pair in range(pairs):
            lanes = slice(pair * wide, (pair + 1) * wide)
            attn = attend(feat_ref[cut, pair * both : (pair + 1) * both], mat_ref[pair], wide)
            attn_ref[:, lanes] = attn
            kept = own_ref[cut, lanes]
            square = attn * attn + kept * kept
            total = square if total is None else total + square
        scale = lax.rsqrt(jnp.sum(total, axis=1, keepdims=True) * (1.0 / width) + 1e-06)
        out = x_ref[cut, :].astype(F32)
        for part, attn in ((mine, own_ref[cut, :]), (other, attn_ref[...])):
            mixed = (attn * scale * gain_ref[:, part] + pos_ref[cut, part]).astype(BF)
            out = out + jnp.dot(mixed, wo_ref[part, :], preferred_element_type=F32)
        out_ref[cut, :] = out.astype(BF)


def call(kernel, out_shape, in_specs, scratch, flops, limit=VMEM_LIMIT):
    return pl.pallas_call(
        kernel,
        out_shape=out_shape,
        in_specs=in_specs,
        out_specs=[pl.BlockSpec(memory_space=pltpu.VMEM)] * len(out_shape),
        scratch_shapes=scratch,
        compiler_params=pltpu.CompilerParams(vmem_limit_bytes=limit),
        cost_estimate=pl.CostEstimate(flops=flops, bytes_accessed=0, transcendentals=0),
    )


def swap(block, bit, count):
    return lax.ppermute(block, "row", [(i, i ^ bit) for i in range(count)])


def reduce_half(send, keep, count, split):
    other = swap(send, 1, count)
    chip = keep + other.astype(F32)
    other = swap(chip[1].astype(BF), split, count)
    part = chip[0] + other.astype(F32)
    bit = count // 2
    while bit > 1:
        if bit != split:
            other = swap(part.astype(BF), bit, count)
            part = part + other.astype(F32)
        bit //= 2
    done = part.astype(BF)
    other = swap(done, split, count)
    return jnp.stack([done, other])


def layer(tokens, w_query, w_key, w_value, w_out, omega, conv_kernel, norm_gain):
    here, cols, width = tokens.shape
    heads, dim_head, nfeat = omega.shape
    count = lax.axis_size("row")
    split = min(4, count // 2)
    flat = tokens.reshape(here * cols, width)
    amount = here * cols
    half, span = heads // 2, width // 2
    rows = half // 2 * dim_head + 16
    spot = lax.axis_index("row").astype(jnp.int32)
    place = jnp.stack([lax.bitwise_and(spot, 1), lax.bitwise_and(lax.shift_right_logical(spot, split.bit_length() - 1), 1)])
    proj = 2 * amount * width * width
    feats = 2 * amount * width * nfeat
    vmem = pl.BlockSpec(memory_space=pltpu.VMEM)
    smem = pl.BlockSpec(memory_space=pltpu.SMEM)
    hbm = pl.BlockSpec(memory_space=pltpu.HBM)
    pairs = pltpu.VMEM((half // 2, 2 * dim_head, 2 * nfeat), BF)
    ones = pltpu.VMEM((4 * dim_head, 4 * dim_head), BF)
    turned = pltpu.VMEM((half, dim_head + 16, amount), BF)
    feat = pltpu.VMEM((amount, 2 * nfeat), BF)
    mats = pltpu.VMEM((half // 2, 4 * dim_head, 2 * nfeat), BF)

    send, key, own, *values = call(
        first_kernel,
        [
            jax.ShapeDtypeStruct((2, rows, nfeat), BF),
            jax.ShapeDtypeStruct((amount, span), BF),
            jax.ShapeDtypeStruct((amount, span), BF),
        ]
        + [jax.ShapeDtypeStruct((cols, width), BF)] * here,
        [smem] + [hbm] * 4,
        [
            pltpu.VMEM((amount, width), BF),
            pltpu.VMEM((2, width, span), BF),
            pltpu.VMEM((2, width, span), BF),
            pltpu.VMEM((half, dim_head, nfeat), BF),
            pltpu.SemaphoreType.DMA((6,)),
            pairs,
            ones,
            turned,
            feat,
        ],
        2 * proj + feats,
        FIRST_LIMIT,
    )(place, flat, w_key, w_value, omega)
    (keep,) = call(
        second_kernel,
        [jax.ShapeDtypeStruct((2, rows, nfeat), F32)],
        [smem] + [vmem] * 3,
        [pairs, ones, turned, feat],
        feats,
    )(place, key, own, omega)
    top = lax.ppermute(values[-1], "row", [(i, i + 1) for i in range(count - 1)])
    low = lax.ppermute(values[0], "row", [(i + 1, i) for i in range(count - 1)])
    feat_own, feat_other = call(
        query_kernel,
        [jax.ShapeDtypeStruct((amount, half * nfeat), BF)] * 2,
        [smem] + [vmem] * 3,
        [pltpu.VMEM((half, 2 * dim_head, 2 * nfeat), BF), ones],
        proj + feats,
    )(place, flat, w_query, omega)
    (position,) = call(
        conv_kernel_body, [jax.ShapeDtypeStruct((here, cols, width), F32)], [vmem] * (here + 3), [], proj
    )(top, *values, low, conv_kernel)
    mine = reduce_half(send, keep, count, split)
    theirs = swap(mine, 1, count)
    (attn,) = call(
        own_kernel, [jax.ShapeDtypeStruct((amount, span), F32)], [smem] + [vmem] * 2, [mats], feats
    )(place, mine, feat_own)
    (out,) = call(
        out_kernel,
        [jax.ShapeDtypeStruct((amount, width), BF)],
        [smem] + [vmem] * 7,
        [mats, pltpu.VMEM((tiles_of(amount, 256), span), F32)],
        proj + feats,
    )(place, theirs, feat_other, attn, position.reshape(amount, width), flat, norm_gain.reshape(1, width), w_out)
    return out.reshape(here, cols, width)


def solution(mesh):
    return jax.shard_map(
        layer,
        mesh=mesh,
        in_specs=(P(("parts", "row"), None, None), P(), P(), P(), P(), P(), P(), P()),
        out_specs=P(("parts", "row"), None, None),
        check_vma=False,
    )
```

time: 116 us -> 48.1 us (0.41)
  blocking collectives: 73 us -> 0 us
  matrix products: 21.9 us -> 0 us
  Pallas kernels: 0 us -> 17 us
  waiting for transfers between devices: 0.01 us -> 16.3 us
  starting transfers between devices: 4.42 us -> 14 us
  local copies, waits for them, and re-layouts: 8.3 us -> 0.14 us
  other arithmetic: 7.33 us -> 0.27 us
    psum x1 -> x0, blocking collectives: 73 us -> none  [shards(): lax.psum((local_state.reshape(nfeat, width), local_sum), 'row')]
    dot_general x9 -> x0, matrix products: 21.9 us -> none  [the longest x2 7.36 us: feature_map(): jnp.einsum('thd,hdf->thf', heads_in, omega, preferred_element_type=jnp.fl...]
    pallas_call x0 -> x6, Pallas kernels: none -> 17 us  [the longest x1 5.53 us: layer(): call(first_kernel, [jax.ShapeDtypeStruct((2, rows, nfeat), BF), jax.Shape...]
    ppermute x2 -> x8, waiting for transfers between devices: 0.01 us -> 16.3 us  [the longest x6 16.3 us: swap(): return lax.ppermute(block, 'row', [(i, i ^ bit) for i in range(count)])]
    ppermute x2 -> x8, starting transfers between devices: 4.42 us -> 14 us  [the longest x6 11.4 us: swap(): return lax.ppermute(block, 'row', [(i, i ^ bit) for i in range(count)])]
    convert_element_type x3 -> x1, local copies, waits for them, and re-layouts: 3.1 us -> 0.01 us  [reduce_half(): other = swap(chip[1].astype(BF), split, count)]
    convert_element_type x2 -> x3, other arithmetic: 3.11 us -> 0.12 us  [the longest x1 0.06 us: reduce_half(): done = part.astype(BF)]
    add x1, other arithmetic: 2.48 us -> 0.05 us  [reduce_half(): chip = keep + other.astype(F32)]
  transfers between devices with their start and end apart: 2 -> 8, of which waited for: 0 -> 4; matrix products, arithmetic and copies ran while one was open for 20% -> 0% of each run, Pallas kernels for 0% -> 17%
where the time goes in v3:
time: 48.1 us; the launch traced here: 47.9 us
  Pallas kernels  17 us (35%)
  waiting for transfers between devices  16.3 us (34%)
  starting transfers between devices  14 us (29%)
    ppermute x6, waiting for transfers between devices, swap(): return lax.ppermute(block, 'row', [(i, i ^ bit) for i in range(count)])  16.3 us
    ppermute x6, starting transfers between devices, swap(): return lax.ppermute(block, 'row', [(i, i ^ bit) for i in range(count)])  11.4 us
    pallas_call x1, Pallas kernels, layer(): call(first_kernel, [jax.ShapeDtypeStruct((2, rows, nfeat), BF), jax.Shape...  5.53 us
    pallas_call x1, Pallas kernels, layer(): call(query_kernel, [jax.ShapeDtypeStruct((amount, half * nfeat), BF)] * 2...  3.69 us
    pallas_call x1, Pallas kernels, layer(): call(out_kernel, [jax.ShapeDtypeStruct((amount, width), BF)], [smem] + [v...  3.53 us
    pallas_call x1, Pallas kernels, layer(): call(second_kernel, [jax.ShapeDtypeStruct((2, rows, nfeat), F32)], [smem]...  1.94 us
    ppermute x1, starting transfers between devices, layer(): lax.ppermute(values[-1], 'row', [(i, i + 1) for i in range(count - 1)])  1.3 us
    ppermute x1, starting transfers between devices, layer(): low = lax.ppermute(values[0], 'row', [(i + 1, i) for i in range(count - 1)])  1.29 us
  transfers between devices with their start and end apart: 8, of which 4 were waited for; matrix products, arithmetic and copies ran while one was open for 0% of the time, Pallas kernels for 17%

profile of v3, /device:TPU:0, one launch (start us, length us, event | category | flops | bytes accessed | tf_op | source)
XLA Modules:
  0.0 47.9 jit_solution(9528602429530023710)
XLA Ops:
  0.0 0.1 pad_add_fusion.place_ref
  0.1 0.0 copy-start.2
  0.1 5.5 %shard_map.82 = (bf16[2,208,256]{2,1,0:T(8,128)(2,1)S(1)}, bf16[512,384]{1,0:T(8,128)(2,1)S(1)}, bf16[512,384]{1,0:T(8,128)(2,1)S(1)}, bf16[256,768]{1,0:T(8,128)(2,1)S(1)}, bf16[256,768]{1,0:T(8,128)(2,1)S(1)}) custom-call(s32[2]{0:T(128)S(1)} %pad_add_fusion.place_ref, bf16[512,768]{1,0:T(8,128)(2,1)} %bitcast.20, bf16[768,768]{1,0:T(8,128)(2,1)} %wk_hbm.1, ...), custom_call_target="tpu_custom_call" | custom-call | flops 1409286144 | tf_op jit(solution)/shard_map/pallas_call | solution.py:302
  5.6 0.6 %collective-permute-start = (bf16[2,208,256]{2,1,0:T(8,128)(2,1)S(1)}, bf16[2,208,256]{2,1,0:T(8,128)(2,1)S(1)}, u32[]{:S(2)}, u32[]{:S(2)}) collective-permute-start(bf16[2,208,256]{2,1,0:T(8,128)(2,1)S(1)} %get-tuple-element.14), channel_id=1, source_target_pairs={{0,1},{1,0},{2,3},{3,2},{4,5},{5,4},{6,7},{7,6},{8,9},{9,8},{10,11... | collective-permute-start | bytes 638984 | tf_op jit(solution)/shard_map/ppermute | solution.py:261
  6.2 0.0 copy-done.2
  6.2 1.9 %shard_map.83 = f32[2,208,256]{2,1,0:T(8,128)S(1)} custom-call(s32[2]{0:T(128)S(1)} %pad_add_fusion.place_ref, bf16[512,384]{1,0:T(8,128)(2,1)S(1)} %get-tuple-element.12.key_ref, bf16[512,384]{1,0:T(8,128)(2,1)S(1)} %get-tuple-element.13.own_ref, bf16[12,64,256]{2,1,0:T(8,128)(2,1)S(1)} %copy-done.2), custom_call_target="tpu_custom_call" | custom-call | flops 201326592 | tf_op jit(solution)/shard_map/pallas_call | solution.py:325
  8.1 0.0 collective-permute-done
  8.2 0.0 copy-start.5
  8.2 0.0 copy-start.1
  8.2 0.0 copy-start.4
  8.2 2.7 %collective-permute-start.1 = (bf16[208,256]{1,0:T(8,128)(2,1)S(1)}, bf16[208,256]{1,0:T(8,128)(2,1)S(1)}, u32[]{:S(2)}, u32[]{:S(2)}) collective-permute-start(bf16[208,256]{1,0:T(8,128)(2,1)S(1)} %fusion.2), channel_id=1, source_target_pairs={{0,4},{1,5},{2,6},{3,7},{4,0},{5,1},{6,2},{7,3},{8,12},{9,13},{10,... | collective-permute-start | bytes 319496 | tf_op jit(solution)/shard_map/ppermute | solution.py:261
  10.9 3.6 %collective-permute-done.1 = bf16[208,256]{1,0:T(8,128)(2,1)S(1)} collective-permute-done((bf16[208,256]{1,0:T(8,128)(2,1)S(1)}, bf16[208,256]{1,0:T(8,128)(2,1)S(1)}, u32[]{:S(2)}, u32[]{:S(2)}) %collective-permute-start.1) | collective-permute-done | bytes 106528 | tf_op jit(solution)/shard_map/ppermute | solution.py:261
  14.5 2.8 %collective-permute-start.2 = (bf16[208,256]{1,0:T(8,128)(2,1)S(1)}, bf16[208,256]{1,0:T(8,128)(2,1)S(1)}, u32[]{:S(2)}, u32[]{:S(2)}) collective-permute-start(bf16[208,256]{1,0:T(8,128)(2,1)S(1)} %fusion.3), channel_id=1, source_target_pairs={{0,8},{1,9},{2,10},{3,11},{4,12},{5,13},{6,14},{7,15},{8,0},{9,1},... | collective-permute-start | bytes 319496 | tf_op jit(solution)/shard_map/ppermute | solution.py:261
  17.4 5.2 %collective-permute-done.2 = bf16[208,256]{1,0:T(8,128)(2,1)S(1)} collective-permute-done((bf16[208,256]{1,0:T(8,128)(2,1)S(1)}, bf16[208,256]{1,0:T(8,128)(2,1)S(1)}, u32[]{:S(2)}, u32[]{:S(2)}) %collective-permute-start.2) | collective-permute-done | bytes 106528 | tf_op jit(solution)/shard_map/ppermute | solution.py:261
  22.6 1.5 %collective-permute-start.3 = (bf16[208,256]{1,0:T(8,128)(2,1)S(1)}, bf16[208,256]{1,0:T(8,128)(2,1)S(1)}, u32[]{:S(2)}, u32[]{:S(2)}) collective-permute-start(bf16[208,256]{1,0:T(8,128)(2,1)S(1)} %fusion.1), channel_id=1, source_target_pairs={{0,2},{1,3},{2,0},{3,1},{4,6},{5,7},{6,4},{7,5},{8,10},{9,11},{10,... | collective-permute-start | bytes 319496 | tf_op jit(solution)/shard_map/ppermute | solution.py:261
  24.1 1.3 %collective-permute-start.6 = (bf16[256,768]{1,0:T(8,128)(2,1)S(1)}, bf16[256,768]{1,0:T(8,128)(2,1)S(1)}, u32[]{:S(2)}, u32[]{:S(2)}) collective-permute-start(bf16[256,768]{1,0:T(8,128)(2,1)S(1)} %get-tuple-element.17.refs_2_), channel_id=1, source_target_pairs={{0,1},{1,2},{2,3},{3,4},{4,5},{5,6},{6,7},{7,8},{8,9},{9,10},{10,1... | collective-permute-start | bytes 1179656 | tf_op jit(solution)/shard_map/ppermute | solution.py:332
  25.4 1.3 %collective-permute-start.7 = (bf16[256,768]{1,0:T(8,128)(2,1)S(1)}, bf16[256,768]{1,0:T(8,128)(2,1)S(1)}, u32[]{:S(2)}, u32[]{:S(2)}) collective-permute-start(bf16[256,768]{1,0:T(8,128)(2,1)S(1)} %get-tuple-element.18.refs_1_), channel_id=1, source_target_pairs={{1,0},{2,1},{3,2},{4,3},{5,4},{6,5},{7,6},{8,7},{9,8},{10,9},{11,1... | collective-permute-start | bytes 1179656 | tf_op jit(solution)/shard_map/ppermute | solution.py:333
  26.7 0.7 %collective-permute-done.3 = bf16[208,256]{1,0:T(8,128)(2,1)S(1)} collective-permute-done((bf16[208,256]{1,0:T(8,128)(2,1)S(1)}, bf16[208,256]{1,0:T(8,128)(2,1)S(1)}, u32[]{:S(2)}, u32[]{:S(2)}) %collective-permute-start.3) | collective-permute-done | bytes 106528 | tf_op jit(solution)/shard_map/ppermute | solution.py:261
  27.4 0.1 add_convert_fusion
  27.4 3.9 %collective-permute-start.4 = (bf16[208,256]{1,0:T(8,128)(2,1)S(1)}, bf16[208,256]{1,0:T(8,128)(2,1)S(1)}, u32[]{:S(2)}, u32[]{:S(2)}) collective-permute-start(bf16[208,256]{1,0:T(8,128)(2,1)S(1)} %add_convert_fusion), channel_id=1, source_target_pairs={{0,4},{1,5},{2,6},{3,7},{4,0},{5,1},{6,2},{7,3},{8,12},{9,13},{10,... | collective-permute-start | bytes 319496 | tf_op jit(solution)/shard_map/ppermute | solution.py:261
  31.3 6.7 %collective-permute-done.4 = bf16[208,256]{1,0:T(8,128)(2,1)S(1)} collective-permute-done((bf16[208,256]{1,0:T(8,128)(2,1)S(1)}, bf16[208,256]{1,0:T(8,128)(2,1)S(1)}, u32[]{:S(2)}, u32[]{:S(2)}) %collective-permute-start.4) | collective-permute-done | bytes 106528 | tf_op jit(solution)/shard_map/ppermute | solution.py:261
  38.1 0.1 collective-permute-start.5
  38.2 0.0 copy-done.5
  38.2 0.0 copy-done.1
  38.2 0.0 copy-done.4
  38.2 0.0 copy-start.3
  38.2 3.7 %shard_map.84 = (bf16[512,1536]{1,0:T(8,128)(2,1)S(1)}, bf16[512,1536]{1,0:T(8,128)(2,1)S(1)}) custom-call(s32[2]{0:T(128)S(1)} %pad_add_fusion.place_ref, bf16[512,768]{1,0:T(8,128)(2,1)S(1)} %bitcast.21, bf16[768,768]{1,0:T(8,128)(2,1)S(1)} %copy-done.4, bf16[12,64,256]{2,1,0:T(8,128)(2,1)S(1)} %copy-done.2), custom_call_target="tpu_custom_call" | custom-call | flops 805306368 | tf_op jit(solution)/shard_map/pallas_call | solution.py:334
  41.9 0.0 collective-permute-done.6.refs_0_
  41.9 0.0 collective-permute-done.7.refs_3_
  41.9 0.0 copy-done.3
  41.9 1.2 %shard_map.86 = f32[2,256,768]{2,1,0:T(8,128)S(1)} custom-call(bf16[256,768]{1,0:T(8,128)(2,1)S(1)} %collective-permute-done.6.refs_0_, bf16[256,768]{1,0:T(8,128)(2,1)S(1)} %get-tuple-element.18.refs_1_, bf16[256,768]{1,0:T(8,128)(2,1)S(1)} %get-tuple-element.17.refs_2_, bf16[256,768]{1,0:T(8,128)(2,1)S(1)} %collective-permute-done.7.refs_3_, ...), custom_call_target="tpu_custom_call" | custom-call | flops 603979776 | tf_op jit(solution)/shard_map/pallas_call | solution.py:341
  43.1 0.0 copy-start
  43.1 1.2 %shard_map.85.own_ref = f32[512,384]{1,0:T(8,128)S(1)} custom-call(s32[2]{0:T(128)S(1)} %pad_add_fusion.place_ref, bf16[2,208,256]{2,1,0:T(8,128)(2,1)S(1)} %pad_maximum_fusion.state_ref, bf16[512,1536]{1,0:T(8,128)(2,1)S(1)} %get-tuple-element.16.feat_ref), custom_call_target="tpu_custom_call" | custom-call | flops 201326592 | tf_op jit(solution)/shard_map/pallas_call | solution.py:346
  44.3 0.0 collective-permute-done.5.state_ref
  44.3 0.1 copy-done
  44.4 3.5 %shard_map.87 = bf16[512,768]{1,0:T(8,128)(2,1)} custom-call(s32[2]{0:T(128)S(1)} %pad_add_fusion.place_ref, bf16[2,208,256]{2,1,0:T(8,128)(2,1)S(1)} %collective-permute-done.5.state_ref, bf16[512,1536]{1,0:T(8,128)(2,1)S(1)} %get-tuple-element.15.feat_ref, f32[512,384]{1,0:T(8,128)S(1)} %shard_map.85.own_ref, f32[512,768]{1,0:T(8,128)S(1)} %bitcast.19, ...), custom_call_target="tpu_custom_call" | custom-call | flops 805306368 | tf_op jit(solution)/shard_map/pallas_call | solution.py:349
  (6 shorter events, 0.1 us)
Async XLA Ops:
  0.1 6.1 %copy-start.2 = (bf16[12,64,256]{2,1,0:T(8,128)(2,1)S(1)}, bf16[12,64,256]{2,1,0:T(8,128)(2,1)}, u32[]{:S(2)}) copy-start(bf16[12,64,256]{2,1,0:T(8,128)(2,1)} %omega_ref.3) | copy-start | bytes 1179652
  5.6 2.5 %collective-permute-start = (bf16[2,208,256]{2,1,0:T(8,128)(2,1)S(1)}, bf16[2,208,256]{2,1,0:T(8,128)(2,1)S(1)}, u32[]{:S(2)}, u32[]{:S(2)}) collective-permute-start(bf16[2,208,256]{2,1,0:T(8,128)(2,1)S(1)} %get-tuple-element.14), channel_id=1, source_target_pairs={{0,1},{1,0},{2,3},{3,2},{4,5},{5,4},{6,7},{7,6},{8,9},{9,8},{10,11... | collective-permute-start | bytes 638984 | tf_op jit(solution)/shard_map/ppermute | solution.py:261
  8.2 30.0 %copy-start.5 = (f32[768]{0:T(1024)S(1)}, f32[768]{0:T(1024)}, u32[]{:S(2)}) copy-start(f32[768]{0:T(1024)} %param.15) | copy-start | bytes 9220
  8.2 30.0 %copy-start.1 = (bf16[2,256,768]{2,1,0:T(8,128)(2,1)S(1)}, bf16[2,256,768]{2,1,0:T(8,128)(2,1)}, u32[]{:S(2)}) copy-start(bf16[2,256,768]{2,1,0:T(8,128)(2,1)} %param.8) | copy-start | bytes 2359300
  8.2 30.0 %copy-start.4 = (bf16[768,768]{1,0:T(8,128)(2,1)S(1)}, bf16[768,768]{1,0:T(8,128)(2,1)}, u32[]{:S(2)}) copy-start(bf16[768,768]{1,0:T(8,128)(2,1)} %wq_ref.1) | copy-start | bytes 3538948
  8.2 6.3 %collective-permute-start.1 = (bf16[208,256]{1,0:T(8,128)(2,1)S(1)}, bf16[208,256]{1,0:T(8,128)(2,1)S(1)}, u32[]{:S(2)}, u32[]{:S(2)}) collective-permute-start(bf16[208,256]{1,0:T(8,128)(2,1)S(1)} %fusion.2), channel_id=1, source_target_pairs={{0,4},{1,5},{2,6},{3,7},{4,0},{5,1},{6,2},{7,3},{8,12},{9,13},{10,... | collective-permute-start | bytes 319496 | tf_op jit(solution)/shard_map/ppermute | solution.py:261
  14.5 8.0 %collective-permute-start.2 = (bf16[208,256]{1,0:T(8,128)(2,1)S(1)}, bf16[208,256]{1,0:T(8,128)(2,1)S(1)}, u32[]{:S(2)}, u32[]{:S(2)}) collective-permute-start(bf16[208,256]{1,0:T(8,128)(2,1)S(1)} %fusion.3), channel_id=1, source_target_pairs={{0,8},{1,9},{2,10},{3,11},{4,12},{5,13},{6,14},{7,15},{8,0},{9,1},... | collective-permute-start | bytes 319496 | tf_op jit(solution)/shard_map/ppermute | solution.py:261
  22.6 4.8 %collective-permute-start.3 = (bf16[208,256]{1,0:T(8,128)(2,1)S(1)}, bf16[208,256]{1,0:T(8,128)(2,1)S(1)}, u32[]{:S(2)}, u32[]{:S(2)}) collective-permute-start(bf16[208,256]{1,0:T(8,128)(2,1)S(1)} %fusion.1), channel_id=1, source_target_pairs={{0,2},{1,3},{2,0},{3,1},{4,6},{5,7},{6,4},{7,5},{8,10},{9,11},{10,... | collective-permute-start | bytes 319496 | tf_op jit(solution)/shard_map/ppermute | solution.py:261
  24.1 17.8 %collective-permute-start.6 = (bf16[256,768]{1,0:T(8,128)(2,1)S(1)}, bf16[256,768]{1,0:T(8,128)(2,1)S(1)}, u32[]{:S(2)}, u32[]{:S(2)}) collective-permute-start(bf16[256,768]{1,0:T(8,128)(2,1)S(1)} %get-tuple-element.17.refs_2_), channel_id=1, source_target_pairs={{0,1},{1,2},{2,3},{3,4},{4,5},{5,6},{6,7},{7,8},{8,9},{9,10},{10,1... | collective-permute-start | bytes 1179656 | tf_op jit(solution)/shard_map/ppermute | solution.py:332
  25.4 16.5 %collective-permute-start.7 = (bf16[256,768]{1,0:T(8,128)(2,1)S(1)}, bf16[256,768]{1,0:T(8,128)(2,1)S(1)}, u32[]{:S(2)}, u32[]{:S(2)}) collective-permute-start(bf16[256,768]{1,0:T(8,128)(2,1)S(1)} %get-tuple-element.18.refs_1_), channel_id=1, source_target_pairs={{1,0},{2,1},{3,2},{4,3},{5,4},{6,5},{7,6},{8,7},{9,8},{10,9},{11,1... | collective-permute-start | bytes 1179656 | tf_op jit(solution)/shard_map/ppermute | solution.py:333
  27.4 10.6 %collective-permute-start.4 = (bf16[208,256]{1,0:T(8,128)(2,1)S(1)}, bf16[208,256]{1,0:T(8,128)(2,1)S(1)}, u32[]{:S(2)}, u32[]{:S(2)}) collective-permute-start(bf16[208,256]{1,0:T(8,128)(2,1)S(1)} %add_convert_fusion), channel_id=1, source_target_pairs={{0,4},{1,5},{2,6},{3,7},{4,0},{5,1},{6,2},{7,3},{8,12},{9,13},{10,... | collective-permute-start | bytes 319496 | tf_op jit(solution)/shard_map/ppermute | solution.py:261
  38.1 6.2 %collective-permute-start.5 = (bf16[2,208,256]{2,1,0:T(8,128)(2,1)S(1)}, bf16[2,208,256]{2,1,0:T(8,128)(2,1)S(1)}, u32[]{:S(2)}, u32[]{:S(2)}) collective-permute-start(bf16[2,208,256]{2,1,0:T(8,128)(2,1)S(1)} %pad_maximum_fusion.state_ref), channel_id=1, source_target_pairs={{0,1},{1,0},{2,3},{3,2},{4,5},{5,4},{6,7},{7,6},{8,9},{9,8},{10,11... | collective-permute-start | bytes 638984 | tf_op jit(solution)/shard_map/ppermute | solution.py:261
  38.2 3.7 %copy-start.3 = (f32[3,3,768]{2,1,0:T(4,128)S(1)}, f32[3,3,768]{2,1,0:T(4,128)}, u32[]{:S(2)}) copy-start(f32[3,3,768]{2,1,0:T(4,128)} %refs_4_.1) | copy-start | bytes 82948
  43.1 1.3 %copy-start = (bf16[768,768]{1,0:T(8,128)(2,1)S(1)}, bf16[768,768]{1,0:T(8,128)(2,1)}, u32[]{:S(2)}) copy-start(bf16[768,768]{1,0:T(8,128)(2,1)} %wo_ref.1) | copy-start | bytes 3538948

commit v4 on v3

v4 whole, which is shorter than its diff:
```python
import functools
import math

import jax
import jax.numpy as jnp
from jax import lax
from jax.experimental import pallas as pl
from jax.experimental.pallas import tpu as pltpu
from jax.sharding import PartitionSpec as P


BF = jnp.bfloat16
F32 = jnp.float32
LOG2E = 1.4426950408889634
TILE = 256
VMEM_LIMIT = 28 * 1024 * 1024
FIRST_LIMIT = 54900000


def tiles_of(total, wanted):
    return wanted if total % wanted == 0 else total


def feature_tile(proj, omega_pair, dim_head, nfeat):
    lifted = jnp.dot(proj, omega_pair, preferred_element_type=F32)
    values = proj.astype(F32)
    square = values * values * (0.5 * dim_head ** (-0.5) * LOG2E)
    first = lax.broadcasted_iota(jnp.int32, square.shape, 1) < dim_head
    halves = []
    for head, mine in enumerate((jnp.where(first, square, 0.0), jnp.where(first, 0.0, square))):
        drop = jnp.sum(mine, axis=1, keepdims=True) + 0.5 * math.log2(nfeat)
        grown = lifted[:, head * nfeat : (head + 1) * nfeat] * (dim_head ** (-0.25) * LOG2E)
        halves.append(jnp.exp2(grown - drop).astype(BF))
    return jnp.concatenate(halves, axis=1)


def fill_pair(pair_ref, which, omegas):
    dim_head, nfeat = omegas[0].shape
    empty = jnp.zeros((dim_head, nfeat), BF)
    for side in range(2):
        rows = slice(side * dim_head, (side + 1) * dim_head)
        pair_ref[which, rows, side * nfeat : (side + 1) * nfeat] = omegas[side]
        pair_ref[which, rows, (1 - side) * nfeat : (2 - side) * nfeat] = empty


def fill_marks(vt_ref, group):
    heads, rows, tokens = vt_ref.shape
    mark = lax.broadcasted_iota(jnp.int32, (16, tokens), 0)
    for head in range(heads):
        vt_ref[head, rows - 16 :, :] = jnp.where(mark == head % group, 1.0, 0.0).astype(BF)


def half_state(bit, key_ref, offset, pair_ref, vt_ref, feat_ref, state_ref):
    heads, rows, tokens = vt_ref.shape
    dim_head = rows - 16
    wide = 2 * dim_head
    nfeat = feat_ref.shape[1] // 2
    group = heads // 2
    tile = tiles_of(tokens, TILE)
    sums = None
    for head in range(heads):
        pair, side = head // 2, head % 2
        if side == 0:
            lanes = slice(pair * wide, (pair + 1) * wide) if isinstance(offset, int) else pl.ds(pl.multiple_of(offset + pair * wide, wide), wide)
            for start in range(0, tokens, tile):
                feat_ref[start : start + tile, :] = feature_tile(key_ref[start : start + tile, lanes], pair_ref[pair], dim_head, nfeat)
        local = jnp.dot(vt_ref[head], feat_ref[:, side * nfeat : (side + 1) * nfeat], preferred_element_type=F32)
        slot = lax.rem(bit + head // group, 2)
        spot = head % group
        state_ref[slot, spot * dim_head : (spot + 1) * dim_head, :] = local[:dim_head].astype(state_ref.dtype)
        sums = local[dim_head:] if spot == 0 else sums + local[dim_head:]
        if spot == group - 1:
            state_ref[slot, group * dim_head :, :] = sums.astype(state_ref.dtype)


def turn_values(value_refs, offset, span, vt_ref):
    heads, rows, _ = vt_ref.shape
    dim_head = rows - 16
    lanes = pl.ds(pl.multiple_of(offset, span), span)
    turned = jnp.concatenate([ref[:, lanes] for ref in value_refs], axis=0).T
    for head in range(heads):
        vt_ref[head, :dim_head, :] = turned[head * dim_head : (head + 1) * dim_head]


def first_kernel(place_ref, x_hbm, wk_hbm, wv_hbm, omega_hbm, *refs):
    heads, _, _ = omega_hbm.shape
    tokens, width = x_hbm.shape
    here = len(refs) - 11
    send_ref, own_ref = refs[:2]
    value_refs = refs[2 : 2 + here]
    x_ref, wk_ref, wv_ref, omega_ref, key_ref, sems, pair_ref, vt_ref, feat_ref = refs[2 + here :]
    half, span = heads // 2, width // 2
    other = 1 - place_ref[0]
    moves = [(x_hbm, x_ref), (wv_hbm, wv_ref), (omega_hbm.at[pl.ds(other * half, half)], omega_ref), (wk_hbm, wk_ref)]
    copies = [pltpu.make_async_copy(source, target, sems.at[i]) for i, (source, target) in enumerate(moves)]
    for copy in copies:
        copy.start()
    fill_marks(vt_ref, half // 2)
    cols = tokens // here
    blocks = [slice(row * cols, (row + 1) * cols) for row in range(here)]
    copies[0].wait()
    copies[1].wait()
    for block, value_ref in zip(blocks, value_refs):
        value_ref[...] = jnp.dot(x_ref[block, :], wv_ref[...], preferred_element_type=F32).astype(BF)
    copies[2].wait()
    for pair in range(half // 2):
        fill_pair(pair_ref, pair, [omega_ref[2 * pair], omega_ref[2 * pair + 1]])
    copies[3].wait()
    for block in blocks:
        key_ref[block, :] = jnp.dot(x_ref[block, :], wk_ref[...], preferred_element_type=F32).astype(BF)
    own_ref[...] = key_ref[:, pl.ds(pl.multiple_of(place_ref[0] * span, span), span)]
    turn_values(value_refs, other * span, span, vt_ref)
    half_state(place_ref[1], key_ref, other * span, pair_ref, vt_ref, feat_ref, send_ref)


def second_kernel(place_ref, key_ref, omega_ref, *refs):
    heads, _, _ = omega_ref.shape
    value_refs = refs[:-4]
    state_ref, pair_ref, vt_ref, feat_ref = refs[-4:]
    half, span = heads // 2, key_ref.shape[1]
    core = place_ref[0]
    fill_marks(vt_ref, half // 2)
    for pair in range(half // 2):
        fill_pair(pair_ref, pair, [omega_ref[core * half + 2 * pair], omega_ref[core * half + 2 * pair + 1]])
    turn_values(value_refs, core * span, span, vt_ref)
    half_state(place_ref[1], key_ref, 0, pair_ref, vt_ref, feat_ref, state_ref)


def query_kernel(x_ref, wq_ref, omega_ref, feat_ref, pair_ref):
    heads, dim_head, nfeat = omega_ref.shape
    tokens = x_ref.shape[0]
    for pair in range(heads // 2):
        fill_pair(pair_ref, pair, [omega_ref[2 * pair], omega_ref[2 * pair + 1]])
    tile = tiles_of(tokens, TILE)
    for start in range(0, tokens, tile):
        query = jnp.dot(x_ref[start : start + tile, :], wq_ref[...], preferred_element_type=F32).astype(BF)
        for pair in range(heads // 2):
            proj = query[:, pair * 2 * dim_head : (pair + 1) * 2 * dim_head]
            feat_ref[start : start + tile, pair * 2 * nfeat : (pair + 1) * 2 * nfeat] = feature_tile(
                proj, pair_ref[pair], dim_head, nfeat
            )


def conv_kernel_body(*refs):
    taps_ref, out_ref = refs[-2:]
    values = refs[:-2]
    here, cols, width = out_ref.shape
    lanes = 128
    col = lax.broadcasted_iota(jnp.int32, (cols, lanes), 0)
    for start in range(0, width, lanes):
        cut = slice(start, start + lanes)
        wide = [value[:, cut].astype(F32) for value in values]
        for row in range(here):
            sums = []
            for shift in range(3):
                terms = [wide[row + step] * taps_ref[step, shift : shift + 1, cut] for step in range(3)]
                sums.append(terms[0] + terms[1] + terms[2])
            left = jnp.where(col == 0, 0.0, pltpu.roll(sums[0], 1, 0))
            right = jnp.where(col == cols - 1, 0.0, pltpu.roll(sums[2], cols - 1, 0))
            out_ref[row, :, cut] = left + sums[1] + right


def fill_mats(bit, state_ref, mat_ref, dim_head):
    pairs, _, both = mat_ref.shape
    nfeat = both // 2
    group = pairs
    wide = 2 * dim_head
    empty = jnp.zeros((dim_head, nfeat), BF)
    for head in range(2 * pairs):
        pair, side = head // 2, head % 2
        slot = lax.rem(bit + head // group, 2)
        spot = head % group
        mine, other = slice(side * nfeat, (side + 1) * nfeat), slice((1 - side) * nfeat, (2 - side) * nfeat)
        sums = state_ref[slot, group * dim_head :, :][spot : spot + 1]
        for base, block in (
            (0, state_ref[slot, spot * dim_head : (spot + 1) * dim_head, :]),
            (wide, jnp.broadcast_to(sums, (dim_head, nfeat))),
        ):
            rows = slice(base + side * dim_head, base + (side + 1) * dim_head)
            mat_ref[pair, rows, mine] = block
            mat_ref[pair, rows, other] = empty


def attend(feat, mat, wide):
    both = lax.dot_general(feat, mat, (((1,), (1,)), ((), ())), preferred_element_type=F32)
    return both[:, :wide] / both[:, wide:]


def own_kernel(place_ref, state_ref, feat_ref, attn_ref, mat_ref):
    pairs, rows, both = mat_ref.shape
    wide = rows // 2
    tokens = attn_ref.shape[0]
    fill_mats(place_ref[1], state_ref, mat_ref, wide // 2)
    tile = tiles_of(tokens, 256)
    for start in range(0, tokens, tile):
        for pair in range(pairs):
            attn_ref[start : start + tile, pair * wide : (pair + 1) * wide] = attend(
                feat_ref[start : start + tile, pl.ds(pl.multiple_of((place_ref[0] * pairs + pair) * both, both), both)], mat_ref[pair], wide
            )


def out_kernel(place_ref, state_ref, feat_ref, own_ref, pos_ref, x_ref, gain_ref, wo_ref, out_ref, mat_ref, attn_ref):
    pairs, rows, both = mat_ref.shape
    wide = rows // 2
    tokens, width = x_ref.shape
    span = width // 2
    core = place_ref[0]
    fill_mats(place_ref[1], state_ref, mat_ref, wide // 2)
    mine = pl.ds(pl.multiple_of(core * span, span), span)
    other = pl.ds(pl.multiple_of((1 - core) * span, span), span)
    tile = tiles_of(tokens, 256)
    for start in range(0, tokens, tile):
        cut = slice(start, start + tile)
        total = None
        for pair in range(pairs):
            lanes = slice(pair * wide, (pair + 1) * wide)
            attn = attend(feat_ref[cut, pl.ds(pl.multiple_of(((1 - core) * pairs + pair) * both, both), both)], mat_ref[pair], wide)
            attn_ref[:, lanes] = attn
            kept = own_ref[cut, lanes]
            square = attn * attn + kept * kept
            total = square if total is None else total + square
        scale = lax.rsqrt(jnp.sum(total, axis=1, keepdims=True) * (1.0 / width) + 1e-06)
        out = x_ref[cut, :].astype(F32)
        for part, attn in ((mine, own_ref[cut, :]), (other, attn_ref[...])):
            mixed = (attn * scale * gain_ref[:, part] + pos_ref[cut, part]).astype(BF)
            out = out + jnp.dot(mixed, wo_ref[part, :], preferred_element_type=F32)
        out_ref[cut, :] = out.astype(BF)


def call(kernel, out_shape, in_specs, scratch, flops, limit=VMEM_LIMIT):
    return pl.pallas_call(
        kernel,
        out_shape=out_shape,
        in_specs=in_specs,
        out_specs=[pl.BlockSpec(memory_space=pltpu.VMEM)] * len(out_shape),
        scratch_shapes=scratch,
        compiler_params=pltpu.CompilerParams(vmem_limit_bytes=limit),
        cost_estimate=pl.CostEstimate(flops=flops, bytes_accessed=0, transcendentals=0),
    )


def swap(block, bit, count):
    return lax.ppermute(block, "row", [(i, i ^ bit ^ (bit > 1)) for i in range(count)])


def reduce_half(send, keep, count, split):
    other = swap(send, 1, count)
    chip = keep + other.astype(F32)
    other = swap(chip[1].astype(BF), split, count)
    part = chip[0] + other.astype(F32)
    bit = count // 2
    while bit > 1:
        if bit != split:
            other = swap(part.astype(BF), bit, count)
            part = part + other.astype(F32)
        bit //= 2
    done = part.astype(BF)
    other = swap(done, split, count)
    return jnp.stack([done, other])


def layer(tokens, w_query, w_key, w_value, w_out, omega, conv_kernel, norm_gain):
    here, cols, width = tokens.shape
    heads, dim_head, nfeat = omega.shape
    count = lax.axis_size("row")
    split = min(4, count // 2)
    flat = tokens.reshape(here * cols, width)
    amount = here * cols
    half, span = heads // 2, width // 2
    rows = half // 2 * dim_head + 16
    spot = lax.axis_index("row").astype(jnp.int32)
    bits = [lax.bitwise_and(lax.shift_right_logical(spot, i), 1) for i in range(count.bit_length() - 1)]
    place = jnp.stack([functools.reduce(lax.bitwise_xor, bits), bits[split.bit_length() - 1]])
    proj = 2 * amount * width * width
    feats = 2 * amount * width * nfeat
    vmem = pl.BlockSpec(memory_space=pltpu.VMEM)
    smem = pl.BlockSpec(memory_space=pltpu.SMEM)
    hbm = pl.BlockSpec(memory_space=pltpu.HBM)
    pairs = pltpu.VMEM((half // 2, 2 * dim_head, 2 * nfeat), BF)
    turned = pltpu.VMEM((half, dim_head + 16, amount), BF)
    feat = pltpu.VMEM((amount, 2 * nfeat), BF)
    mats = pltpu.VMEM((half // 2, 4 * dim_head, 2 * nfeat), BF)

    send, key, *values = call(
        first_kernel,
        [jax.ShapeDtypeStruct((2, rows, nfeat), BF), jax.ShapeDtypeStruct((amount, span), BF)]
        + [jax.ShapeDtypeStruct((cols, width), BF)] * here,
        [smem] + [hbm] * 4,
        [
            pltpu.VMEM((amount, width), BF),
            pltpu.VMEM((width, width), BF),
            pltpu.VMEM((width, width), BF),
            pltpu.VMEM((half, dim_head, nfeat), BF),
            pltpu.VMEM((amount, width), BF),
            pltpu.SemaphoreType.DMA((4,)),
            pairs,
            turned,
            feat,
        ],
        2 * proj + feats,
        FIRST_LIMIT,
    )(place, flat, w_key, w_value, omega)
    (keep,) = call(
        second_kernel,
        [jax.ShapeDtypeStruct((2, rows, nfeat), F32)],
        [smem] + [vmem] * (2 + here),
        [pairs, turned, feat],
        feats,
    )(place, key, omega, *values)
    top = lax.ppermute(values[-1], "row", [(i, i + 1) for i in range(count - 1)])
    low = lax.ppermute(values[0], "row", [(i + 1, i) for i in range(count - 1)])
    (feat_query,) = call(
        query_kernel,
        [jax.ShapeDtypeStruct((amount, heads * nfeat), BF)],
        [vmem] * 3,
        [pltpu.VMEM((half, 2 * dim_head, 2 * nfeat), BF)],
        proj + feats,
    )(flat, w_query, omega)
    (position,) = call(
        conv_kernel_body, [jax.ShapeDtypeStruct((here, cols, width), F32)], [vmem] * (here + 3), [], proj
    )(top, *values, low, conv_kernel)
    mine = reduce_half(send, keep, count, split)
    theirs = swap(mine, 1, count)
    (attn,) = call(
        own_kernel, [jax.ShapeDtypeStruct((amount, span), F32)], [smem] + [vmem] * 2, [mats], feats
    )(place, mine, feat_query)
    (out,) = call(
        out_kernel,
        [jax.ShapeDtypeStruct((amount, width), BF)],
        [smem] + [vmem] * 7,
        [mats, pltpu.VMEM((tiles_of(amount, 256), span), F32)],
        proj + feats,
    )(place, theirs, feat_query, attn, position.reshape(amount, width), flat, norm_gain.reshape(1, width), w_out)
    return out.reshape(here, cols, width)


def solution(mesh):
    return jax.shard_map(
        layer,
        mesh=mesh,
        in_specs=(P(("parts", "row"), None, None), P(), P(), P(), P(), P(), P(), P()),
        out_specs=P(("parts", "row"), None, None),
        check_vma=False,
    )
```

time: 48.1 us -> 44.3 us (0.921)
  the two profiles are of different devices: /device:TPU:0 before, /device:TPU:11 now
where the time goes in v4:
time: 44.3 us; the launch traced here: 44.1 us
  waiting for transfers between devices  15 us (34%)
  Pallas kernels  14.5 us (33%)
  starting transfers between devices  14 us (32%)
    ppermute x6, waiting for transfers between devices, swap(): lax.ppermute(block, 'row', [(i, i ^ bit ^ (bit > 1)) for i in range(count)])  15 us
    ppermute x6, starting transfers between devices, swap(): lax.ppermute(block, 'row', [(i, i ^ bit ^ (bit > 1)) for i in range(count)])  7.59 us
    pallas_call x1, Pallas kernels, layer(): call(first_kernel, [jax.ShapeDtypeStruct((2, rows, nfeat), BF), jax.Shape...  4.94 us
    ppermute x1, starting transfers between devices, layer(): lax.ppermute(values[-1], 'row', [(i, i + 1) for i in range(count - 1)])  4.51 us
    pallas_call x1, Pallas kernels, layer(): call(out_kernel, [jax.ShapeDtypeStruct((amount, width), BF)], [smem] + [v...  3.54 us
    ppermute x1, starting transfers between devices, layer(): low = lax.ppermute(values[0], 'row', [(i + 1, i) for i in range(count - 1)])  1.94 us
    pallas_call x1, Pallas kernels, layer(): call(query_kernel, [jax.ShapeDtypeStruct((amount, heads * nfeat), BF)], [...  1.89 us
    pallas_call x1, Pallas kernels, layer(): call(second_kernel, [jax.ShapeDtypeStruct((2, rows, nfeat), F32)], [smem]...  1.76 us
  transfers between devices with their start and end apart: 8, of which 3 were waited for; matrix products, arithmetic and copies ran while one was open for 0% of the time, Pallas kernels for 14%

profile of v4, /device:TPU:11, one launch (start us, length us, event | category | flops | bytes accessed | tf_op | source)
XLA Modules:
  0.0 44.1 jit_solution(1798529904729013393)
XLA Ops:
  0.0 0.1 pad_add_fusion.place_ref
  0.1 0.0 copy-start.1
  0.1 4.9 %shard_map.82 = (bf16[2,208,256]{2,1,0:T(8,128)(2,1)S(1)}, bf16[512,384]{1,0:T(8,128)(2,1)S(1)}, bf16[256,768]{1,0:T(8,128)(2,1)S(1)}, bf16[256,768]{1,0:T(8,128)(2,1)S(1)}) custom-call(s32[2]{0:T(128)S(1)} %pad_add_fusion.place_ref, bf16[512,768]{1,0:T(8,128)(2,1)} %bitcast.20, bf16[768,768]{1,0:T(8,128)(2,1)} %wk_hbm.1, bf16[768,768]{1,0:T(8,128)(2,1)} %wv_hbm.1, ...), custom_call_target="tpu_custom_call" | custom-call | flops 1409286144 | tf_op jit(solution)/shard_map/pallas_call | solution.py:284
  5.0 0.7 %collective-permute-start = (bf16[2,208,256]{2,1,0:T(8,128)(2,1)S(1)}, bf16[2,208,256]{2,1,0:T(8,128)(2,1)S(1)}, u32[]{:S(2)}, u32[]{:S(2)}) collective-permute-start(bf16[2,208,256]{2,1,0:T(8,128)(2,1)S(1)} %get-tuple-element.12), channel_id=1, source_target_pairs={{0,1},{1,0},{2,3},{3,2},{4,5},{5,4},{6,7},{7,6},{8,9},{9,8},{10,11... | collective-permute-start | bytes 638984 | tf_op jit(solution)/shard_map/ppermute | solution.py:243
  5.8 0.0 copy-done.1
  5.8 1.8 %shard_map.83 = f32[2,208,256]{2,1,0:T(8,128)S(1)} custom-call(s32[2]{0:T(128)S(1)} %pad_add_fusion.place_ref, bf16[512,384]{1,0:T(8,128)(2,1)S(1)} %get-tuple-element.9.key_ref, bf16[12,64,256]{2,1,0:T(8,128)(2,1)S(1)} %copy-done.1, bf16[256,768]{1,0:T(8,128)(2,1)S(1)} %get-tuple-element.10.refs_0_.refs_1_, ...), custom_call_target="tpu_custom_call" | custom-call | flops 201326592 | tf_op jit(solution)/shard_map/pallas_call | solution.py:303
  7.5 0.0 collective-permute-done
  7.6 0.0 copy-start.5
  7.6 0.0 copy-start
  7.6 0.0 copy-start.3
  7.7 0.1 collective-permute-start.1
  7.8 4.5 %collective-permute-done.1 = bf16[208,256]{1,0:T(8,128)(2,1)S(1)} collective-permute-done((bf16[208,256]{1,0:T(8,128)(2,1)S(1)}, bf16[208,256]{1,0:T(8,128)(2,1)S(1)}, u32[]{:S(2)}, u32[]{:S(2)}) %collective-permute-start.1) | collective-permute-done | bytes 106528 | tf_op jit(solution)/shard_map/ppermute | solution.py:243
  12.4 2.3 %collective-permute-start.2 = (bf16[208,256]{1,0:T(8,128)(2,1)S(1)}, bf16[208,256]{1,0:T(8,128)(2,1)S(1)}, u32[]{:S(2)}, u32[]{:S(2)}) collective-permute-start(bf16[208,256]{1,0:T(8,128)(2,1)S(1)} %fusion.3), channel_id=1, source_target_pairs={{0,9},{1,8},{2,11},{3,10},{4,13},{5,12},{6,15},{7,14},{8,1},{9,0},... | collective-permute-start | bytes 319496 | tf_op jit(solution)/shard_map/ppermute | solution.py:243
  14.6 4.9 %collective-permute-done.2 = bf16[208,256]{1,0:T(8,128)(2,1)S(1)} collective-permute-done((bf16[208,256]{1,0:T(8,128)(2,1)S(1)}, bf16[208,256]{1,0:T(8,128)(2,1)S(1)}, u32[]{:S(2)}, u32[]{:S(2)}) %collective-permute-start.2) | collective-permute-done | bytes 106528 | tf_op jit(solution)/shard_map/ppermute | solution.py:243
  19.6 0.7 %collective-permute-start.3 = (bf16[208,256]{1,0:T(8,128)(2,1)S(1)}, bf16[208,256]{1,0:T(8,128)(2,1)S(1)}, u32[]{:S(2)}, u32[]{:S(2)}) collective-permute-start(bf16[208,256]{1,0:T(8,128)(2,1)S(1)} %fusion.1), channel_id=1, source_target_pairs={{0,3},{1,2},{2,1},{3,0},{4,7},{5,6},{6,5},{7,4},{8,11},{9,10},{10,... | collective-permute-start | bytes 319496 | tf_op jit(solution)/shard_map/ppermute | solution.py:243
  20.2 1.9 %collective-permute-start.7 = (bf16[256,768]{1,0:T(8,128)(2,1)S(1)}, bf16[256,768]{1,0:T(8,128)(2,1)S(1)}, u32[]{:S(2)}, u32[]{:S(2)}) collective-permute-start(bf16[256,768]{1,0:T(8,128)(2,1)S(1)} %get-tuple-element.10.refs_0_.refs_1_), channel_id=1, source_target_pairs={{1,0},{2,1},{3,2},{4,3},{5,4},{6,5},{7,6},{8,7},{9,8},{10,9},{11,1... | collective-permute-start | bytes 1179656 | tf_op jit(solution)/shard_map/ppermute | solution.py:311
  22.2 4.5 %collective-permute-start.6 = (bf16[256,768]{1,0:T(8,128)(2,1)S(1)}, bf16[256,768]{1,0:T(8,128)(2,1)S(1)}, u32[]{:S(2)}, u32[]{:S(2)}) collective-permute-start(bf16[256,768]{1,0:T(8,128)(2,1)S(1)} %get-tuple-element.11.refs_1_.refs_2_), channel_id=1, source_target_pairs={{0,1},{1,2},{2,3},{3,4},{4,5},{5,6},{6,7},{7,8},{8,9},{9,10},{10,1... | collective-permute-start | bytes 1179656 | tf_op jit(solution)/shard_map/ppermute | solution.py:310
  26.7 0.0 collective-permute-done.3
  26.7 0.1 add_convert_fusion
  26.8 0.1 collective-permute-start.4
  26.9 5.6 %collective-permute-done.4 = bf16[208,256]{1,0:T(8,128)(2,1)S(1)} collective-permute-done((bf16[208,256]{1,0:T(8,128)(2,1)S(1)}, bf16[208,256]{1,0:T(8,128)(2,1)S(1)}, u32[]{:S(2)}, u32[]{:S(2)}) %collective-permute-start.4) | collective-permute-done | bytes 106528 | tf_op jit(solution)/shard_map/ppermute | solution.py:243
  32.4 3.7 %collective-permute-start.5 = (bf16[2,208,256]{2,1,0:T(8,128)(2,1)S(1)}, bf16[2,208,256]{2,1,0:T(8,128)(2,1)S(1)}, u32[]{:S(2)}, u32[]{:S(2)}) collective-permute-start(bf16[2,208,256]{2,1,0:T(8,128)(2,1)S(1)} %pad_maximum_fusion.state_ref), channel_id=1, source_target_pairs={{0,1},{1,0},{2,3},{3,2},{4,5},{5,4},{6,7},{7,6},{8,9},{9,8},{10,11... | collective-permute-start | bytes 638984 | tf_op jit(solution)/shard_map/ppermute | solution.py:243
  36.1 0.0 copy-done.5
  36.1 0.0 copy-done
  36.1 0.0 copy-done.3
  36.1 0.0 copy-start.4
  36.1 1.9 %shard_map.84.feat_ref = bf16[512,3072]{1,0:T(8,128)(2,1)S(1)} custom-call(bf16[512,768]{1,0:T(8,128)(2,1)S(1)} %bitcast.21, bf16[768,768]{1,0:T(8,128)(2,1)S(1)} %copy-done.3, bf16[12,64,256]{2,1,0:T(8,128)(2,1)S(1)} %copy-done.1), custom_call_target="tpu_custom_call" | custom-call | flops 805306368 | tf_op jit(solution)/shard_map/pallas_call | solution.py:312
  38.0 0.0 collective-permute-done.7.refs_3_
  38.0 0.0 collective-permute-done.6.refs_0_
  38.1 0.0 copy-done.4
  38.1 1.2 %shard_map.86 = f32[2,256,768]{2,1,0:T(8,128)S(1)} custom-call(bf16[256,768]{1,0:T(8,128)(2,1)S(1)} %collective-permute-done.6.refs_0_, bf16[256,768]{1,0:T(8,128)(2,1)S(1)} %get-tuple-element.10.refs_0_.refs_1_, bf16[256,768]{1,0:T(8,128)(2,1)S(1)} %get-tuple-element.11.refs_1_.refs_2_, bf16[256,768]{1,0:T(8,128)(2,1)S(1)} %collective-permute-done.7.refs_3_, ...), custom_call_target="tpu_custom_call" | custom-call | flops 603979776 | tf_op jit(solution)/shard_map/pallas_call | solution.py:319
  39.2 0.0 copy-start.2
  39.3 1.2 %shard_map.85.own_ref = f32[512,384]{1,0:T(8,128)S(1)} custom-call(s32[2]{0:T(128)S(1)} %pad_add_fusion.place_ref, bf16[2,208,256]{2,1,0:T(8,128)(2,1)S(1)} %pad_maximum_fusion.state_ref, bf16[512,3072]{1,0:T(8,128)(2,1)S(1)} %shard_map.84.feat_ref), custom_call_target="tpu_custom_call" | custom-call | flops 201326592 | tf_op jit(solution)/shard_map/pallas_call | solution.py:324
  40.4 0.0 collective-permute-done.5.state_ref
  40.4 0.1 copy-done.2
  40.5 3.5 %shard_map.87 = bf16[512,768]{1,0:T(8,128)(2,1)} custom-call(s32[2]{0:T(128)S(1)} %pad_add_fusion.place_ref, bf16[2,208,256]{2,1,0:T(8,128)(2,1)S(1)} %collective-permute-done.5.state_ref, bf16[512,3072]{1,0:T(8,128)(2,1)S(1)} %shard_map.84.feat_ref, f32[512,384]{1,0:T(8,128)S(1)} %shard_map.85.own_ref, f32[512,768]{1,0:T(8,128)S(1)} %bitcast.19, ...), custom_call_target="tpu_custom_call" | custom-call | flops 805306368 | tf_op jit(solution)/shard_map/pallas_call | solution.py:327
  (6 shorter events, 0.1 us)
Async XLA Ops:
  0.1 5.7 %copy-start.1 = (bf16[12,64,256]{2,1,0:T(8,128)(2,1)S(1)}, bf16[12,64,256]{2,1,0:T(8,128)(2,1)}, u32[]{:S(2)}) copy-start(bf16[12,64,256]{2,1,0:T(8,128)(2,1)} %omega_ref.3) | copy-start | bytes 1179652
  5.0 2.5 %collective-permute-start = (bf16[2,208,256]{2,1,0:T(8,128)(2,1)S(1)}, bf16[2,208,256]{2,1,0:T(8,128)(2,1)S(1)}, u32[]{:S(2)}, u32[]{:S(2)}) collective-permute-start(bf16[2,208,256]{2,1,0:T(8,128)(2,1)S(1)} %get-tuple-element.12), channel_id=1, source_target_pairs={{0,1},{1,0},{2,3},{3,2},{4,5},{5,4},{6,7},{7,6},{8,9},{9,8},{10,11... | collective-permute-start | bytes 638984 | tf_op jit(solution)/shard_map/ppermute | solution.py:243
  7.6 28.5 %copy-start.5 = (f32[768]{0:T(1024)S(1)}, f32[768]{0:T(1024)}, u32[]{:S(2)}) copy-start(f32[768]{0:T(1024)} %param.15) | copy-start | bytes 9220
  7.6 28.5 %copy-start = (bf16[2,256,768]{2,1,0:T(8,128)(2,1)S(1)}, bf16[2,256,768]{2,1,0:T(8,128)(2,1)}, u32[]{:S(2)}) copy-start(bf16[2,256,768]{2,1,0:T(8,128)(2,1)} %param.8) | copy-start | bytes 2359300
  7.6 28.5 %copy-start.3 = (bf16[768,768]{1,0:T(8,128)(2,1)S(1)}, bf16[768,768]{1,0:T(8,128)(2,1)}, u32[]{:S(2)}) copy-start(bf16[768,768]{1,0:T(8,128)(2,1)} %wq_ref.1) | copy-start | bytes 3538948
  7.7 4.7 %collective-permute-start.1 = (bf16[208,256]{1,0:T(8,128)(2,1)S(1)}, bf16[208,256]{1,0:T(8,128)(2,1)S(1)}, u32[]{:S(2)}, u32[]{:S(2)}) collective-permute-start(bf16[208,256]{1,0:T(8,128)(2,1)S(1)} %fusion.2), channel_id=1, source_target_pairs={{0,5},{1,4},{2,7},{3,6},{4,1},{5,0},{6,3},{7,2},{8,13},{9,12},{10,... | collective-permute-start | bytes 319496 | tf_op jit(solution)/shard_map/ppermute | solution.py:243
  12.4 7.2 %collective-permute-start.2 = (bf16[208,256]{1,0:T(8,128)(2,1)S(1)}, bf16[208,256]{1,0:T(8,128)(2,1)S(1)}, u32[]{:S(2)}, u32[]{:S(2)}) collective-permute-start(bf16[208,256]{1,0:T(8,128)(2,1)S(1)} %fusion.3), channel_id=1, source_target_pairs={{0,9},{1,8},{2,11},{3,10},{4,13},{5,12},{6,15},{7,14},{8,1},{9,0},... | collective-permute-start | bytes 319496 | tf_op jit(solution)/shard_map/ppermute | solution.py:243
  19.6 7.2 %collective-permute-start.3 = (bf16[208,256]{1,0:T(8,128)(2,1)S(1)}, bf16[208,256]{1,0:T(8,128)(2,1)S(1)}, u32[]{:S(2)}, u32[]{:S(2)}) collective-permute-start(bf16[208,256]{1,0:T(8,128)(2,1)S(1)} %fusion.1), channel_id=1, source_target_pairs={{0,3},{1,2},{2,1},{3,0},{4,7},{5,6},{6,5},{7,4},{8,11},{9,10},{10,... | collective-permute-start | bytes 319496 | tf_op jit(solution)/shard_map/ppermute | solution.py:243
  20.2 17.8 %collective-permute-start.7 = (bf16[256,768]{1,0:T(8,128)(2,1)S(1)}, bf16[256,768]{1,0:T(8,128)(2,1)S(1)}, u32[]{:S(2)}, u32[]{:S(2)}) collective-permute-start(bf16[256,768]{1,0:T(8,128)(2,1)S(1)} %get-tuple-element.10.refs_0_.refs_1_), channel_id=1, source_target_pairs={{1,0},{2,1},{3,2},{4,3},{5,4},{6,5},{7,6},{8,7},{9,8},{10,9},{11,1... | collective-permute-start | bytes 1179656 | tf_op jit(solution)/shard_map/ppermute | solution.py:311
  22.2 15.9 %collective-permute-start.6 = (bf16[256,768]{1,0:T(8,128)(2,1)S(1)}, bf16[256,768]{1,0:T(8,128)(2,1)S(1)}, u32[]{:S(2)}, u32[]{:S(2)}) collective-permute-start(bf16[256,768]{1,0:T(8,128)(2,1)S(1)} %get-tuple-element.11.refs_1_.refs_2_), channel_id=1, source_target_pairs={{0,1},{1,2},{2,3},{3,4},{4,5},{5,6},{6,7},{7,8},{8,9},{9,10},{10,1... | collective-permute-start | bytes 1179656 | tf_op jit(solution)/shard_map/ppermute | solution.py:310
  26.8 5.6 %collective-permute-start.4 = (bf16[208,256]{1,0:T(8,128)(2,1)S(1)}, bf16[208,256]{1,0:T(8,128)(2,1)S(1)}, u32[]{:S(2)}, u32[]{:S(2)}) collective-permute-start(bf16[208,256]{1,0:T(8,128)(2,1)S(1)} %add_convert_fusion), channel_id=1, source_target_pairs={{0,5},{1,4},{2,7},{3,6},{4,1},{5,0},{6,3},{7,2},{8,13},{9,12},{10,... | collective-permute-start | bytes 319496 | tf_op jit(solution)/shard_map/ppermute | solution.py:243
  32.4 8.0 %collective-permute-start.5 = (bf16[2,208,256]{2,1,0:T(8,128)(2,1)S(1)}, bf16[2,208,256]{2,1,0:T(8,128)(2,1)S(1)}, u32[]{:S(2)}, u32[]{:S(2)}) collective-permute-start(bf16[2,208,256]{2,1,0:T(8,128)(2,1)S(1)} %pad_maximum_fusion.state_ref), channel_id=1, source_target_pairs={{0,1},{1,0},{2,3},{3,2},{4,5},{5,4},{6,7},{7,6},{8,9},{9,8},{10,11... | collective-permute-start | bytes 638984 | tf_op jit(solution)/shard_map/ppermute | solution.py:243
  36.1 1.9 %copy-start.4 = (f32[3,3,768]{2,1,0:T(4,128)S(1)}, f32[3,3,768]{2,1,0:T(4,128)}, u32[]{:S(2)}) copy-start(f32[3,3,768]{2,1,0:T(4,128)} %refs_4_.1) | copy-start | bytes 82948
  39.2 1.3 %copy-start.2 = (bf16[768,768]{1,0:T(8,128)(2,1)S(1)}, bf16[768,768]{1,0:T(8,128)(2,1)}, u32[]{:S(2)}) copy-start(bf16[768,768]{1,0:T(8,128)(2,1)} %wo_ref.1) | copy-start | bytes 3538948

commit v5 on v4

--- a/solution.py
+++ b/solution.py
@@ -97,7 +97,8 @@
         copy.start()
     fill_marks(vt_ref, half // 2)
     cols = tokens // here
-    blocks = [slice(row * cols, (row + 1) * cols) for row in range(here)]
+    turn = 1 - place_ref[2]
+    blocks = [pl.ds(pl.multiple_of((row + turn * (here - 1 - 2 * row)) * cols, cols), cols) for row in range(here)]
     copies[0].wait()
     copies[1].wait()
     for block, value_ref in zip(blocks, value_refs):
@@ -106,8 +107,8 @@
     for pair in range(half // 2):
         fill_pair(pair_ref, pair, [omega_ref[2 * pair], omega_ref[2 * pair + 1]])
     copies[3].wait()
-    for block in blocks:
-        key_ref[block, :] = jnp.dot(x_ref[block, :], wk_ref[...], preferred_element_type=F32).astype(BF)
+    for row, block in enumerate(blocks):
+        key_ref[row * cols : (row + 1) * cols, :] = jnp.dot(x_ref[block, :], wk_ref[...], preferred_element_type=F32).astype(BF)
     own_ref[...] = key_ref[:, pl.ds(pl.multiple_of(place_ref[0] * span, span), span)]
     turn_values(value_refs, other * span, span, vt_ref)
     half_state(place_ref[1], key_ref, other * span, pair_ref, vt_ref, feat_ref, send_ref)
@@ -141,23 +142,25 @@
             )
 
 
-def conv_kernel_body(*refs):
+def conv_kernel_body(place_ref, *refs):
     taps_ref, out_ref = refs[-2:]
     values = refs[:-2]
     here, cols, width = out_ref.shape
+    turn = 1 - place_ref[2]
     lanes = 128
     col = lax.broadcasted_iota(jnp.int32, (cols, lanes), 0)
     for start in range(0, width, lanes):
         cut = slice(start, start + lanes)
         wide = [value[:, cut].astype(F32) for value in values]
+        taps = [taps_ref[step + turn * (2 - 2 * step), :, cut] for step in range(3)]
         for row in range(here):
             sums = []
             for shift in range(3):
-                terms = [wide[row + step] * taps_ref[step, shift : shift + 1, cut] for step in range(3)]
+                terms = [wide[row + step] * taps[step][shift : shift + 1] for step in range(3)]
                 sums.append(terms[0] + terms[1] + terms[2])
             left = jnp.where(col == 0, 0.0, pltpu.roll(sums[0], 1, 0))
             right = jnp.where(col == cols - 1, 0.0, pltpu.roll(sums[2], cols - 1, 0))
-            out_ref[row, :, cut] = left + sums[1] + right
+            out_ref[row + turn * (here - 1 - 2 * row), :, cut] = left + sums[1] + right
 
 
 def fill_mats(bit, state_ref, mat_ref, dim_head):
@@ -270,7 +273,7 @@
     rows = half // 2 * dim_head + 16
     spot = lax.axis_index("row").astype(jnp.int32)
     bits = [lax.bitwise_and(lax.shift_right_logical(spot, i), 1) for i in range(count.bit_length() - 1)]
-    place = jnp.stack([functools.reduce(lax.bitwise_xor, bits), bits[split.bit_length() - 1]])
+    place = jnp.stack([functools.reduce(lax.bitwise_xor, bits), bits[split.bit_length() - 1], bits[0]])
     proj = 2 * amount * width * width
     feats = 2 * amount * width * nfeat
     vmem = pl.BlockSpec(memory_space=pltpu.VMEM)
@@ -307,8 +310,9 @@
         [pairs, turned, feat],
         feats,
     )(place, key, omega, *values)
-    top = lax.ppermute(values[-1], "row", [(i, i + 1) for i in range(count - 1)])
-    low = lax.ppermute(values[0], "row", [(i + 1, i) for i in range(count - 1)])
+    near = swap(values[0], 1, count)
+    gaps = [(i, i + 1) for i in range(1, count - 1, 2)]
+    far = lax.ppermute(values[-1], "row", gaps + [(high, low) for low, high in gaps])
     (feat_query,) = call(
         query_kernel,
         [jax.ShapeDtypeStruct((amount, heads * nfeat), BF)],
@@ -317,8 +321,8 @@
         proj + feats,
     )(flat, w_query, omega)
     (position,) = call(
-        conv_kernel_body, [jax.ShapeDtypeStruct((here, cols, width), F32)], [vmem] * (here + 3), [], proj
-    )(top, *values, low, conv_kernel)
+        conv_kernel_body, [jax.ShapeDtypeStruct((here, cols, width), F32)], [smem] + [vmem] * (here + 3), [], proj
+    )(place, near, *values, far, conv_kernel)
     mine = reduce_half(send, keep, count, split)
     theirs = swap(mine, 1, count)
     (attn,) = call(

time: 44.3 us -> 44 us (level)
  the two profiles are of different devices: /device:TPU:11 before, /device:TPU:0 now
where the time goes in v5:
time: 44 us; the launch traced here: 43.8 us
  waiting for transfers between devices  17.4 us (40%)
  Pallas kernels  15.2 us (35%)
  starting transfers between devices  10.6 us (24%)
    ppermute x7, waiting for transfers between devices, swap(): lax.ppermute(block, 'row', [(i, i ^ bit ^ (bit > 1)) for i in range(count)])  17.4 us
    ppermute x7, starting transfers between devices, swap(): lax.ppermute(block, 'row', [(i, i ^ bit ^ (bit > 1)) for i in range(count)])  9.93 us
    pallas_call x1, Pallas kernels, layer(): call(first_kernel, [jax.ShapeDtypeStruct((2, rows, nfeat), BF), jax.Shape...  4.95 us
    pallas_call x1, Pallas kernels, layer(): call(out_kernel, [jax.ShapeDtypeStruct((amount, width), BF)], [smem] + [v...  3.54 us
    pallas_call x1, Pallas kernels, layer(): call(conv_kernel_body, [jax.ShapeDtypeStruct((here, cols, width), F32)],...  1.93 us
    pallas_call x1, Pallas kernels, layer(): call(query_kernel, [jax.ShapeDtypeStruct((amount, heads * nfeat), BF)], [...  1.89 us
    pallas_call x1, Pallas kernels, layer(): call(second_kernel, [jax.ShapeDtypeStruct((2, rows, nfeat), F32)], [smem]...  1.76 us
    pallas_call x1, Pallas kernels, layer(): call(own_kernel, [jax.ShapeDtypeStruct((amount, span), F32)], [smem] + [v...  1.16 us
  transfers between devices with their start and end apart: 8, of which 4 were waited for; matrix products, arithmetic and copies ran while one was open for 0% of the time, Pallas kernels for 15%

profile of v5, /device:TPU:0, one launch (start us, length us, event | category | flops | bytes accessed | tf_op | source)
XLA Modules:
  0.0 43.8 jit_solution(1099378346155840765)
XLA Ops:
  0.0 0.1 pad_add_fusion.place_ref
  0.1 0.0 copy-start.1
  0.1 4.9 %shard_map.82 = (bf16[2,208,256]{2,1,0:T(8,128)(2,1)S(1)}, bf16[512,384]{1,0:T(8,128)(2,1)S(1)}, bf16[256,768]{1,0:T(8,128)(2,1)S(1)}, bf16[256,768]{1,0:T(8,128)(2,1)S(1)}) custom-call(s32[3]{0:T(128)S(1)} %pad_add_fusion.place_ref, bf16[512,768]{1,0:T(8,128)(2,1)} %bitcast.21, bf16[768,768]{1,0:T(8,128)(2,1)} %wk_hbm.1, bf16[768,768]{1,0:T(8,128)(2,1)} %wv_hbm.1, ...), custom_call_target="tpu_custom_call" | custom-call | flops 1409286144 | tf_op jit(solution)/shard_map/pallas_call | solution.py:287
  5.0 0.6 %collective-permute-start = (bf16[2,208,256]{2,1,0:T(8,128)(2,1)S(1)}, bf16[2,208,256]{2,1,0:T(8,128)(2,1)S(1)}, u32[]{:S(2)}, u32[]{:S(2)}) collective-permute-start(bf16[2,208,256]{2,1,0:T(8,128)(2,1)S(1)} %get-tuple-element.12), channel_id=1, source_target_pairs={{0,1},{1,0},{2,3},{3,2},{4,5},{5,4},{6,7},{7,6},{8,9},{9,8},{10,11... | collective-permute-start | bytes 638984 | tf_op jit(solution)/shard_map/ppermute | solution.py:246
  5.6 0.0 copy-done.1
  5.6 1.8 %shard_map.83 = f32[2,208,256]{2,1,0:T(8,128)S(1)} custom-call(s32[3]{0:T(128)S(1)} %pad_add_fusion.place_ref, bf16[512,384]{1,0:T(8,128)(2,1)S(1)} %get-tuple-element.9.key_ref, bf16[12,64,256]{2,1,0:T(8,128)(2,1)S(1)} %copy-done.1, bf16[256,768]{1,0:T(8,128)(2,1)S(1)} %get-tuple-element.10.refs_0_.refs_1_, ...), custom_call_target="tpu_custom_call" | custom-call | flops 201326592 | tf_op jit(solution)/shard_map/pallas_call | solution.py:306
  7.4 0.0 collective-permute-done
  7.4 0.0 copy-start.5
  7.4 0.0 copy-start
  7.4 0.0 copy-start.3
  7.5 2.7 %collective-permute-start.1 = (bf16[208,256]{1,0:T(8,128)(2,1)S(1)}, bf16[208,256]{1,0:T(8,128)(2,1)S(1)}, u32[]{:S(2)}, u32[]{:S(2)}) collective-permute-start(bf16[208,256]{1,0:T(8,128)(2,1)S(1)} %fusion.2), channel_id=1, source_target_pairs={{0,5},{1,4},{2,7},{3,6},{4,1},{5,0},{6,3},{7,2},{8,13},{9,12},{10,... | collective-permute-start | bytes 319496 | tf_op jit(solution)/shard_map/ppermute | solution.py:246
  10.2 3.3 %collective-permute-done.1 = bf16[208,256]{1,0:T(8,128)(2,1)S(1)} collective-permute-done((bf16[208,256]{1,0:T(8,128)(2,1)S(1)}, bf16[208,256]{1,0:T(8,128)(2,1)S(1)}, u32[]{:S(2)}, u32[]{:S(2)}) %collective-permute-start.1) | collective-permute-done | bytes 106528 | tf_op jit(solution)/shard_map/ppermute | solution.py:246
  13.6 2.4 %collective-permute-start.2 = (bf16[208,256]{1,0:T(8,128)(2,1)S(1)}, bf16[208,256]{1,0:T(8,128)(2,1)S(1)}, u32[]{:S(2)}, u32[]{:S(2)}) collective-permute-start(bf16[208,256]{1,0:T(8,128)(2,1)S(1)} %fusion.3), channel_id=1, source_target_pairs={{0,9},{1,8},{2,11},{3,10},{4,13},{5,12},{6,15},{7,14},{8,1},{9,0},... | collective-permute-start | bytes 319496 | tf_op jit(solution)/shard_map/ppermute | solution.py:246
  15.9 5.9 %collective-permute-done.2 = bf16[208,256]{1,0:T(8,128)(2,1)S(1)} collective-permute-done((bf16[208,256]{1,0:T(8,128)(2,1)S(1)}, bf16[208,256]{1,0:T(8,128)(2,1)S(1)}, u32[]{:S(2)}, u32[]{:S(2)}) %collective-permute-start.2) | collective-permute-done | bytes 106528 | tf_op jit(solution)/shard_map/ppermute | solution.py:246
  21.8 0.9 %collective-permute-start.3 = (bf16[208,256]{1,0:T(8,128)(2,1)S(1)}, bf16[208,256]{1,0:T(8,128)(2,1)S(1)}, u32[]{:S(2)}, u32[]{:S(2)}) collective-permute-start(bf16[208,256]{1,0:T(8,128)(2,1)S(1)} %fusion.1), channel_id=1, source_target_pairs={{0,3},{1,2},{2,1},{3,0},{4,7},{5,6},{6,5},{7,4},{8,11},{9,10},{10,... | collective-permute-start | bytes 319496 | tf_op jit(solution)/shard_map/ppermute | solution.py:246
  22.8 0.1 collective-permute-start.6
  22.8 0.7 %collective-permute-start.7 = (bf16[256,768]{1,0:T(8,128)(2,1)S(1)}, bf16[256,768]{1,0:T(8,128)(2,1)S(1)}, u32[]{:S(2)}, u32[]{:S(2)}) collective-permute-start(bf16[256,768]{1,0:T(8,128)(2,1)S(1)} %get-tuple-element.11.refs_1_.refs_2_), channel_id=1, source_target_pairs={{1,2},{3,4},{5,6},{7,8},{9,10},{11,12},{13,14},{2,1},{4,3},{6,5},{... | collective-permute-start | bytes 1179656 | tf_op jit(solution)/shard_map/ppermute | solution.py:315
  23.5 3.4 %collective-permute-done.3 = bf16[208,256]{1,0:T(8,128)(2,1)S(1)} collective-permute-done((bf16[208,256]{1,0:T(8,128)(2,1)S(1)}, bf16[208,256]{1,0:T(8,128)(2,1)S(1)}, u32[]{:S(2)}, u32[]{:S(2)}) %collective-permute-start.3) | collective-permute-done | bytes 106528 | tf_op jit(solution)/shard_map/ppermute | solution.py:246
  26.9 0.1 add_convert_fusion
  26.9 0.5 %collective-permute-start.4 = (bf16[208,256]{1,0:T(8,128)(2,1)S(1)}, bf16[208,256]{1,0:T(8,128)(2,1)S(1)}, u32[]{:S(2)}, u32[]{:S(2)}) collective-permute-start(bf16[208,256]{1,0:T(8,128)(2,1)S(1)} %add_convert_fusion), channel_id=1, source_target_pairs={{0,5},{1,4},{2,7},{3,6},{4,1},{5,0},{6,3},{7,2},{8,13},{9,12},{10,... | collective-permute-start | bytes 319496 | tf_op jit(solution)/shard_map/ppermute | solution.py:246
  27.4 4.9 %collective-permute-done.4 = bf16[208,256]{1,0:T(8,128)(2,1)S(1)} collective-permute-done((bf16[208,256]{1,0:T(8,128)(2,1)S(1)}, bf16[208,256]{1,0:T(8,128)(2,1)S(1)}, u32[]{:S(2)}, u32[]{:S(2)}) %collective-permute-start.4) | collective-permute-done | bytes 106528 | tf_op jit(solution)/shard_map/ppermute | solution.py:246
  32.3 2.8 %collective-permute-start.5 = (bf16[2,208,256]{2,1,0:T(8,128)(2,1)S(1)}, bf16[2,208,256]{2,1,0:T(8,128)(2,1)S(1)}, u32[]{:S(2)}, u32[]{:S(2)}) collective-permute-start(bf16[2,208,256]{2,1,0:T(8,128)(2,1)S(1)} %pad_maximum_fusion.state_ref), channel_id=1, source_target_pairs={{0,1},{1,0},{2,3},{3,2},{4,5},{5,4},{6,7},{7,6},{8,9},{9,8},{10,11... | collective-permute-start | bytes 638984 | tf_op jit(solution)/shard_map/ppermute | solution.py:246
  35.1 0.0 copy-done.5
  35.1 0.0 copy-done
  35.1 0.0 copy-done.3
  35.1 0.0 copy-start.4
  35.1 1.9 %shard_map.84.feat_ref = bf16[512,3072]{1,0:T(8,128)(2,1)S(1)} custom-call(bf16[512,768]{1,0:T(8,128)(2,1)S(1)} %bitcast.22, bf16[768,768]{1,0:T(8,128)(2,1)S(1)} %copy-done.3, bf16[12,64,256]{2,1,0:T(8,128)(2,1)S(1)} %copy-done.1), custom_call_target="tpu_custom_call" | custom-call | flops 805306368 | tf_op jit(solution)/shard_map/pallas_call | solution.py:316
  37.0 0.0 collective-permute-done.6.refs_0_
  37.0 0.0 collective-permute-done.7.refs_3_
  37.0 0.0 copy-done.4
  37.1 1.9 %shard_map.86 = f32[2,256,768]{2,1,0:T(8,128)S(1)} custom-call(s32[3]{0:T(128)S(1)} %pad_add_fusion.place_ref, bf16[256,768]{1,0:T(8,128)(2,1)S(1)} %collective-permute-done.6.refs_0_, bf16[256,768]{1,0:T(8,128)(2,1)S(1)} %get-tuple-element.10.refs_0_.refs_1_, bf16[256,768]{1,0:T(8,128)(2,1)S(1)} %get-tuple-element.11.refs_1_.refs_2_, ...), custom_call_target="tpu_custom_call" | custom-call | flops 603979776 | tf_op jit(solution)/shard_map/pallas_call | solution.py:323
  39.0 0.0 copy-start.2
  39.0 1.2 %shard_map.85.own_ref = f32[512,384]{1,0:T(8,128)S(1)} custom-call(s32[3]{0:T(128)S(1)} %pad_add_fusion.place_ref, bf16[2,208,256]{2,1,0:T(8,128)(2,1)S(1)} %pad_maximum_fusion.state_ref, bf16[512,3072]{1,0:T(8,128)(2,1)S(1)} %shard_map.84.feat_ref), custom_call_target="tpu_custom_call" | custom-call | flops 201326592 | tf_op jit(solution)/shard_map/pallas_call | solution.py:328
  40.2 0.0 collective-permute-done.5.state_ref
  40.2 0.1 copy-done.2
  40.3 3.5 %shard_map.87 = bf16[512,768]{1,0:T(8,128)(2,1)} custom-call(s32[3]{0:T(128)S(1)} %pad_add_fusion.place_ref, bf16[2,208,256]{2,1,0:T(8,128)(2,1)S(1)} %collective-permute-done.5.state_ref, bf16[512,3072]{1,0:T(8,128)(2,1)S(1)} %shard_map.84.feat_ref, f32[512,384]{1,0:T(8,128)S(1)} %shard_map.85.own_ref, f32[512,768]{1,0:T(8,128)S(1)} %bitcast.20, ...), custom_call_target="tpu_custom_call" | custom-call | flops 805306368 | tf_op jit(solution)/shard_map/pallas_call | solution.py:331
  (6 shorter events, 0.2 us)
Async XLA Ops:
  0.1 5.5 %copy-start.1 = (bf16[12,64,256]{2,1,0:T(8,128)(2,1)S(1)}, bf16[12,64,256]{2,1,0:T(8,128)(2,1)}, u32[]{:S(2)}) copy-start(bf16[12,64,256]{2,1,0:T(8,128)(2,1)} %omega_ref.3) | copy-start | bytes 1179652
  5.0 2.3 %collective-permute-start = (bf16[2,208,256]{2,1,0:T(8,128)(2,1)S(1)}, bf16[2,208,256]{2,1,0:T(8,128)(2,1)S(1)}, u32[]{:S(2)}, u32[]{:S(2)}) collective-permute-start(bf16[2,208,256]{2,1,0:T(8,128)(2,1)S(1)} %get-tuple-element.12), channel_id=1, source_target_pairs={{0,1},{1,0},{2,3},{3,2},{4,5},{5,4},{6,7},{7,6},{8,9},{9,8},{10,11... | collective-permute-start | bytes 638984 | tf_op jit(solution)/shard_map/ppermute | solution.py:246
  7.4 27.7 %copy-start.5 = (f32[768]{0:T(1024)S(1)}, f32[768]{0:T(1024)}, u32[]{:S(2)}) copy-start(f32[768]{0:T(1024)} %param.15) | copy-start | bytes 9220
  7.4 27.7 %copy-start = (bf16[2,256,768]{2,1,0:T(8,128)(2,1)S(1)}, bf16[2,256,768]{2,1,0:T(8,128)(2,1)}, u32[]{:S(2)}) copy-start(bf16[2,256,768]{2,1,0:T(8,128)(2,1)} %param.8) | copy-start | bytes 2359300
  7.4 27.7 %copy-start.3 = (bf16[768,768]{1,0:T(8,128)(2,1)S(1)}, bf16[768,768]{1,0:T(8,128)(2,1)}, u32[]{:S(2)}) copy-start(bf16[768,768]{1,0:T(8,128)(2,1)} %wq_ref.1) | copy-start | bytes 3538948
  7.5 6.1 %collective-permute-start.1 = (bf16[208,256]{1,0:T(8,128)(2,1)S(1)}, bf16[208,256]{1,0:T(8,128)(2,1)S(1)}, u32[]{:S(2)}, u32[]{:S(2)}) collective-permute-start(bf16[208,256]{1,0:T(8,128)(2,1)S(1)} %fusion.2), channel_id=1, source_target_pairs={{0,5},{1,4},{2,7},{3,6},{4,1},{5,0},{6,3},{7,2},{8,13},{9,12},{10,... | collective-permute-start | bytes 319496 | tf_op jit(solution)/shard_map/ppermute | solution.py:246
  13.6 8.2 %collective-permute-start.2 = (bf16[208,256]{1,0:T(8,128)(2,1)S(1)}, bf16[208,256]{1,0:T(8,128)(2,1)S(1)}, u32[]{:S(2)}, u32[]{:S(2)}) collective-permute-start(bf16[208,256]{1,0:T(8,128)(2,1)S(1)} %fusion.3), channel_id=1, source_target_pairs={{0,9},{1,8},{2,11},{3,10},{4,13},{5,12},{6,15},{7,14},{8,1},{9,0},... | collective-permute-start | bytes 319496 | tf_op jit(solution)/shard_map/ppermute | solution.py:246
  21.8 5.0 %collective-permute-start.3 = (bf16[208,256]{1,0:T(8,128)(2,1)S(1)}, bf16[208,256]{1,0:T(8,128)(2,1)S(1)}, u32[]{:S(2)}, u32[]{:S(2)}) collective-permute-start(bf16[208,256]{1,0:T(8,128)(2,1)S(1)} %fusion.1), channel_id=1, source_target_pairs={{0,3},{1,2},{2,1},{3,0},{4,7},{5,6},{6,5},{7,4},{8,11},{9,10},{10,... | collective-permute-start | bytes 319496 | tf_op jit(solution)/shard_map/ppermute | solution.py:246
  22.8 14.3 %collective-permute-start.6 = (bf16[256,768]{1,0:T(8,128)(2,1)S(1)}, bf16[256,768]{1,0:T(8,128)(2,1)S(1)}, u32[]{:S(2)}, u32[]{:S(2)}) collective-permute-start(bf16[256,768]{1,0:T(8,128)(2,1)S(1)} %get-tuple-element.10.refs_0_.refs_1_), channel_id=1, source_target_pairs={{0,1},{1,0},{2,3},{3,2},{4,5},{5,4},{6,7},{7,6},{8,9},{9,8},{10,11... | collective-permute-start | bytes 1179656 | tf_op jit(solution)/shard_map/ppermute | solution.py:246
  22.8 14.2 %collective-permute-start.7 = (bf16[256,768]{1,0:T(8,128)(2,1)S(1)}, bf16[256,768]{1,0:T(8,128)(2,1)S(1)}, u32[]{:S(2)}, u32[]{:S(2)}) collective-permute-start(bf16[256,768]{1,0:T(8,128)(2,1)S(1)} %get-tuple-element.11.refs_1_.refs_2_), channel_id=1, source_target_pairs={{1,2},{3,4},{5,6},{7,8},{9,10},{11,12},{13,14},{2,1},{4,3},{6,5},{... | collective-permute-start | bytes 1179656 | tf_op jit(solution)/shard_map/ppermute | solution.py:315
  26.9 5.3 %collective-permute-start.4 = (bf16[208,256]{1,0:T(8,128)(2,1)S(1)}, bf16[208,256]{1,0:T(8,128)(2,1)S(1)}, u32[]{:S(2)}, u32[]{:S(2)}) collective-permute-start(bf16[208,256]{1,0:T(8,128)(2,1)S(1)} %add_convert_fusion), channel_id=1, source_target_pairs={{0,5},{1,4},{2,7},{3,6},{4,1},{5,0},{6,3},{7,2},{8,13},{9,12},{10,... | collective-permute-start | bytes 319496 | tf_op jit(solution)/shard_map/ppermute | solution.py:246
  32.3 7.9 %collective-permute-start.5 = (bf16[2,208,256]{2,1,0:T(8,128)(2,1)S(1)}, bf16[2,208,256]{2,1,0:T(8,128)(2,1)S(1)}, u32[]{:S(2)}, u32[]{:S(2)}) collective-permute-start(bf16[2,208,256]{2,1,0:T(8,128)(2,1)S(1)} %pad_maximum_fusion.state_ref), channel_id=1, source_target_pairs={{0,1},{1,0},{2,3},{3,2},{4,5},{5,4},{6,7},{7,6},{8,9},{9,8},{10,11... | collective-permute-start | bytes 638984 | tf_op jit(solution)/shard_map/ppermute | solution.py:246
  35.1 1.9 %copy-start.4 = (f32[3,3,768]{2,1,0:T(4,128)S(1)}, f32[3,3,768]{2,1,0:T(4,128)}, u32[]{:S(2)}) copy-start(f32[3,3,768]{2,1,0:T(4,128)} %refs_4_.1) | copy-start | bytes 82948
  39.0 1.3 %copy-start.2 = (bf16[768,768]{1,0:T(8,128)(2,1)S(1)}, bf16[768,768]{1,0:T(8,128)(2,1)}, u32[]{:S(2)}) copy-start(bf16[768,768]{1,0:T(8,128)(2,1)} %wo_ref.1) | copy-start | bytes 3538948

commit v6 on v4

--- a/solution.py
+++ b/solution.py
@@ -1,4 +1,3 @@
-import functools
 import math
 
 import jax
@@ -54,23 +53,23 @@
     heads, rows, tokens = vt_ref.shape
     dim_head = rows - 16
     wide = 2 * dim_head
-    nfeat = feat_ref.shape[1] // 2
+    nfeat = feat_ref.shape[2] // 2
     group = heads // 2
     tile = tiles_of(tokens, TILE)
     sums = None
+    for pair in range(heads // 2):
+            lanes = slice(pair * wide, (pair + 1) * wide) if isinstance(offset, int) else pl.ds(pl.multiple_of(offset + pair * wide, wide), wide)
+            for start in range(0, tokens, tile):
+                feat_ref[pair, start : start + tile, :] = feature_tile(key_ref[start : start + tile, lanes], pair_ref[pair], dim_head, nfeat)
     for head in range(heads):
         pair, side = head // 2, head % 2
-        if side == 0:
-            lanes = slice(pair * wide, (pair + 1) * wide) if isinstance(offset, int) else pl.ds(pl.multiple_of(offset + pair * wide, wide), wide)
-            for start in range(0, tokens, tile):
-                feat_ref[start : start + tile, :] = feature_tile(key_ref[start : start + tile, lanes], pair_ref[pair], dim_head, nfeat)
-        local = jnp.dot(vt_ref[head], feat_ref[:, side * nfeat : (side + 1) * nfeat], preferred_element_type=F32)
+        local = jnp.dot(vt_ref[head], feat_ref[pair, :, side * nfeat : (side + 1) * nfeat], preferred_element_type=F32)
         slot = lax.rem(bit + head // group, 2)
         spot = head % group
         state_ref[slot, spot * dim_head : (spot + 1) * dim_head, :] = local[:dim_head].astype(state_ref.dtype)
         sums = local[dim_head:] if spot == 0 else sums + local[dim_head:]
         if spot == group - 1:
-            state_ref[slot, group * dim_head :, :] = sums.astype(state_ref.dtype)
+            state_ref[slot, group * dim_head :, :] = sums[:8].astype(state_ref.dtype)
 
 
 def turn_values(value_refs, offset, span, vt_ref):
@@ -142,9 +141,10 @@
 
 
 def conv_kernel_body(*refs):
-    taps_ref, out_ref = refs[-2:]
-    values = refs[:-2]
-    here, cols, width = out_ref.shape
+    x_ref, wo_ref, taps_ref, out_ref, pos_ref = refs[-5:]
+    values = refs[:-5]
+    here = len(values) - 2
+    cols, width = values[0].shape
     lanes = 128
     col = lax.broadcasted_iota(jnp.int32, (cols, lanes), 0)
     for start in range(0, width, lanes):
@@ -157,7 +157,10 @@
                 sums.append(terms[0] + terms[1] + terms[2])
             left = jnp.where(col == 0, 0.0, pltpu.roll(sums[0], 1, 0))
             right = jnp.where(col == cols - 1, 0.0, pltpu.roll(sums[2], cols - 1, 0))
-            out_ref[row, :, cut] = left + sums[1] + right
+            pos_ref[row * cols : (row + 1) * cols, cut] = (left + sums[1] + right).astype(BF)
+    for row in range(here):
+        cut = slice(row * cols, (row + 1) * cols)
+        out_ref[cut, :] = x_ref[cut, :].astype(F32) + jnp.dot(pos_ref[cut, :], wo_ref[...], preferred_element_type=F32)
 
 
 def fill_mats(bit, state_ref, mat_ref, dim_head):
@@ -186,53 +189,59 @@
     return both[:, :wide] / both[:, wide:]
 
 
-def own_kernel(place_ref, state_ref, feat_ref, attn_ref, mat_ref):
-    pairs, rows, both = mat_ref.shape
+def own_kernel(place_ref, state_ref, feat_ref, gain_ref, wo_ref, part_ref, square_ref, mat_ref):
+    pairs, rows, _ = mat_ref.shape
     wide = rows // 2
-    tokens = attn_ref.shape[0]
+    tokens = part_ref.shape[0]
+    span = pairs * wide
+    core = place_ref[0]
     fill_mats(place_ref[1], state_ref, mat_ref, wide // 2)
     tile = tiles_of(tokens, 256)
     for start in range(0, tokens, tile):
-        for pair in range(pairs):
-            attn_ref[start : start + tile, pair * wide : (pair + 1) * wide] = attend(
-                feat_ref[start : start + tile, pl.ds(pl.multiple_of((place_ref[0] * pairs + pair) * both, both), both)], mat_ref[pair], wide
-            )
-
-
-def out_kernel(place_ref, state_ref, feat_ref, own_ref, pos_ref, x_ref, gain_ref, wo_ref, out_ref, mat_ref, attn_ref):
+        cut = slice(start, start + tile)
+        part_ref[cut, :], square_ref[cut, :] = half_share(core, span, feat_ref, cut, gain_ref, wo_ref, mat_ref)
+
+
+def half_share(side, span, feat_ref, cut, gain_ref, wo_ref, mat_ref):
     pairs, rows, both = mat_ref.shape
     wide = rows // 2
-    tokens, width = x_ref.shape
-    span = width // 2
-    core = place_ref[0]
+    base = pl.multiple_of(side * span, span)
+    total, scaled = None, []
+    for pair in range(pairs):
+        lanes = pl.ds(pl.multiple_of((side * pairs + pair) * both, both), both)
+        attn = attend(feat_ref[cut, lanes], mat_ref[pair], wide)
+        total = attn * attn if total is None else total + attn * attn
+        gain = gain_ref[:, pl.ds(pl.multiple_of(base + pair * wide, wide), wide)]
+        scaled.append((attn * gain).astype(BF))
+    share = jnp.dot(jnp.concatenate(scaled, axis=1), wo_ref[pl.ds(base, span), :], preferred_element_type=F32)
+    return share, total
+
+
+def out_kernel(place_ref, state_ref, feat_ref, part_ref, square_ref, base_ref, gain_ref, wo_ref, out_hbm, mat_ref, out_ref, sems):
+    _, rows, _ = mat_ref.shape
+    wide = rows // 2
+    tokens, width = base_ref.shape
     fill_mats(place_ref[1], state_ref, mat_ref, wide // 2)
-    mine = pl.ds(pl.multiple_of(core * span, span), span)
-    other = pl.ds(pl.multiple_of((1 - core) * span, span), span)
     tile = tiles_of(tokens, 256)
+    copies = []
     for start in range(0, tokens, tile):
         cut = slice(start, start + tile)
-        total = None
-        for pair in range(pairs):
-            lanes = slice(pair * wide, (pair + 1) * wide)
-            attn = attend(feat_ref[cut, pl.ds(pl.multiple_of(((1 - core) * pairs + pair) * both, both), both)], mat_ref[pair], wide)
-            attn_ref[:, lanes] = attn
-            kept = own_ref[cut, lanes]
-            square = attn * attn + kept * kept
-            total = square if total is None else total + square
+        share, total = half_share(1 - place_ref[0], width // 2, feat_ref, cut, gain_ref, wo_ref, mat_ref)
+        total = total + square_ref[cut, :]
         scale = lax.rsqrt(jnp.sum(total, axis=1, keepdims=True) * (1.0 / width) + 1e-06)
-        out = x_ref[cut, :].astype(F32)
-        for part, attn in ((mine, own_ref[cut, :]), (other, attn_ref[...])):
-            mixed = (attn * scale * gain_ref[:, part] + pos_ref[cut, part]).astype(BF)
-            out = out + jnp.dot(mixed, wo_ref[part, :], preferred_element_type=F32)
-        out_ref[cut, :] = out.astype(BF)
-
-
-def call(kernel, out_shape, in_specs, scratch, flops, limit=VMEM_LIMIT):
+        out_ref[cut, :] = (base_ref[cut, :] + scale * (share + part_ref[cut, :])).astype(BF)
+        copies.append(pltpu.make_async_copy(out_ref.at[cut], out_hbm.at[cut], sems.at[start // tile]))
+        copies[-1].start()
+    for copy in copies:
+        copy.wait()
+
+
+def call(kernel, out_shape, in_specs, scratch, flops, limit=VMEM_LIMIT, space=pltpu.VMEM):
     return pl.pallas_call(
         kernel,
         out_shape=out_shape,
         in_specs=in_specs,
-        out_specs=[pl.BlockSpec(memory_space=pltpu.VMEM)] * len(out_shape),
+        out_specs=[pl.BlockSpec(memory_space=space)] * len(out_shape),
         scratch_shapes=scratch,
         compiler_params=pltpu.CompilerParams(vmem_limit_bytes=limit),
         cost_estimate=pl.CostEstimate(flops=flops, bytes_accessed=0, transcendentals=0),
@@ -240,7 +249,7 @@
 
 
 def swap(block, bit, count):
-    return lax.ppermute(block, "row", [(i, i ^ bit ^ (bit > 1)) for i in range(count)])
+    return lax.ppermute(block, "row", [(i, i ^ bit) for i in range(count)])
 
 
 def reduce_half(send, keep, count, split):
@@ -267,10 +276,10 @@
     flat = tokens.reshape(here * cols, width)
     amount = here * cols
     half, span = heads // 2, width // 2
-    rows = half // 2 * dim_head + 16
+    rows = half // 2 * dim_head + 8
     spot = lax.axis_index("row").astype(jnp.int32)
     bits = [lax.bitwise_and(lax.shift_right_logical(spot, i), 1) for i in range(count.bit_length() - 1)]
-    place = jnp.stack([functools.reduce(lax.bitwise_xor, bits), bits[split.bit_length() - 1]])
+    place = jnp.stack([bits[0], bits[split.bit_length() - 1]])
     proj = 2 * amount * width * width
     feats = 2 * amount * width * nfeat
     vmem = pl.BlockSpec(memory_space=pltpu.VMEM)
@@ -278,7 +287,7 @@
     hbm = pl.BlockSpec(memory_space=pltpu.HBM)
     pairs = pltpu.VMEM((half // 2, 2 * dim_head, 2 * nfeat), BF)
     turned = pltpu.VMEM((half, dim_head + 16, amount), BF)
-    feat = pltpu.VMEM((amount, 2 * nfeat), BF)
+    feat = pltpu.VMEM((half // 2, amount, 2 * nfeat), BF)
     mats = pltpu.VMEM((half // 2, 4 * dim_head, 2 * nfeat), BF)
 
     send, key, *values = call(
@@ -316,21 +325,32 @@
         [pltpu.VMEM((half, 2 * dim_head, 2 * nfeat), BF)],
         proj + feats,
     )(flat, w_query, omega)
-    (position,) = call(
-        conv_kernel_body, [jax.ShapeDtypeStruct((here, cols, width), F32)], [vmem] * (here + 3), [], proj
-    )(top, *values, low, conv_kernel)
+    (base,) = call(
+        conv_kernel_body,
+        [jax.ShapeDtypeStruct((amount, width), F32)],
+        [vmem] * (here + 5),
+        [pltpu.VMEM((amount, width), BF)],
+        proj,
+    )(top, *values, low, flat, w_out, conv_kernel)
     mine = reduce_half(send, keep, count, split)
     theirs = swap(mine, 1, count)
-    (attn,) = call(
-        own_kernel, [jax.ShapeDtypeStruct((amount, span), F32)], [smem] + [vmem] * 2, [mats], feats
-    )(place, mine, feat_query)
+    gain = norm_gain.reshape(1, width)
+    part, square = call(
+        own_kernel,
+        [jax.ShapeDtypeStruct((amount, width), F32), jax.ShapeDtypeStruct((amount, 2 * dim_head), F32)],
+        [smem] + [vmem] * 4,
+        [mats],
+        feats,
+    )(place, mine, feat_query, gain, w_out)
+    tile = tiles_of(amount, 256)
     (out,) = call(
         out_kernel,
         [jax.ShapeDtypeStruct((amount, width), BF)],
         [smem] + [vmem] * 7,
-        [mats, pltpu.VMEM((tiles_of(amount, 256), span), F32)],
+        [mats, pltpu.VMEM((amount, width), BF), pltpu.SemaphoreType.DMA((amount // tile,))],
         proj + feats,
-    )(place, theirs, feat_query, attn, position.reshape(amount, width), flat, norm_gain.reshape(1, width), w_out)
+        space=pltpu.HBM,
+    )(place, theirs, feat_query, part, square, base, gain, w_out)
     return out.reshape(here, cols, width)
 
 

time: 44.3 us -> 42.9 us (0.968)
  the two profiles are of different devices: /device:TPU:11 before, /device:TPU:27 now
where the time goes in v6:
time: 42.9 us; the launch traced here: 42.7 us
  waiting for transfers between devices  19.1 us (45%)
  Pallas kernels  14.6 us (34%)
  starting transfers between devices  8.56 us (20%)
    ppermute x6, waiting for transfers between devices, swap(): return lax.ppermute(block, 'row', [(i, i ^ bit) for i in range(count)])  19.1 us
    pallas_call x1, Pallas kernels, layer(): call(first_kernel, [jax.ShapeDtypeStruct((2, rows, nfeat), BF), jax.Shape...  4.82 us
    ppermute x6, starting transfers between devices, swap(): return lax.ppermute(block, 'row', [(i, i ^ bit) for i in range(count)])  4.44 us
    ppermute x1, starting transfers between devices, layer(): low = lax.ppermute(values[0], 'row', [(i + 1, i) for i in range(count - 1)])  2.83 us
    pallas_call x1, Pallas kernels, layer(): call(out_kernel, [jax.ShapeDtypeStruct((amount, width), BF)], [smem] + [v...  2.58 us
    pallas_call x1, Pallas kernels, layer(): call(query_kernel, [jax.ShapeDtypeStruct((amount, heads * nfeat), BF)], [...  1.9 us
    pallas_call x1, Pallas kernels, layer(): call(conv_kernel_body, [jax.ShapeDtypeStruct((amount, width), F32)], [vme...  1.86 us
    pallas_call x1, Pallas kernels, layer(): call(own_kernel, [jax.ShapeDtypeStruct((amount, width), F32), jax.ShapeDt...  1.78 us
  transfers between devices with their start and end apart: 8, of which 3 were waited for; matrix products, arithmetic and copies ran while one was open for 0% of the time, Pallas kernels for 17%

profile of v6, /device:TPU:27, one launch (start us, length us, event | category | flops | bytes accessed | tf_op | source)
XLA Modules:
  0.0 42.7 jit_solution(17053883142865482620)
XLA Ops:
  0.0 0.1 pad_add_fusion.place_ref
  0.1 0.0 copy-start.2
  0.1 4.8 %shard_map.82 = (bf16[2,200,256]{2,1,0:T(8,128)(2,1)S(1)}, bf16[512,384]{1,0:T(8,128)(2,1)S(1)}, bf16[256,768]{1,0:T(8,128)(2,1)S(1)}, bf16[256,768]{1,0:T(8,128)(2,1)S(1)}) custom-call(s32[2]{0:T(128)S(1)} %pad_add_fusion.place_ref, bf16[512,768]{1,0:T(8,128)(2,1)} %bitcast.18, bf16[768,768]{1,0:T(8,128)(2,1)} %wk_hbm.1, bf16[768,768]{1,0:T(8,128)(2,1)} %wv_hbm.1, ...), custom_call_target="tpu_custom_call" | custom-call | flops 1409286144 | tf_op jit(solution)/shard_map/pallas_call | solution.py:293
  4.9 0.7 %collective-permute-start = (bf16[2,200,256]{2,1,0:T(8,128)(2,1)S(1)}, bf16[2,200,256]{2,1,0:T(8,128)(2,1)S(1)}, u32[]{:S(2)}, u32[]{:S(2)}) collective-permute-start(bf16[2,200,256]{2,1,0:T(8,128)(2,1)S(1)} %get-tuple-element.14), channel_id=1, source_target_pairs={{0,1},{1,0},{2,3},{3,2},{4,5},{5,4},{6,7},{7,6},{8,9},{9,8},{10,11... | collective-permute-start | bytes 614408 | tf_op jit(solution)/shard_map/ppermute | solution.py:252
  5.6 0.0 copy-done.2
  5.6 1.7 %shard_map.83 = f32[2,200,256]{2,1,0:T(8,128)S(1)} custom-call(s32[2]{0:T(128)S(1)} %pad_add_fusion.place_ref, bf16[512,384]{1,0:T(8,128)(2,1)S(1)} %get-tuple-element.11.key_ref, bf16[12,64,256]{2,1,0:T(8,128)(2,1)S(1)} %copy-done.2, bf16[256,768]{1,0:T(8,128)(2,1)S(1)} %get-tuple-element.12.refs_0_.refs_1_, ...), custom_call_target="tpu_custom_call" | custom-call | flops 201326592 | tf_op jit(solution)/shard_map/pallas_call | solution.py:312
  7.3 0.0 collective-permute-done
  7.4 0.0 copy-start.5
  7.4 0.0 copy-start.1
  7.4 0.0 copy-start.3
  7.4 0.2 collective-permute-start.1
  7.7 4.3 %collective-permute-done.1 = bf16[200,256]{1,0:T(8,128)(2,1)S(1)} collective-permute-done((bf16[200,256]{1,0:T(8,128)(2,1)S(1)}, bf16[200,256]{1,0:T(8,128)(2,1)S(1)}, u32[]{:S(2)}, u32[]{:S(2)}) %collective-permute-start.1) | collective-permute-done | bytes 102432 | tf_op jit(solution)/shard_map/ppermute | solution.py:252
  11.9 0.1 collective-permute-start.2
  12.1 7.6 %collective-permute-done.2 = bf16[200,256]{1,0:T(8,128)(2,1)S(1)} collective-permute-done((bf16[200,256]{1,0:T(8,128)(2,1)S(1)}, bf16[200,256]{1,0:T(8,128)(2,1)S(1)}, u32[]{:S(2)}, u32[]{:S(2)}) %collective-permute-start.2) | collective-permute-done | bytes 102432 | tf_op jit(solution)/shard_map/ppermute | solution.py:252
  19.7 0.3 collective-permute-start.3
  20.0 2.8 %collective-permute-start.7 = (bf16[256,768]{1,0:T(8,128)(2,1)S(1)}, bf16[256,768]{1,0:T(8,128)(2,1)S(1)}, u32[]{:S(2)}, u32[]{:S(2)}) collective-permute-start(bf16[256,768]{1,0:T(8,128)(2,1)S(1)} %get-tuple-element.12.refs_0_.refs_1_), channel_id=1, source_target_pairs={{1,0},{2,1},{3,2},{4,3},{5,4},{6,5},{7,6},{8,7},{9,8},{10,9},{11,1... | collective-permute-start | bytes 1179656 | tf_op jit(solution)/shard_map/ppermute | solution.py:320
  22.9 1.3 %collective-permute-start.6 = (bf16[256,768]{1,0:T(8,128)(2,1)S(1)}, bf16[256,768]{1,0:T(8,128)(2,1)S(1)}, u32[]{:S(2)}, u32[]{:S(2)}) collective-permute-start(bf16[256,768]{1,0:T(8,128)(2,1)S(1)} %get-tuple-element.13.refs_1_.refs_2_), channel_id=1, source_target_pairs={{0,1},{1,2},{2,3},{3,4},{4,5},{5,6},{6,7},{7,8},{8,9},{9,10},{10,1... | collective-permute-start | bytes 1179656 | tf_op jit(solution)/shard_map/ppermute | solution.py:319
  24.2 0.0 collective-permute-done.3
  24.2 0.1 add_convert_fusion
  24.2 3.0 %collective-permute-start.4 = (bf16[200,256]{1,0:T(8,128)(2,1)S(1)}, bf16[200,256]{1,0:T(8,128)(2,1)S(1)}, u32[]{:S(2)}, u32[]{:S(2)}) collective-permute-start(bf16[200,256]{1,0:T(8,128)(2,1)S(1)} %add_convert_fusion), channel_id=1, source_target_pairs={{0,4},{1,5},{2,6},{3,7},{4,0},{5,1},{6,2},{7,3},{8,12},{9,13},{10,... | collective-permute-start | bytes 307208 | tf_op jit(solution)/shard_map/ppermute | solution.py:252
  27.2 7.2 %collective-permute-done.4 = bf16[200,256]{1,0:T(8,128)(2,1)S(1)} collective-permute-done((bf16[200,256]{1,0:T(8,128)(2,1)S(1)}, bf16[200,256]{1,0:T(8,128)(2,1)S(1)}, u32[]{:S(2)}, u32[]{:S(2)}) %collective-permute-start.4) | collective-permute-done | bytes 102432 | tf_op jit(solution)/shard_map/ppermute | solution.py:252
  34.4 0.1 collective-permute-start.5
  34.5 0.0 copy-done.5
  34.5 0.0 copy-done.1
  34.5 0.0 copy-done.3
  34.5 0.0 copy-start
  34.5 0.0 copy-start.4
  34.5 1.9 %shard_map.84.feat_ref = bf16[512,3072]{1,0:T(8,128)(2,1)S(1)} custom-call(bf16[512,768]{1,0:T(8,128)(2,1)S(1)} %bitcast.19, bf16[768,768]{1,0:T(8,128)(2,1)S(1)} %copy-done.3, bf16[12,64,256]{2,1,0:T(8,128)(2,1)S(1)} %copy-done.2), custom_call_target="tpu_custom_call" | custom-call | flops 805306368 | tf_op jit(solution)/shard_map/pallas_call | solution.py:321
  36.5 0.0 collective-permute-done.7.refs_3_
  36.5 0.0 collective-permute-done.6.refs_0_
  36.5 0.0 copy-done
  36.5 0.0 copy-done.4
  36.5 1.9 %shard_map.86.base_ref = f32[512,768]{1,0:T(8,128)S(1)} custom-call(bf16[256,768]{1,0:T(8,128)(2,1)S(1)} %collective-permute-done.6.refs_0_, bf16[256,768]{1,0:T(8,128)(2,1)S(1)} %get-tuple-element.12.refs_0_.refs_1_, bf16[256,768]{1,0:T(8,128)(2,1)S(1)} %get-tuple-element.13.refs_1_.refs_2_, bf16[256,768]{1,0:T(8,128)(2,1)S(1)} %collective-permute-done.7.refs_3_, ...), custom_call_target="tpu_custom_call" | custom-call | flops 603979776 | tf_op jit(solution)/shard_map/pallas_call | solution.py:328
  38.4 1.8 %shard_map.85 = (f32[512,768]{1,0:T(8,128)S(1)}, f32[512,128]{1,0:T(8,128)S(1)}) custom-call(s32[2]{0:T(128)S(1)} %pad_add_fusion.place_ref, bf16[2,200,256]{2,1,0:T(8,128)(2,1)S(1)} %pad_maximum_fusion.state_ref, bf16[512,3072]{1,0:T(8,128)(2,1)S(1)} %shard_map.84.feat_ref, f32[1,768]{1,0:T(1,128)S(1)} %reshape.11.gain_ref, bf16[768,768]{1,0:T(8,128)(2,1)S(1)} %copy-done), custom_call_target="tpu_custom_call" | custom-call | flops 201326592 | tf_op jit(solution)/shard_map/pallas_call | solution.py:338
  40.1 0.0 collective-permute-done.5.state_ref
  40.2 2.6 %shard_map.87 = bf16[512,768]{1,0:T(8,128)(2,1)} custom-call(s32[2]{0:T(128)S(1)} %pad_add_fusion.place_ref, bf16[2,200,256]{2,1,0:T(8,128)(2,1)S(1)} %collective-permute-done.5.state_ref, bf16[512,3072]{1,0:T(8,128)(2,1)S(1)} %shard_map.84.feat_ref, f32[512,768]{1,0:T(8,128)S(1)} %get-tuple-element.15.part_ref, ...), custom_call_target="tpu_custom_call" | custom-call | flops 805306368 | tf_op jit(solution)/shard_map/pallas_call | solution.py:346
  (6 shorter events, 0.1 us)
Async XLA Ops:
  0.1 5.6 %copy-start.2 = (bf16[12,64,256]{2,1,0:T(8,128)(2,1)S(1)}, bf16[12,64,256]{2,1,0:T(8,128)(2,1)}, u32[]{:S(2)}) copy-start(bf16[12,64,256]{2,1,0:T(8,128)(2,1)} %omega_ref.3) | copy-start | bytes 1179652
  4.9 2.4 %collective-permute-start = (bf16[2,200,256]{2,1,0:T(8,128)(2,1)S(1)}, bf16[2,200,256]{2,1,0:T(8,128)(2,1)S(1)}, u32[]{:S(2)}, u32[]{:S(2)}) collective-permute-start(bf16[2,200,256]{2,1,0:T(8,128)(2,1)S(1)} %get-tuple-element.14), channel_id=1, source_target_pairs={{0,1},{1,0},{2,3},{3,2},{4,5},{5,4},{6,7},{7,6},{8,9},{9,8},{10,11... | collective-permute-start | bytes 614408 | tf_op jit(solution)/shard_map/ppermute | solution.py:252
  7.4 27.1 %copy-start.5 = (f32[768]{0:T(1024)S(1)}, f32[768]{0:T(1024)}, u32[]{:S(2)}) copy-start(f32[768]{0:T(1024)} %param.15) | copy-start | bytes 9220
  7.4 27.1 %copy-start.1 = (bf16[2,256,768]{2,1,0:T(8,128)(2,1)S(1)}, bf16[2,256,768]{2,1,0:T(8,128)(2,1)}, u32[]{:S(2)}) copy-start(bf16[2,256,768]{2,1,0:T(8,128)(2,1)} %param.8) | copy-start | bytes 2359300
  7.4 27.1 %copy-start.3 = (bf16[768,768]{1,0:T(8,128)(2,1)S(1)}, bf16[768,768]{1,0:T(8,128)(2,1)}, u32[]{:S(2)}) copy-start(bf16[768,768]{1,0:T(8,128)(2,1)} %wq_ref.1) | copy-start | bytes 3538948
  7.4 4.5 %collective-permute-start.1 = (bf16[200,256]{1,0:T(8,128)(2,1)S(1)}, bf16[200,256]{1,0:T(8,128)(2,1)S(1)}, u32[]{:S(2)}, u32[]{:S(2)}) collective-permute-start(bf16[200,256]{1,0:T(8,128)(2,1)S(1)} %fusion.2), channel_id=1, source_target_pairs={{0,4},{1,5},{2,6},{3,7},{4,0},{5,1},{6,2},{7,3},{8,12},{9,13},{10,... | collective-permute-start | bytes 307208 | tf_op jit(solution)/shard_map/ppermute | solution.py:252
  11.9 7.7 %collective-permute-start.2 = (bf16[200,256]{1,0:T(8,128)(2,1)S(1)}, bf16[200,256]{1,0:T(8,128)(2,1)S(1)}, u32[]{:S(2)}, u32[]{:S(2)}) collective-permute-start(bf16[200,256]{1,0:T(8,128)(2,1)S(1)} %fusion.3), channel_id=1, source_target_pairs={{0,8},{1,9},{2,10},{3,11},{4,12},{5,13},{6,14},{7,15},{8,0},{9,1},... | collective-permute-start | bytes 307208 | tf_op jit(solution)/shard_map/ppermute | solution.py:252
  19.7 4.5 %collective-permute-start.3 = (bf16[200,256]{1,0:T(8,128)(2,1)S(1)}, bf16[200,256]{1,0:T(8,128)(2,1)S(1)}, u32[]{:S(2)}, u32[]{:S(2)}) collective-permute-start(bf16[200,256]{1,0:T(8,128)(2,1)S(1)} %fusion.1), channel_id=1, source_target_pairs={{0,2},{1,3},{2,0},{3,1},{4,6},{5,7},{6,4},{7,5},{8,10},{9,11},{10,... | collective-permute-start | bytes 307208 | tf_op jit(solution)/shard_map/ppermute | solution.py:252
  20.0 16.4 %collective-permute-start.7 = (bf16[256,768]{1,0:T(8,128)(2,1)S(1)}, bf16[256,768]{1,0:T(8,128)(2,1)S(1)}, u32[]{:S(2)}, u32[]{:S(2)}) collective-permute-start(bf16[256,768]{1,0:T(8,128)(2,1)S(1)} %get-tuple-element.12.refs_0_.refs_1_), channel_id=1, source_target_pairs={{1,0},{2,1},{3,2},{4,3},{5,4},{6,5},{7,6},{8,7},{9,8},{10,9},{11,1... | collective-permute-start | bytes 1179656 | tf_op jit(solution)/shard_map/ppermute | solution.py:320
  22.9 13.6 %collective-permute-start.6 = (bf16[256,768]{1,0:T(8,128)(2,1)S(1)}, bf16[256,768]{1,0:T(8,128)(2,1)S(1)}, u32[]{:S(2)}, u32[]{:S(2)}) collective-permute-start(bf16[256,768]{1,0:T(8,128)(2,1)S(1)} %get-tuple-element.13.refs_1_.refs_2_), channel_id=1, source_target_pairs={{0,1},{1,2},{2,3},{3,4},{4,5},{5,6},{6,7},{7,8},{8,9},{9,10},{10,1... | collective-permute-start | bytes 1179656 | tf_op jit(solution)/shard_map/ppermute | solution.py:319
  24.2 10.2 %collective-permute-start.4 = (bf16[200,256]{1,0:T(8,128)(2,1)S(1)}, bf16[200,256]{1,0:T(8,128)(2,1)S(1)}, u32[]{:S(2)}, u32[]{:S(2)}) collective-permute-start(bf16[200,256]{1,0:T(8,128)(2,1)S(1)} %add_convert_fusion), channel_id=1, source_target_pairs={{0,4},{1,5},{2,6},{3,7},{4,0},{5,1},{6,2},{7,3},{8,12},{9,13},{10,... | collective-permute-start | bytes 307208 | tf_op jit(solution)/shard_map/ppermute | solution.py:252
  34.4 5.8 %collective-permute-start.5 = (bf16[2,200,256]{2,1,0:T(8,128)(2,1)S(1)}, bf16[2,200,256]{2,1,0:T(8,128)(2,1)S(1)}, u32[]{:S(2)}, u32[]{:S(2)}) collective-permute-start(bf16[2,200,256]{2,1,0:T(8,128)(2,1)S(1)} %pad_maximum_fusion.state_ref), channel_id=1, source_target_pairs={{0,1},{1,0},{2,3},{3,2},{4,5},{5,4},{6,7},{7,6},{8,9},{9,8},{10,11... | collective-permute-start | bytes 614408 | tf_op jit(solution)/shard_map/ppermute | solution.py:252
  34.5 2.0 %copy-start = (bf16[768,768]{1,0:T(8,128)(2,1)S(1)}, bf16[768,768]{1,0:T(8,128)(2,1)}, u32[]{:S(2)}) copy-start(bf16[768,768]{1,0:T(8,128)(2,1)} %wo_ref.3) | copy-start | bytes 3538948
  34.5 2.0 %copy-start.4 = (f32[3,3,768]{2,1,0:T(4,128)S(1)}, f32[3,3,768]{2,1,0:T(4,128)}, u32[]{:S(2)}) copy-start(f32[3,3,768]{2,1,0:T(4,128)} %refs_6_.1) | copy-start | bytes 82948

commit v7 on v6

--- a/solution.py
+++ b/solution.py
@@ -14,6 +14,16 @@
 TILE = 256
 VMEM_LIMIT = 28 * 1024 * 1024
 FIRST_LIMIT = 54900000
+
+
+def split_of(count):
+    return min(4, count // 2)
+
+
+def place_here():
+    spot = lax.axis_index("row")
+    shift = split_of(lax.axis_size("row")).bit_length() - 1
+    return lax.bitwise_and(spot, 1), lax.bitwise_and(lax.shift_right_logical(spot, shift), 1)
 
 
 def tiles_of(total, wanted):
@@ -81,7 +91,8 @@
         vt_ref[head, :dim_head, :] = turned[head * dim_head : (head + 1) * dim_head]
 
 
-def first_kernel(place_ref, x_hbm, wk_hbm, wv_hbm, omega_hbm, *refs):
+def first_kernel(x_hbm, wk_hbm, wv_hbm, omega_hbm, *refs):
+    place = place_here()
     heads, _, _ = omega_hbm.shape
     tokens, width = x_hbm.shape
     here = len(refs) - 11
@@ -89,7 +100,7 @@
     value_refs = refs[2 : 2 + here]
     x_ref, wk_ref, wv_ref, omega_ref, key_ref, sems, pair_ref, vt_ref, feat_ref = refs[2 + here :]
     half, span = heads // 2, width // 2
-    other = 1 - place_ref[0]
+    other = 1 - place[0]
     moves = [(x_hbm, x_ref), (wv_hbm, wv_ref), (omega_hbm.at[pl.ds(other * half, half)], omega_ref), (wk_hbm, wk_ref)]
     copies = [pltpu.make_async_copy(source, target, sems.at[i]) for i, (source, target) in enumerate(moves)]
     for copy in copies:
@@ -107,22 +118,23 @@
     copies[3].wait()
     for block in blocks:
         key_ref[block, :] = jnp.dot(x_ref[block, :], wk_ref[...], preferred_element_type=F32).astype(BF)
-    own_ref[...] = key_ref[:, pl.ds(pl.multiple_of(place_ref[0] * span, span), span)]
+    own_ref[...] = key_ref[:, pl.ds(pl.multiple_of(place[0] * span, span), span)]
     turn_values(value_refs, other * span, span, vt_ref)
-    half_state(place_ref[1], key_ref, other * span, pair_ref, vt_ref, feat_ref, send_ref)
-
-
-def second_kernel(place_ref, key_ref, omega_ref, *refs):
+    half_state(place[1], key_ref, other * span, pair_ref, vt_ref, feat_ref, send_ref)
+
+
+def second_kernel(key_ref, omega_ref, *refs):
+    place = place_here()
     heads, _, _ = omega_ref.shape
     value_refs = refs[:-4]
     state_ref, pair_ref, vt_ref, feat_ref = refs[-4:]
     half, span = heads // 2, key_ref.shape[1]
-    core = place_ref[0]
+    core = place[0]
     fill_marks(vt_ref, half // 2)
     for pair in range(half // 2):
         fill_pair(pair_ref, pair, [omega_ref[core * half + 2 * pair], omega_ref[core * half + 2 * pair + 1]])
     turn_values(value_refs, core * span, span, vt_ref)
-    half_state(place_ref[1], key_ref, 0, pair_ref, vt_ref, feat_ref, state_ref)
+    half_state(place[1], key_ref, 0, pair_ref, vt_ref, feat_ref, state_ref)
 
 
 def query_kernel(x_ref, wq_ref, omega_ref, feat_ref, pair_ref):
@@ -189,13 +201,14 @@
     return both[:, :wide] / both[:, wide:]
 
 
-def own_kernel(place_ref, state_ref, feat_ref, gain_ref, wo_ref, part_ref, square_ref, mat_ref):
+def own_kernel(state_ref, feat_ref, gain_ref, wo_ref, part_ref, square_ref, mat_ref):
+    place = place_here()
     pairs, rows, _ = mat_ref.shape
     wide = rows // 2
     tokens = part_ref.shape[0]
     span = pairs * wide
-    core = place_ref[0]
-    fill_mats(place_ref[1], state_ref, mat_ref, wide // 2)
+    core = place[0]
+    fill_mats(place[1], state_ref, mat_ref, wide // 2)
     tile = tiles_of(tokens, 256)
     for start in range(0, tokens, tile):
         cut = slice(start, start + tile)
@@ -217,16 +230,17 @@
     return share, total
 
 
-def out_kernel(place_ref, state_ref, feat_ref, part_ref, square_ref, base_ref, gain_ref, wo_ref, out_hbm, mat_ref, out_ref, sems):
+def out_kernel(state_ref, feat_ref, part_ref, square_ref, base_ref, gain_ref, wo_ref, out_hbm, mat_ref, out_ref, sems):
+    place = place_here()
     _, rows, _ = mat_ref.shape
     wide = rows // 2
     tokens, width = base_ref.shape
-    fill_mats(place_ref[1], state_ref, mat_ref, wide // 2)
+    fill_mats(place[1], state_ref, mat_ref, wide // 2)
     tile = tiles_of(tokens, 256)
     copies = []
     for start in range(0, tokens, tile):
         cut = slice(start, start + tile)
-        share, total = half_share(1 - place_ref[0], width // 2, feat_ref, cut, gain_ref, wo_ref, mat_ref)
+        share, total = half_share(1 - place[0], width // 2, feat_ref, cut, gain_ref, wo_ref, mat_ref)
         total = total + square_ref[cut, :]
         scale = lax.rsqrt(jnp.sum(total, axis=1, keepdims=True) * (1.0 / width) + 1e-06)
         out_ref[cut, :] = (base_ref[cut, :] + scale * (share + part_ref[cut, :])).astype(BF)
@@ -272,18 +286,14 @@
     here, cols, width = tokens.shape
     heads, dim_head, nfeat = omega.shape
     count = lax.axis_size("row")
-    split = min(4, count // 2)
+    split = split_of(count)
     flat = tokens.reshape(here * cols, width)
     amount = here * cols
     half, span = heads // 2, width // 2
     rows = half // 2 * dim_head + 8
-    spot = lax.axis_index("row").astype(jnp.int32)
-    bits = [lax.bitwise_and(lax.shift_right_logical(spot, i), 1) for i in range(count.bit_length() - 1)]
-    place = jnp.stack([bits[0], bits[split.bit_length() - 1]])
     proj = 2 * amount * width * width
     feats = 2 * amount * width * nfeat
     vmem = pl.BlockSpec(memory_space=pltpu.VMEM)
-    smem = pl.BlockSpec(memory_space=pltpu.SMEM)
     hbm = pl.BlockSpec(memory_space=pltpu.HBM)
     pairs = pltpu.VMEM((half // 2, 2 * dim_head, 2 * nfeat), BF)
     turned = pltpu.VMEM((half, dim_head + 16, amount), BF)
@@ -294,7 +304,7 @@
         first_kernel,
         [jax.ShapeDtypeStruct((2, rows, nfeat), BF), jax.ShapeDtypeStruct((amount, span), BF)]
         + [jax.ShapeDtypeStruct((cols, width), BF)] * here,
-        [smem] + [hbm] * 4,
+        [hbm] * 4,
         [
             pltpu.VMEM((amount, width), BF),
             pltpu.VMEM((width, width), BF),
@@ -308,14 +318,14 @@
         ],
         2 * proj + feats,
         FIRST_LIMIT,
-    )(place, flat, w_key, w_value, omega)
+    )(flat, w_key, w_value, omega)
     (keep,) = call(
         second_kernel,
         [jax.ShapeDtypeStruct((2, rows, nfeat), F32)],
-        [smem] + [vmem] * (2 + here),
+        [vmem] * (2 + here),
         [pairs, turned, feat],
         feats,
-    )(place, key, omega, *values)
+    )(key, omega, *values)
     top = lax.ppermute(values[-1], "row", [(i, i + 1) for i in range(count - 1)])
     low = lax.ppermute(values[0], "row", [(i + 1, i) for i in range(count - 1)])
     (feat_query,) = call(
@@ -338,19 +348,19 @@
     part, square = call(
         own_kernel,
         [jax.ShapeDtypeStruct((amount, width), F32), jax.ShapeDtypeStruct((amount, 2 * dim_head), F32)],
-        [smem] + [vmem] * 4,
+        [vmem] * 4,
         [mats],
         feats,
-    )(place, mine, feat_query, gain, w_out)
+    )(mine, feat_query, gain, w_out)
     tile = tiles_of(amount, 256)
     (out,) = call(
         out_kernel,
         [jax.ShapeDtypeStruct((amount, width), BF)],
-        [smem] + [vmem] * 7,
+        [vmem] * 7,
         [mats, pltpu.VMEM((amount, width), BF), pltpu.SemaphoreType.DMA((amount // tile,))],
         proj + feats,
         space=pltpu.HBM,
-    )(place, theirs, feat_query, part, square, base, gain, w_out)
+    )(theirs, feat_query, part, square, base, gain, w_out)
     return out.reshape(here, cols, width)
 
 

time: 42.9 us -> 40.4 us (0.942)
  Pallas kernels: 14.6 us -> 12.5 us
  waiting for transfers between devices: 19.1 us -> 18.3 us
    pallas_call x2, Pallas kernels: 4.24 us -> 3.14 us  [the longest x1 2.05 us: layer(): call(out_kernel, [jax.ShapeDtypeStruct((amount, width), BF)], [vmem] * 7,...]
    ppermute x6, waiting for transfers between devices: 19.1 us -> 18.3 us  [swap(): return lax.ppermute(block, 'row', [(i, i ^ bit) for i in range(count)])]
    pallas_call x1, Pallas kernels: 4.82 us -> 4.28 us  [layer(): call(first_kernel, [jax.ShapeDtypeStruct((2, rows, nfeat), BF), jax.Shape...]
    pallas_call x1, Pallas kernels: 1.78 us -> 1.26 us  [layer(): call(own_kernel, [jax.ShapeDtypeStruct((amount, width), F32), jax.ShapeDt...]
  transfers between devices with their start and end apart: 8 -> 8, of which waited for: 3 -> 3; matrix products, arithmetic and copies ran while one was open for 0% -> 0% of each run, Pallas kernels for 17% -> 15%
where the time goes in v7:
time: 40.4 us; the launch traced here: 40.2 us
  waiting for transfers between devices  18.3 us (45%)
  Pallas kernels  12.5 us (31%)
  starting transfers between devices  8.97 us (22%)
    ppermute x6, waiting for transfers between devices, swap(): return lax.ppermute(block, 'row', [(i, i ^ bit) for i in range(count)])  18.3 us
    ppermute x6, starting transfers between devices, swap(): return lax.ppermute(block, 'row', [(i, i ^ bit) for i in range(count)])  4.42 us
    pallas_call x1, Pallas kernels, layer(): call(first_kernel, [jax.ShapeDtypeStruct((2, rows, nfeat), BF), jax.Shape...  4.28 us
    ppermute x1, starting transfers between devices, layer(): low = lax.ppermute(values[0], 'row', [(i + 1, i) for i in range(count - 1)])  3.25 us
    pallas_call x1, Pallas kernels, layer(): call(out_kernel, [jax.ShapeDtypeStruct((amount, width), BF)], [vmem] * 7,...  2.05 us
    pallas_call x1, Pallas kernels, layer(): call(query_kernel, [jax.ShapeDtypeStruct((amount, heads * nfeat), BF)], [...  1.91 us
    pallas_call x1, Pallas kernels, layer(): call(conv_kernel_body, [jax.ShapeDtypeStruct((amount, width), F32)], [vme...  1.88 us
    ppermute x1, starting transfers between devices, layer(): lax.ppermute(values[-1], 'row', [(i, i + 1) for i in range(count - 1)])  1.29 us
  transfers between devices with their start and end apart: 8, of which 3 were waited for; matrix products, arithmetic and copies ran while one was open for 0% of the time, Pallas kernels for 15%

profile of v7, /device:TPU:27, one launch (start us, length us, event | category | flops | bytes accessed | tf_op | source)
XLA Modules:
  0.0 40.2 jit_solution(17363950899400724653)
XLA Ops:
  0.0 0.0 copy-start.2
  0.0 4.3 %shard_map.82 = (bf16[2,200,256]{2,1,0:T(8,128)(2,1)S(1)}, bf16[512,384]{1,0:T(8,128)(2,1)S(1)}, bf16[256,768]{1,0:T(8,128)(2,1)S(1)}, bf16[256,768]{1,0:T(8,128)(2,1)S(1)}) custom-call(bf16[512,768]{1,0:T(8,128)(2,1)} %bitcast.16, bf16[768,768]{1,0:T(8,128)(2,1)} %wk_hbm.1, bf16[768,768]{1,0:T(8,128)(2,1)} %wv_hbm.1, bf16[12,64,256]{2,1,0:T(8,128)(2,1)} %omega_ref.3), custom_call_target="tpu_custom_call" | custom-call | flops 1409286144 | tf_op jit(solution)/shard_map/pallas_call | solution.py:303
  4.3 0.7 %collective-permute-start = (bf16[2,200,256]{2,1,0:T(8,128)(2,1)S(1)}, bf16[2,200,256]{2,1,0:T(8,128)(2,1)S(1)}, u32[]{:S(2)}, u32[]{:S(2)}) collective-permute-start(bf16[2,200,256]{2,1,0:T(8,128)(2,1)S(1)} %get-tuple-element.14), channel_id=1, source_target_pairs={{0,1},{1,0},{2,3},{3,2},{4,5},{5,4},{6,7},{7,6},{8,9},{9,8},{10,11... | collective-permute-start | bytes 614408 | tf_op jit(solution)/shard_map/ppermute | solution.py:266
  5.0 0.0 copy-done.2
  5.0 1.1 %shard_map.83 = f32[2,200,256]{2,1,0:T(8,128)S(1)} custom-call(bf16[512,384]{1,0:T(8,128)(2,1)S(1)} %get-tuple-element.11.key_ref, bf16[12,64,256]{2,1,0:T(8,128)(2,1)S(1)} %copy-done.2, bf16[256,768]{1,0:T(8,128)(2,1)S(1)} %get-tuple-element.12.refs_0_.refs_1_, bf16[256,768]{1,0:T(8,128)(2,1)S(1)} %get-tuple-element.13.refs_1_.refs_2_), custom_call_target="tpu_custom_call" | custom-call | flops 201326592 | tf_op jit(solution)/shard_map/pallas_call | solution.py:322
  6.1 0.0 collective-permute-done
  6.2 0.0 copy-start.5
  6.2 0.0 copy-start.1
  6.2 0.0 copy-start.3
  6.2 0.2 collective-permute-start.1
  6.5 3.9 %collective-permute-done.1 = bf16[200,256]{1,0:T(8,128)(2,1)S(1)} collective-permute-done((bf16[200,256]{1,0:T(8,128)(2,1)S(1)}, bf16[200,256]{1,0:T(8,128)(2,1)S(1)}, u32[]{:S(2)}, u32[]{:S(2)}) %collective-permute-start.1) | collective-permute-done | bytes 102432 | tf_op jit(solution)/shard_map/ppermute | solution.py:266
  10.4 0.1 collective-permute-start.2
  10.5 7.2 %collective-permute-done.2 = bf16[200,256]{1,0:T(8,128)(2,1)S(1)} collective-permute-done((bf16[200,256]{1,0:T(8,128)(2,1)S(1)}, bf16[200,256]{1,0:T(8,128)(2,1)S(1)}, u32[]{:S(2)}, u32[]{:S(2)}) %collective-permute-start.2) | collective-permute-done | bytes 102432 | tf_op jit(solution)/shard_map/ppermute | solution.py:266
  17.8 0.3 collective-permute-start.3
  18.1 3.2 %collective-permute-start.7 = (bf16[256,768]{1,0:T(8,128)(2,1)S(1)}, bf16[256,768]{1,0:T(8,128)(2,1)S(1)}, u32[]{:S(2)}, u32[]{:S(2)}) collective-permute-start(bf16[256,768]{1,0:T(8,128)(2,1)S(1)} %get-tuple-element.12.refs_0_.refs_1_), channel_id=1, source_target_pairs={{1,0},{2,1},{3,2},{4,3},{5,4},{6,5},{7,6},{8,7},{9,8},{10,9},{11,1... | collective-permute-start | bytes 1179656 | tf_op jit(solution)/shard_map/ppermute | solution.py:330
  21.3 1.3 %collective-permute-start.6 = (bf16[256,768]{1,0:T(8,128)(2,1)S(1)}, bf16[256,768]{1,0:T(8,128)(2,1)S(1)}, u32[]{:S(2)}, u32[]{:S(2)}) collective-permute-start(bf16[256,768]{1,0:T(8,128)(2,1)S(1)} %get-tuple-element.13.refs_1_.refs_2_), channel_id=1, source_target_pairs={{0,1},{1,2},{2,3},{3,4},{4,5},{5,6},{6,7},{7,8},{8,9},{9,10},{10,1... | collective-permute-start | bytes 1179656 | tf_op jit(solution)/shard_map/ppermute | solution.py:329
  22.6 0.0 collective-permute-done.3
  22.6 0.1 add_convert_fusion
  22.7 3.0 %collective-permute-start.4 = (bf16[200,256]{1,0:T(8,128)(2,1)S(1)}, bf16[200,256]{1,0:T(8,128)(2,1)S(1)}, u32[]{:S(2)}, u32[]{:S(2)}) collective-permute-start(bf16[200,256]{1,0:T(8,128)(2,1)S(1)} %add_convert_fusion), channel_id=1, source_target_pairs={{0,4},{1,5},{2,6},{3,7},{4,0},{5,1},{6,2},{7,3},{8,12},{9,13},{10,... | collective-permute-start | bytes 307208 | tf_op jit(solution)/shard_map/ppermute | solution.py:266
  25.7 7.2 %collective-permute-done.4 = bf16[200,256]{1,0:T(8,128)(2,1)S(1)} collective-permute-done((bf16[200,256]{1,0:T(8,128)(2,1)S(1)}, bf16[200,256]{1,0:T(8,128)(2,1)S(1)}, u32[]{:S(2)}, u32[]{:S(2)}) %collective-permute-start.4) | collective-permute-done | bytes 102432 | tf_op jit(solution)/shard_map/ppermute | solution.py:266
  32.9 0.1 collective-permute-start.5
  33.0 0.0 copy-done.5
  33.0 0.0 copy-done.1
  33.0 0.0 copy-done.3
  33.0 0.0 copy-start
  33.0 0.0 copy-start.4
  33.0 1.9 %shard_map.84.feat_ref = bf16[512,3072]{1,0:T(8,128)(2,1)S(1)} custom-call(bf16[512,768]{1,0:T(8,128)(2,1)S(1)} %bitcast.17, bf16[768,768]{1,0:T(8,128)(2,1)S(1)} %copy-done.3, bf16[12,64,256]{2,1,0:T(8,128)(2,1)S(1)} %copy-done.2), custom_call_target="tpu_custom_call" | custom-call | flops 805306368 | tf_op jit(solution)/shard_map/pallas_call | solution.py:331
  34.9 0.0 collective-permute-done.7.refs_3_
  34.9 0.0 collective-permute-done.6.refs_0_
  35.0 0.0 copy-done
  35.0 0.0 copy-done.4
  35.0 1.9 %shard_map.86.base_ref = f32[512,768]{1,0:T(8,128)S(1)} custom-call(bf16[256,768]{1,0:T(8,128)(2,1)S(1)} %collective-permute-done.6.refs_0_, bf16[256,768]{1,0:T(8,128)(2,1)S(1)} %get-tuple-element.12.refs_0_.refs_1_, bf16[256,768]{1,0:T(8,128)(2,1)S(1)} %get-tuple-element.13.refs_1_.refs_2_, bf16[256,768]{1,0:T(8,128)(2,1)S(1)} %collective-permute-done.7.refs_3_, ...), custom_call_target="tpu_custom_call" | custom-call | flops 603979776 | tf_op jit(solution)/shard_map/pallas_call | solution.py:338
  36.9 1.3 %shard_map.85 = (f32[512,768]{1,0:T(8,128)S(1)}, f32[512,128]{1,0:T(8,128)S(1)}) custom-call(bf16[2,200,256]{2,1,0:T(8,128)(2,1)S(1)} %pad_maximum_fusion.state_ref, bf16[512,3072]{1,0:T(8,128)(2,1)S(1)} %shard_map.84.feat_ref, f32[1,768]{1,0:T(1,128)S(1)} %reshape.11.gain_ref, bf16[768,768]{1,0:T(8,128)(2,1)S(1)} %copy-done), custom_call_target="tpu_custom_call" | custom-call | flops 201326592 | tf_op jit(solution)/shard_map/pallas_call | solution.py:348
  38.1 0.0 collective-permute-done.5.state_ref
  38.1 2.1 %shard_map.87 = bf16[512,768]{1,0:T(8,128)(2,1)} custom-call(bf16[2,200,256]{2,1,0:T(8,128)(2,1)S(1)} %collective-permute-done.5.state_ref, bf16[512,3072]{1,0:T(8,128)(2,1)S(1)} %shard_map.84.feat_ref, f32[512,768]{1,0:T(8,128)S(1)} %get-tuple-element.15.part_ref, f32[512,128]{1,0:T(8,128)S(1)} %get-tuple-element.16.square_ref, ...), custom_call_target="tpu_custom_call" | custom-call | flops 805306368 | tf_op jit(solution)/shard_map/pallas_call | solution.py:356
  (6 shorter events, 0.1 us)
Async XLA Ops:
  0.0 5.0 %copy-start.2 = (bf16[12,64,256]{2,1,0:T(8,128)(2,1)S(1)}, bf16[12,64,256]{2,1,0:T(8,128)(2,1)}, u32[]{:S(2)}) copy-start(bf16[12,64,256]{2,1,0:T(8,128)(2,1)} %omega_ref.3) | copy-start | bytes 1179652
  4.3 1.8 %collective-permute-start = (bf16[2,200,256]{2,1,0:T(8,128)(2,1)S(1)}, bf16[2,200,256]{2,1,0:T(8,128)(2,1)S(1)}, u32[]{:S(2)}, u32[]{:S(2)}) collective-permute-start(bf16[2,200,256]{2,1,0:T(8,128)(2,1)S(1)} %get-tuple-element.14), channel_id=1, source_target_pairs={{0,1},{1,0},{2,3},{3,2},{4,5},{5,4},{6,7},{7,6},{8,9},{9,8},{10,11... | collective-permute-start | bytes 614408 | tf_op jit(solution)/shard_map/ppermute | solution.py:266
  6.2 26.8 %copy-start.5 = (f32[768]{0:T(1024)S(1)}, f32[768]{0:T(1024)}, u32[]{:S(2)}) copy-start(f32[768]{0:T(1024)} %param.15) | copy-start | bytes 9220
  6.2 26.8 %copy-start.1 = (bf16[2,256,768]{2,1,0:T(8,128)(2,1)S(1)}, bf16[2,256,768]{2,1,0:T(8,128)(2,1)}, u32[]{:S(2)}) copy-start(bf16[2,256,768]{2,1,0:T(8,128)(2,1)} %param.8) | copy-start | bytes 2359300
  6.2 26.8 %copy-start.3 = (bf16[768,768]{1,0:T(8,128)(2,1)S(1)}, bf16[768,768]{1,0:T(8,128)(2,1)}, u32[]{:S(2)}) copy-start(bf16[768,768]{1,0:T(8,128)(2,1)} %wq_ref.1) | copy-start | bytes 3538948
  6.2 4.2 %collective-permute-start.1 = (bf16[200,256]{1,0:T(8,128)(2,1)S(1)}, bf16[200,256]{1,0:T(8,128)(2,1)S(1)}, u32[]{:S(2)}, u32[]{:S(2)}) collective-permute-start(bf16[200,256]{1,0:T(8,128)(2,1)S(1)} %fusion.2), channel_id=1, source_target_pairs={{0,4},{1,5},{2,6},{3,7},{4,0},{5,1},{6,2},{7,3},{8,12},{9,13},{10,... | collective-permute-start | bytes 307208 | tf_op jit(solution)/shard_map/ppermute | solution.py:266
  10.4 7.3 %collective-permute-start.2 = (bf16[200,256]{1,0:T(8,128)(2,1)S(1)}, bf16[200,256]{1,0:T(8,128)(2,1)S(1)}, u32[]{:S(2)}, u32[]{:S(2)}) collective-permute-start(bf16[200,256]{1,0:T(8,128)(2,1)S(1)} %fusion.3), channel_id=1, source_target_pairs={{0,8},{1,9},{2,10},{3,11},{4,12},{5,13},{6,14},{7,15},{8,0},{9,1},... | collective-permute-start | bytes 307208 | tf_op jit(solution)/shard_map/ppermute | solution.py:266
  17.8 4.9 %collective-permute-start.3 = (bf16[200,256]{1,0:T(8,128)(2,1)S(1)}, bf16[200,256]{1,0:T(8,128)(2,1)S(1)}, u32[]{:S(2)}, u32[]{:S(2)}) collective-permute-start(bf16[200,256]{1,0:T(8,128)(2,1)S(1)} %fusion.1), channel_id=1, source_target_pairs={{0,2},{1,3},{2,0},{3,1},{4,6},{5,7},{6,4},{7,5},{8,10},{9,11},{10,... | collective-permute-start | bytes 307208 | tf_op jit(solution)/shard_map/ppermute | solution.py:266
  18.1 16.9 %collective-permute-start.7 = (bf16[256,768]{1,0:T(8,128)(2,1)S(1)}, bf16[256,768]{1,0:T(8,128)(2,1)S(1)}, u32[]{:S(2)}, u32[]{:S(2)}) collective-permute-start(bf16[256,768]{1,0:T(8,128)(2,1)S(1)} %get-tuple-element.12.refs_0_.refs_1_), channel_id=1, source_target_pairs={{1,0},{2,1},{3,2},{4,3},{5,4},{6,5},{7,6},{8,7},{9,8},{10,9},{11,1... | collective-permute-start | bytes 1179656 | tf_op jit(solution)/shard_map/ppermute | solution.py:330
  21.3 13.6 %collective-permute-start.6 = (bf16[256,768]{1,0:T(8,128)(2,1)S(1)}, bf16[256,768]{1,0:T(8,128)(2,1)S(1)}, u32[]{:S(2)}, u32[]{:S(2)}) collective-permute-start(bf16[256,768]{1,0:T(8,128)(2,1)S(1)} %get-tuple-element.13.refs_1_.refs_2_), channel_id=1, source_target_pairs={{0,1},{1,2},{2,3},{3,4},{4,5},{5,6},{6,7},{7,8},{8,9},{9,10},{10,1... | collective-permute-start | bytes 1179656 | tf_op jit(solution)/shard_map/ppermute | solution.py:329
  22.7 10.1 %collective-permute-start.4 = (bf16[200,256]{1,0:T(8,128)(2,1)S(1)}, bf16[200,256]{1,0:T(8,128)(2,1)S(1)}, u32[]{:S(2)}, u32[]{:S(2)}) collective-permute-start(bf16[200,256]{1,0:T(8,128)(2,1)S(1)} %add_convert_fusion), channel_id=1, source_target_pairs={{0,4},{1,5},{2,6},{3,7},{4,0},{5,1},{6,2},{7,3},{8,12},{9,13},{10,... | collective-permute-start | bytes 307208 | tf_op jit(solution)/shard_map/ppermute | solution.py:266
  32.9 5.3 %collective-permute-start.5 = (bf16[2,200,256]{2,1,0:T(8,128)(2,1)S(1)}, bf16[2,200,256]{2,1,0:T(8,128)(2,1)S(1)}, u32[]{:S(2)}, u32[]{:S(2)}) collective-permute-start(bf16[2,200,256]{2,1,0:T(8,128)(2,1)S(1)} %pad_maximum_fusion.state_ref), channel_id=1, source_target_pairs={{0,1},{1,0},{2,3},{3,2},{4,5},{5,4},{6,7},{7,6},{8,9},{9,8},{10,11... | collective-permute-start | bytes 614408 | tf_op jit(solution)/shard_map/ppermute | solution.py:266
  33.0 2.0 %copy-start = (bf16[768,768]{1,0:T(8,128)(2,1)S(1)}, bf16[768,768]{1,0:T(8,128)(2,1)}, u32[]{:S(2)}) copy-start(bf16[768,768]{1,0:T(8,128)(2,1)} %wo_ref.3) | copy-start | bytes 3538948
  33.0 2.0 %copy-start.4 = (f32[3,3,768]{2,1,0:T(4,128)S(1)}, f32[3,3,768]{2,1,0:T(4,128)}, u32[]{:S(2)}) copy-start(f32[3,3,768]{2,1,0:T(4,128)} %refs_6_.1) | copy-start | bytes 82948
